TPU v7x, 8 devices: a whole 2x2x1 slice. The times are simulated.
8 devices in a mesh: ep: 8 (over z, y, x, core).
Axes of the slice: x: 2, y: 2, z: 1, core: 2. Of those that a mesh axis runs over, the one named last changes fastest.
Arguments:
- tokens: bfloat16 [16, 2048, 2048], P('ep')
- loss_weight: bfloat16 [16, 2048, 2048], P('ep')
- w_gate: bfloat16 [2048, 64], replicated
- w_in: bfloat16 [64, 2048, 1024], P('ep')
- w_out: bfloat16 [64, 1024, 2048], P('ep')
- first_expert: int32 [16, 2048], P('ep')
- second_expert: int32 [16, 2048], P('ep')
- keep_second: int32 [16, 2048], P('ep')
Outputs:
- output 1: float32 [], replicated
- output 2: bfloat16 [16, 2048, 2048], P('ep')
- output 3: bfloat16 [64, 2048, 1024], P('ep')
- output 4: bfloat16 [64, 1024, 2048], P('ep')
- output 5: float32 [2048, 64], replicated
All inputs are finite; a program needn't handle non-finite values.
Results may differ from a plain program's by a relative error of at most 0.00956181.
Values are sent between devices in bfloat16 or wider.
A program may use at most 1 GiB of HBM per device.

v0:
```python
import jax
import jax.numpy as jnp
from jax import lax
from jax.sharding import PartitionSpec as P

ALPHA = 0.01


def gelu_bf16(pre_act):
    return jax.nn.gelu(pre_act, approximate=True).astype(jnp.bfloat16)


def route_masks(first_ids, second_ids, keep_ids, experts, cap_rows):
    seq_len = first_ids.shape[1]
    expert_ids = jnp.arange(experts, dtype=jnp.int32)
    first_hot = (first_ids[..., None] == expert_ids).astype(jnp.bfloat16)
    second_hot = (second_ids[..., None] == expert_ids).astype(jnp.bfloat16)
    second_kept = second_hot * keep_ids.astype(jnp.bfloat16)[..., None]
    seq_ids = jnp.arange(seq_len, dtype=jnp.int32)
    earlier = (seq_ids[:, None] > seq_ids[None, :]).astype(jnp.bfloat16)
    before_first = jnp.einsum('st,gte->gse', earlier, first_hot, preferred_element_type=jnp.float32)
    before_second = jnp.einsum('st,gte->gse', earlier, second_kept, preferred_element_type=jnp.float32)
    first_count = jnp.sum(first_hot, axis=1, dtype=jnp.float32)
    pos_first = jnp.sum(before_first * first_hot, axis=-1)
    pos_second = jnp.sum((before_second + first_count[:, None, :]) * second_hot, axis=-1)
    slot_ids = jnp.arange(cap_rows, dtype=jnp.float32)
    disp_first = first_hot[..., None] * (pos_first[..., None, None] == slot_ids).astype(jnp.bfloat16)
    disp_second = second_kept[..., None] * (pos_second[..., None, None] == slot_ids).astype(jnp.bfloat16)
    return first_hot, second_hot, first_count, disp_first, disp_second


def solution(mesh):
    ep_size = mesh.shape['ep']

    def layer_body(x_loc, r_loc, w_gate, w_in_loc, w_out_loc, first_ids, second_ids, keep_ids):
        local_groups, seq_len, hidden = x_loc.shape
        experts = w_gate.shape[1]
        cap_rows = 2 * seq_len // experts
        tokens_all = local_groups * ep_size * seq_len
        numel = tokens_all * hidden
        first_hot, second_hot, first_count, disp_first, disp_second = route_masks(first_ids, second_ids, keep_ids, experts, cap_rows)
        logits = jnp.einsum('gsh,he->gse', x_loc, w_gate, preferred_element_type=jnp.float32)
        router_prob = jax.nn.softmax(logits, axis=-1)
        gate_first = jnp.sum(router_prob * first_hot, axis=-1)
        gate_second = jnp.sum(router_prob * second_hot, axis=-1)
        gate_sum = gate_first + gate_second
        norm_first = (gate_first / gate_sum).astype(jnp.bfloat16)
        norm_second = (gate_second / gate_sum).astype(jnp.bfloat16)
        dispatch = disp_first + disp_second
        combine = disp_first * norm_first[..., None, None] + disp_second * norm_second[..., None, None]
        send_x = jnp.einsum('gsec,gsh->egch', dispatch, x_loc, preferred_element_type=jnp.float32).astype(jnp.bfloat16)
        expert_x = lax.all_to_all(send_x, 'ep', 0, 1, tiled=True)
        pre_act = jnp.einsum('egch,ehf->egcf', expert_x, w_in_loc, preferred_element_type=jnp.float32)
        act_bf, act_pull = jax.vjp(gelu_bf16, pre_act)
        expert_y = jnp.einsum('egcf,efh->egch', act_bf, w_out_loc, preferred_element_type=jnp.float32).astype(jnp.bfloat16)
        back_y = lax.all_to_all(expert_y, 'ep', 1, 0, tiled=True)
        out_first = jnp.einsum('gsec,egch->gsh', disp_first, back_y, preferred_element_type=jnp.float32).astype(jnp.bfloat16)
        out_second = jnp.einsum('gsec,egch->gsh', disp_second, back_y, preferred_element_type=jnp.float32).astype(jnp.bfloat16)
        moe_out = norm_first.astype(jnp.float32)[..., None] * out_first + norm_second.astype(jnp.float32)[..., None] * out_second
        dot_sum = jnp.einsum('gsh,gsh->', x_loc, r_loc, preferred_element_type=jnp.float32) + jnp.sum(moe_out * r_loc)
        local_stats = jnp.concatenate([jnp.sum(first_count, axis=0), jnp.sum(router_prob, axis=(0, 1)), dot_sum[None]])
        global_stats = lax.psum(local_stats, 'ep')
        frac_first = global_stats[:experts] / tokens_all
        mean_prob = global_stats[experts:2 * experts] / tokens_all
        loss_value = global_stats[2 * experts] / numel + ALPHA * experts * jnp.sum(frac_first * mean_prob)

        grad_send = jnp.einsum('gsec,gsh->egch', combine, r_loc, preferred_element_type=jnp.float32).astype(jnp.bfloat16)
        grad_y = lax.all_to_all(grad_send, 'ep', 0, 1, tiled=True)
        grad_w_out = jnp.einsum('egcf,egch->efh', act_bf, grad_y, preferred_element_type=jnp.float32).astype(jnp.bfloat16)
        grad_act = jnp.einsum('egch,efh->egcf', grad_y, w_out_loc, preferred_element_type=jnp.float32).astype(jnp.bfloat16)
        grad_pre = act_pull(grad_act)[0].astype(jnp.bfloat16)
        grad_w_in = jnp.einsum('egch,egcf->ehf', expert_x, grad_pre, preferred_element_type=jnp.float32).astype(jnp.bfloat16)
        grad_slots = jnp.einsum('egcf,ehf->egch', grad_pre, w_in_loc, preferred_element_type=jnp.float32).astype(jnp.bfloat16)
        grad_back = lax.all_to_all(grad_slots, 'ep', 1, 0, tiled=True)
        grad_x_moe = jnp.einsum('gsec,egch->gsh', dispatch, grad_back, preferred_element_type=jnp.float32)
        grad_norm_first = jnp.einsum('gsh,gsh->gs', r_loc, out_first, preferred_element_type=jnp.float32).astype(jnp.bfloat16).astype(jnp.float32)
        grad_norm_second = jnp.einsum('gsh,gsh->gs', r_loc, out_second, preferred_element_type=jnp.float32).astype(jnp.bfloat16).astype(jnp.float32)
        gate_sq = gate_sum * gate_sum
        grad_gate_first = (grad_norm_first - grad_norm_second) * gate_second / gate_sq
        grad_gate_second = (grad_norm_second - grad_norm_first) * gate_first / gate_sq
        grad_prob = grad_gate_first[..., None] * first_hot + grad_gate_second[..., None] * second_hot + (ALPHA * hidden * experts) * frac_first
        grad_logits = router_prob * (grad_prob - jnp.sum(router_prob * grad_prob, axis=-1, keepdims=True))
        grad_logits_bf = grad_logits.astype(jnp.bfloat16)
        grad_x_router = jnp.einsum('gse,he->gsh', grad_logits_bf, w_gate, preferred_element_type=jnp.float32)
        grad_x = (r_loc.astype(jnp.float32) + grad_x_moe + grad_x_router).astype(jnp.bfloat16)
        grad_gate_w = lax.psum(jnp.einsum('gsh,gse->he', x_loc, grad_logits_bf, preferred_element_type=jnp.float32), 'ep')
        return loss_value, grad_x, grad_w_in, grad_w_out, grad_gate_w

    row_spec = P('ep', None, None)
    id_spec = P('ep', None)
    return jax.shard_map(layer_body, mesh=mesh, in_specs=(row_spec, row_spec, P(None, None), row_spec, row_spec, id_spec, id_spec, id_spec), out_specs=(P(), row_spec, row_spec, row_spec, P(None, None)), check_vma=False)
```

profile of v0, /device:TPU:0, one launch (start us, length us, event | category | flops | bytes accessed | tf_op | source)
XLA Modules:
  0.0 2052.4 jit_solution(898207649522698315)
XLA Ops:
  7.2 0.0 copy-start
  7.2 0.0 copy-start.17
  7.2 0.0 copy-start.20
  7.2 2.8 fusion.105
  10.0 0.8 fusion.122
  10.9 0.8 convert_element_type.154
  11.6 10.9 fusion.168
  22.6 2.1 fusion.247
  24.7 0.1 fusion.112
  24.8 0.9 copy-done.1
  25.7 1.2 fusion.244
  26.9 0.0 copy-done.3
  26.9 2.0 fusion.96
  28.9 0.0 copy-start.11
  28.9 0.7 fusion.245
  29.7 21.6 %fusion.21 = (bf16[2,2048,64,64]{1,2,3,0:T(8,128)(2,1)}, bf16[2,2048,64,64]{1,2,3,0:T(8,128)(2,1)}) fusion(bf16[2,2048]{1,0:T(2,128)(2,1)S(1)} %get-tuple-element.22, bf16[2,2048]{1,0:T(2,128)(2,1)S(1)} %get-tuple-element.14, bf16[2,2048,64]{1,2,0:T(8,128)(2,1)S(1)} %fusion.96, bf16[2,2048,64]{1,2,0:T(8,128)(2,1)S(1)} %fusion.112, ...), kind=kLoop, calls=%fused_computation.36 | loop fusion | flops 100663296 | bytes 69222400 | tf_op jit(solution)/shard_map/add | solution.py:50
  51.3 86.2 %convert_bitcast_fusion = bf16[64,2,64,2048]{3,2,0,1:T(8,128)(2,1)} fusion(bf16[2,2048,64,64]{1,2,3,0:T(8,128)(2,1)} %get-tuple-element.17, bf16[2,2048,2048]{2,1,0:T(8,128)(2,1)} %param.9), kind=kOutput, calls=%fused_computation.58 | convolution fusion | flops 68736253952 | bytes 83886080 | tf_op jit(solution)/shard_map/gsec,gsh->egch/dot_general | solution.py:67
  137.5 23.0 %copy.25 = bf16[64,2,64,2048]{3,2,1,0:T(8,128)(2,1)} copy(bf16[64,2,64,2048]{3,2,0,1:T(8,128)(2,1)} %convert_bitcast_fusion) | data formatting | bytes 67108864 | tf_op jit(solution)/shard_map/convert_element_type | solution.py:67
  160.5 6.0 all-to-all-start.2
  166.4 86.2 %convert_bitcast_fusion.1 = bf16[64,2,64,2048]{3,2,0,1:T(8,128)(2,1)} fusion(bf16[2,2048,64,64]{1,2,3,0:T(8,128)(2,1)} %get-tuple-element.18, bf16[2,2048,2048]{2,1,0:T(8,128)(2,1)} %param.8), kind=kOutput, calls=%fused_computation.60 | convolution fusion | flops 68736253952 | bytes 83886080 | tf_op jit(solution)/shard_map/gsec,gsh->egch/dot_general | solution.py:51
  252.7 22.9 %copy.20 = bf16[64,2,64,2048]{3,2,1,0:T(8,128)(2,1)} copy(bf16[64,2,64,2048]{3,2,0,1:T(8,128)(2,1)} %convert_bitcast_fusion.1) | data formatting | bytes 67108864 | tf_op jit(solution)/shard_map/convert_element_type | solution.py:51
  275.6 255.8 %all-to-all-done.2 = bf16[64,2,64,2048]{3,2,1,0:T(8,128)(2,1)} async-done(((bf16[64,2,64,2048]{3,2,1,0:T(8,128)(2,1)}), bf16[64,2,64,2048]{3,2,1,0:T(8,128)(2,1)}, u32[]{:S(2)}, u32[]{:S(2)}) %all-to-all-start.2) | async-done | bytes 33554464 | tf_op jit(solution)/shard_map/all_to_all | solution.py:68
  531.4 6.2 all-to-all-start
  537.7 15.7 fusion.34
  553.4 22.9 %copy.26 = bf16[8,8,2,64,2048]{4,3,2,0,1:T(8,128)(2,1)} copy(bf16[8,8,2,64,2048]{4,3,2,1,0:T(8,128)(2,1)} %bitcast.29) | data formatting | bytes 67108864 | tf_op jit(solution)/shard_map/all_to_all | solution.py:68
  576.3 325.3 %all-to-all-done = bf16[64,2,64,2048]{3,2,1,0:T(8,128)(2,1)} async-done(((bf16[64,2,64,2048]{3,2,1,0:T(8,128)(2,1)}), bf16[64,2,64,2048]{3,2,1,0:T(8,128)(2,1)}, u32[]{:S(2)}, u32[]{:S(2)}) %all-to-all-start) | async-done | bytes 33554464 | tf_op jit(solution)/shard_map/all_to_all | solution.py:52
  901.6 22.9 %copy.21 = bf16[8,8,2,64,2048]{4,3,2,0,1:T(8,128)(2,1)} copy(bf16[8,8,2,64,2048]{4,3,2,1,0:T(8,128)(2,1)} %bitcast.9) | data formatting | bytes 67108864 | tf_op jit(solution)/shard_map/all_to_all | solution.py:52
  924.5 44.3 %fusion.26 = f32[8,16,64,1024]{3,2,1,0:T(8,128)} fusion(bf16[8,16,64,2048]{3,2,1,0:T(8,128)(2,1)} %bitcast.214, bf16[8,2048,1024]{2,1,0:T(8,128)(2,1)} %param.11), kind=kOutput, calls=%fused_computation.41 | convolution fusion | flops 34359738368 | bytes 100663296 | tf_op jit(solution)/shard_map/egch,ehf->egcf/dot_general | solution.py:53
  968.7 51.8 %fusion.46 = bf16[8,16,64,2048]{3,2,1,0:T(8,128)(2,1)} fusion(bf16[8,1024,2048]{2,1,0:T(8,128)(2,1)} %param.12, f32[8,16,64,1024]{3,2,1,0:T(8,128)} %fusion.26), kind=kOutput, calls=%fused_computation.63 | convolution fusion | flops 34452013056 | bytes 100663296 | tf_op jit(solution)/shard_map/egcf,efh->egch/dot_general | solution.py:55
  1020.5 61.4 %fusion.8 = bf16[8,16,64,1024]{3,2,1,0:T(8,128)(2,1)} fusion(f32[8,16,64,1024]{3,2,1,0:T(8,128)} %fusion.26, bf16[8,16,64,2048]{3,2,1,0:T(8,128)(2,1)} %bitcast.212, bf16[8,1024,2048]{2,1,0:T(8,128)(2,1)} %param.12), kind=kOutput, calls=%fused_computation.23 | convolution fusion | flops 34544287744 | bytes 117440512 | tf_op jit(solution)/shard_map/egch,efh->egcf/dot_general | solution.py:70
  1081.9 22.9 %copy.22 = bf16[8,16,64,2048]{3,2,0,1:T(8,128)(2,1)} copy(bf16[8,16,64,2048]{3,2,1,0:T(8,128)(2,1)} %fusion.46) | data formatting | bytes 67108864 | tf_op jit(solution)/shard_map/convert_element_type | solution.py:55
  1104.9 5.8 all-to-all-start.1
  1110.7 45.9 %fusion.49 = bf16[8,16,64,2048]{3,2,1,0:T(8,128)(2,1)} fusion(bf16[8,16,64,1024]{3,2,1,0:T(8,128)(2,1)} %fusion.8, bf16[8,2048,1024]{2,1,0:T(8,128)(2,1)} %param.11), kind=kOutput, calls=%fused_computation.64 | convolution fusion | flops 34376515584 | bytes 83886080 | tf_op jit(solution)/shard_map/egcf,ehf->egch/dot_general | solution.py:73
  1156.6 22.9 %copy.27 = bf16[8,16,64,2048]{3,2,0,1:T(8,128)(2,1)} copy(bf16[8,16,64,2048]{3,2,1,0:T(8,128)(2,1)} %fusion.49) | data formatting | bytes 67108864 | tf_op jit(solution)/shard_map/convert_element_type | solution.py:73
  1179.6 45.5 %bitcast_convert_fusion.1 = bf16[8,2048,1024]{2,1,0:T(8,128)(2,1)} fusion(bf16[8,16,64,2048]{3,2,1,0:T(8,128)(2,1)} %bitcast.215, bf16[8,16,64,1024]{3,2,1,0:T(8,128)(2,1)} %fusion.8), kind=kOutput, calls=%fused_computation.2 | convolution fusion | flops 34376515584 | bytes 83886080 | tf_op jit(solution)/shard_map/egch,egcf->ehf/dot_general | solution.py:72
  1225.1 51.6 %bitcast_convert_fusion = bf16[8,1024,2048]{2,1,0:T(8,128)(2,1)} fusion(bf16[8,16,64,2048]{3,2,1,0:T(8,128)(2,1)} %bitcast.213, f32[8,16,64,1024]{3,2,1,0:T(8,128)} %fusion.26), kind=kOutput, calls=%fused_computation.1 | convolution fusion | flops 34452013056 | bytes 100663296 | tf_op jit(solution)/shard_map/egcf,egch->efh/dot_general | solution.py:69
  1276.7 197.9 %all-to-all-done.1 = bf16[8,16,64,2048]{3,2,0,1:T(8,128)(2,1)} async-done(((bf16[8,16,64,2048]{3,2,0,1:T(8,128)(2,1)}), bf16[8,16,64,2048]{3,2,0,1:T(8,128)(2,1)}, u32[]{:S(2)}, u32[]{:S(2)}) %all-to-all-start.1) | async-done | bytes 33554464 | tf_op jit(solution)/shard_map/all_to_all | solution.py:56
  1474.6 5.9 all-to-all-start.3
  1480.5 0.0 all-reduce.2.cloned.1.call-start
  1480.6 124.4 %bitcast_convert_fusion.2 = bf16[2,2048,2048]{2,1,0:T(8,128)(2,1)} fusion(bf16[8,8,2,64,2048]{4,3,0,2,1:T(8,128)(2,1)} %bitcast.16, bf16[2,2048,64]{1,2,0:T(8,128)(2,1)S(1)} %copy-done.12, bf16[2,2048,64]{1,2,0:T(8,128)(2,1)S(1)} %copy-done.7), kind=kOutput, calls=%fused_computation.47 | convolution fusion | flops 68744642560 | bytes 51380224 | tf_op jit(solution)/shard_map/gsec,egch->gsh/dot_general | solution.py:58
  1605.1 0.0 copy-done.5
  1605.1 0.0 copy-done.30
  1605.2 0.0 copy-start.18
  1605.2 0.0 copy-start.21
  1605.2 0.0 copy-start.13
  1605.2 125.4 %fusion.19 = (bf16[2,2048]{1,0:T(2,128)(2,1)S(1)}, f32[]{:T(128)}, bf16[2,2048]{1,0:T(2,128)(2,1)S(1)}) fusion(bf16[2,2048,2048]{2,1,0:T(8,128)(2,1)} %param.9, bf16[2,2048,2048]{2,1,0:T(8,128)(2,1)} %bitcast_convert_fusion.2, f32[2,2048]{1,0:T(2,128)S(1)} %copy-done.31, f32[2,2048]{1,0:T(2,128)S(1)} %copy-done.30, ...), kind=kOutput, calls=%fused_computation.34 | convolution fusion | flops 68845305856 | bytes 68206592 | tf_op jit(solution)/shard_map/gsec,egch->gsh/dot_general | solution.py:57
  1731.8 0.1 pad_maximum_fusion
  1731.9 129.1 %psum.14 = f32[129]{0:T(256)S(1)} all-reduce(f32[129]{0:T(256)S(1)} %pad_maximum_fusion), channel_id=1, replica_groups=mesh['ep'=8] {'ep'}, use_global_device_ids=true, to_apply=%region_10.0 | all-reduce | flops 129 | bytes 1032 | tf_op jit(solution)/shard_map/psum | solution.py:62
  1861.0 0.8 slice_multiply_fusion
  1861.8 0.0 copy-start.23
  1861.8 0.0 copy-start.24
  1861.8 0.0 copy-done.2
  1861.8 0.0 copy-done.15
  1861.9 0.5 multiply_reduce_fusion
  1862.4 10.6 convolution_bitcast_fusion
  1873.0 0.0 all-reduce.2.cloned.1.call-update
  1873.0 0.0 all-to-all-done.3
  1873.1 0.0 copy-start.19
  1873.1 0.0 copy-start.22
  1873.1 140.3 %fusion.22 = f32[2,2048,2048,1]{2,1,3,0:T(8,128)} fusion(bf16[8,8,2,64,2048]{4,3,0,2,1:T(8,128)(2,1)} %bitcast.34, bf16[2,2048,64]{1,2,0:T(8,128)(2,1)S(1)} %copy-done.13, bf16[2,2048,64]{1,2,0:T(8,128)(2,1)S(1)} %copy-done.8, bf16[2,2048,64]{1,2,0:T(8,128)(2,1)S(1)} %copy-done.10, bf16[2,2048,64]{1,2,0:T(8,128)(2,1)S(1)} %copy-done.5), kind=kOutput, calls=%fused_computation.37 | convolution fusion | flops 68769808384 | bytes 69206016 | tf_op jit(solution)/shard_map/gsec,egch->gsh/dot_general | solution.py:75
  2013.5 27.0 %fusion.18 = bf16[2,2048,2048]{2,1,0:T(8,128)(2,1)} fusion(bf16[2,2048,2048]{2,1,0:T(8,128)(2,1)} %param.9, f32[2,2048,2048,1]{2,1,3,0:T(8,128)} %fusion.22, bf16[2048,64]{0,1:T(8,128)(2,1)S(1)} %copy-done, f32[2,2048]{1,0:T(2,128)} %copy-done.25, f32[64]{0:T(128)} %copy-done.32, f32[2,2048]{1,0:T(2,128)} %copy-done.24, f32[2,2048]{1,0:T(2,128)} %copy-done.23, ...), kind=kOutput, calls=%fused_computation.33 | convolution fusion | flops 1111232512 | bytes 68518144 | tf_op jit(solution)/shard_map/gse,he->gsh/dot_general | solution.py:84
  2040.5 0.5 slice.9
  2042.4 0.0 all-reduce.2.cloned.1.call-done
  2042.4 1.9 copy.85
  (58 shorter events, 0.1 us)
Async XLA Ops:
  7.2 4.5 copy-start
  7.2 18.5 copy-start.17
  7.2 17.5 copy-start.20
  10.0 41.3 %copy-start.9 = (bf16[2,2048,64]{1,2,0:T(8,128)(2,1)}, bf16[2,2048,64]{1,2,0:T(8,128)(2,1)S(1)}, u32[]{:S(2)}) copy-start(bf16[2,2048,64]{1,2,0:T(8,128)(2,1)S(1)} %fusion.105) | copy-start | bytes 1572868
  10.9 40.4 %copy-start.4 = (bf16[2,2048,64]{1,2,0:T(8,128)(2,1)}, bf16[2,2048,64]{1,2,0:T(8,128)(2,1)S(1)}, u32[]{:S(2)}) copy-start(bf16[2,2048,64]{1,2,0:T(8,128)(2,1)S(1)} %fusion.122) | copy-start | bytes 1572868
  22.6 4.3 copy-start.3
  24.7 1.0 copy-start.1
  24.7 2.2 copy-start.14
  24.8 26.5 %copy-start.6 = (bf16[2,2048,64]{1,2,0:T(8,128)(2,1)}, bf16[2,2048,64]{1,2,0:T(8,128)(2,1)S(1)}, u32[]{:S(2)}) copy-start(bf16[2,2048,64]{1,2,0:T(8,128)(2,1)S(1)} %fusion.112) | copy-start | bytes 1572868
  26.9 24.4 %copy-start.26 = (f32[2,2048]{1,0:T(2,128)}, f32[2,2048]{1,0:T(2,128)S(1)}, u32[]{:S(2)}) copy-start(f32[2,2048]{1,0:T(2,128)S(1)} %get-tuple-element.9) | copy-start | bytes 49156
  26.9 24.4 %copy-start.28 = (f32[2,2048]{1,0:T(2,128)}, f32[2,2048]{1,0:T(2,128)S(1)}, u32[]{:S(2)}) copy-start(f32[2,2048]{1,0:T(2,128)S(1)} %get-tuple-element.10) | copy-start | bytes 49156
  28.9 22.4 %copy-start.11 = (bf16[2,2048,64]{1,2,0:T(8,128)(2,1)}, bf16[2,2048,64]{1,2,0:T(8,128)(2,1)S(1)}, u32[]{:S(2)}) copy-start(bf16[2,2048,64]{1,2,0:T(8,128)(2,1)S(1)} %fusion.96) | copy-start | bytes 1572868
  160.5 371.0 %all-to-all-start.2 = ((bf16[64,2,64,2048]{3,2,1,0:T(8,128)(2,1)}), bf16[64,2,64,2048]{3,2,1,0:T(8,128)(2,1)}, u32[]{:S(2)}, u32[]{:S(2)}) async-start(bf16[64,2,64,2048]{3,2,1,0:T(8,128)(2,1)} %copy.25), calls=%async_computation.2 | async-start | bytes 67108864 | tf_op jit(solution)/shard_map/all_to_all | solution.py:68
  531.4 370.2 %all-to-all-start = ((bf16[64,2,64,2048]{3,2,1,0:T(8,128)(2,1)}), bf16[64,2,64,2048]{3,2,1,0:T(8,128)(2,1)}, u32[]{:S(2)}, u32[]{:S(2)}) async-start(bf16[64,2,64,2048]{3,2,1,0:T(8,128)(2,1)} %copy.20), calls=%async_computation | async-start | bytes 67108864 | tf_op jit(solution)/shard_map/all_to_all | solution.py:52
  1104.9 369.7 %all-to-all-start.1 = ((bf16[8,16,64,2048]{3,2,0,1:T(8,128)(2,1)}), bf16[8,16,64,2048]{3,2,0,1:T(8,128)(2,1)}, u32[]{:S(2)}, u32[]{:S(2)}) async-start(bf16[8,16,64,2048]{3,2,0,1:T(8,128)(2,1)} %copy.22), calls=%async_computation.1 | async-start | bytes 67108864 | tf_op jit(solution)/shard_map/all_to_all | solution.py:56
  1276.7 203.9 %copy-start.7 = (bf16[2,2048,64]{1,2,0:T(8,128)(2,1)S(1)}, bf16[2,2048,64]{1,2,0:T(8,128)(2,1)}, u32[]{:S(2)}) copy-start(bf16[2,2048,64]{1,2,0:T(8,128)(2,1)} %copy-done.6) | copy-start | bytes 1572868
  1276.7 203.9 %copy-start.12 = (bf16[2,2048,64]{1,2,0:T(8,128)(2,1)S(1)}, bf16[2,2048,64]{1,2,0:T(8,128)(2,1)}, u32[]{:S(2)}) copy-start(bf16[2,2048,64]{1,2,0:T(8,128)(2,1)} %copy-done.11) | copy-start | bytes 1572868
  1474.6 398.4 %all-to-all-start.3 = ((bf16[8,16,64,2048]{3,2,0,1:T(8,128)(2,1)}), bf16[8,16,64,2048]{3,2,0,1:T(8,128)(2,1)}, u32[]{:S(2)}, u32[]{:S(2)}) async-start(bf16[8,16,64,2048]{3,2,0,1:T(8,128)(2,1)} %copy.27), calls=%async_computation.3 | async-start | bytes 67108864 | tf_op jit(solution)/shard_map/all_to_all | solution.py:74
  1480.5 561.9 %all-reduce.2.cloned.1.call-start = ((), (), s32[]{:S(2)}) async-start(), calls=%async_computation.4 | async-start | bytes 1048576 | tf_op jit(solution)/shard_map/psum | solution.py:86
  1480.6 124.5 %copy-start.5 = (bf16[2,2048,64]{1,2,0:T(8,128)(2,1)S(1)}, bf16[2,2048,64]{1,2,0:T(8,128)(2,1)}, u32[]{:S(2)}) copy-start(bf16[2,2048,64]{1,2,0:T(8,128)(2,1)} %copy-done.4) | copy-start | bytes 1572868
  1480.6 124.5 %copy-start.10 = (bf16[2,2048,64]{1,2,0:T(8,128)(2,1)S(1)}, bf16[2,2048,64]{1,2,0:T(8,128)(2,1)}, u32[]{:S(2)}) copy-start(bf16[2,2048,64]{1,2,0:T(8,128)(2,1)} %copy-done.9) | copy-start | bytes 1572868
  1480.6 124.5 %copy-start.30 = (f32[2,2048]{1,0:T(2,128)S(1)}, f32[2,2048]{1,0:T(2,128)}, u32[]{:S(2)}) copy-start(f32[2,2048]{1,0:T(2,128)} %get-tuple-element.13) | copy-start | bytes 49156
  1480.6 124.5 %copy-start.31 = (f32[2,2048]{1,0:T(2,128)S(1)}, f32[2,2048]{1,0:T(2,128)}, u32[]{:S(2)}) copy-start(f32[2,2048]{1,0:T(2,128)} %get-tuple-element.21) | copy-start | bytes 49156
  1605.1 126.7 %copy-start.35 = (f32[64]{0:T(128)S(1)}, f32[64]{0:T(128)}, u32[]{:S(2)}) copy-start(f32[64]{0:T(128)} %get-tuple-element.8) | copy-start | bytes 772
  1605.1 126.7 %copy-start.36 = (f32[64]{0:T(128)S(1)}, f32[64]{0:T(128)}, u32[]{:S(2)}) copy-start(f32[64]{0:T(128)} %get-tuple-element.11) | copy-start | bytes 772
  1605.1 256.6 %copy-start.27 = (f32[2,2048]{1,0:T(2,128)S(1)}, f32[2,2048]{1,0:T(2,128)}, u32[]{:S(2)}) copy-start(f32[2,2048]{1,0:T(2,128)} %copy-done.26) | copy-start | bytes 49156
  1605.1 256.6 %copy-start.29 = (f32[2,2048]{1,0:T(2,128)S(1)}, f32[2,2048]{1,0:T(2,128)}, u32[]{:S(2)}) copy-start(f32[2,2048]{1,0:T(2,128)} %copy-done.28) | copy-start | bytes 49156
  1605.1 256.7 %copy-start.2 = (f32[2,2048,64]{1,2,0:T(8,128)S(1)}, f32[2,2048,64]{1,2,0:T(8,128)}, u32[]{:S(2)}) copy-start(f32[2,2048,64]{1,2,0:T(8,128)} %copy-done.1) | copy-start | bytes 3145732
  1605.1 256.7 %copy-start.15 = (f32[2,2048]{1,0:T(2,128)S(1)}, f32[2,2048]{1,0:T(2,128)}, u32[]{:S(2)}) copy-start(f32[2,2048]{1,0:T(2,128)} %copy-done.14) | copy-start | bytes 49156
  1605.2 256.7 %copy-start.18 = (s32[2,2048]{1,0:T(2,128)S(1)}, s32[2,2048]{1,0:T(2,128)}, u32[]{:S(2)}) copy-start(s32[2,2048]{1,0:T(2,128)} %param.13) | copy-start | bytes 49156
  1605.2 256.7 %copy-start.21 = (s32[2,2048]{1,0:T(2,128)S(1)}, s32[2,2048]{1,0:T(2,128)}, u32[]{:S(2)}) copy-start(s32[2,2048]{1,0:T(2,128)} %param.14) | copy-start | bytes 49156
  1605.2 267.9 %copy-start.8 = (bf16[2,2048,64]{1,2,0:T(8,128)(2,1)S(1)}, bf16[2,2048,64]{1,2,0:T(8,128)(2,1)}, u32[]{:S(2)}) copy-start(bf16[2,2048,64]{1,2,0:T(8,128)(2,1)} %copy-done.6) | copy-start | bytes 1572868
  1605.2 267.9 %copy-start.13 = (bf16[2,2048,64]{1,2,0:T(8,128)(2,1)S(1)}, bf16[2,2048,64]{1,2,0:T(8,128)(2,1)}, u32[]{:S(2)}) copy-start(bf16[2,2048,64]{1,2,0:T(8,128)(2,1)} %copy-done.11) | copy-start | bytes 1572868
  1861.0 0.8 copy-start.33
  1861.7 151.7 %copy-start.32 = (f32[64]{0:T(128)}, f32[64]{0:T(128)S(1)}, u32[]{:S(2)}) copy-start(f32[64]{0:T(128)S(1)} %get-tuple-element.23) | copy-start | bytes 772
  1861.8 151.6 %copy-start.23 = (f32[2,2048]{1,0:T(2,128)}, f32[2,2048]{1,0:T(2,128)S(1)}, u32[]{:S(2)}) copy-start(f32[2,2048]{1,0:T(2,128)S(1)} %get-tuple-element.19) | copy-start | bytes 49156
  1861.8 151.6 %copy-start.24 = (f32[2,2048]{1,0:T(2,128)}, f32[2,2048]{1,0:T(2,128)S(1)}, u32[]{:S(2)}) copy-start(f32[2,2048]{1,0:T(2,128)S(1)} %get-tuple-element.20) | copy-start | bytes 49156
  1862.4 151.1 %copy-start.25 = (f32[2,2048]{1,0:T(2,128)}, f32[2,2048]{1,0:T(2,128)S(1)}, u32[]{:S(2)}) copy-start(f32[2,2048]{1,0:T(2,128)S(1)} %multiply_reduce_fusion) | copy-start | bytes 49156
  1873.1 140.4 %copy-start.16 = (f32[2,2048]{1,0:T(2,128)S(1)}, f32[2,2048]{1,0:T(2,128)}, u32[]{:S(2)}) copy-start(f32[2,2048]{1,0:T(2,128)} %copy-done.14) | copy-start | bytes 49156
  1873.1 140.4 %copy-start.19 = (s32[2,2048]{1,0:T(2,128)S(1)}, s32[2,2048]{1,0:T(2,128)}, u32[]{:S(2)}) copy-start(s32[2,2048]{1,0:T(2,128)} %param.13) | copy-start | bytes 49156
  1873.1 140.4 %copy-start.22 = (s32[2,2048]{1,0:T(2,128)S(1)}, s32[2,2048]{1,0:T(2,128)}, u32[]{:S(2)}) copy-start(s32[2,2048]{1,0:T(2,128)} %param.14) | copy-start | bytes 49156
  2013.5 27.0 %copy-start.34 = (f32[129]{0:T(256)S(1)}, f32[129]{0:T(256)}, u32[]{:S(2)}) copy-start(f32[129]{0:T(256)} %copy-done.33) | copy-start | bytes 1552
Sparse Core Ops, SparseCore 0:
  1873.1 44.1 all-reduce.1
where the time goes:
time: 2060 us; the launch traced here: 2050 us
  matrix products  917 us (45%)
  waiting for transfers between devices  779 us (38%)
  local copies, waits for them, and re-layouts  141 us (7%)
  blocking collectives  129 us (6%)
  other arithmetic  44.4 us (2%)
  starting transfers between devices  24 us (1%)
    all_to_all x1, waiting for transfers between devices, layer_body(): expert_x = lax.all_to_all(send_x, 'ep', 0, 1, tiled=True)  325 us
    all_to_all x1, waiting for transfers between devices, layer_body(): grad_y = lax.all_to_all(grad_send, 'ep', 0, 1, tiled=True)  256 us
    all_to_all x1, waiting for transfers between devices, layer_body(): back_y = lax.all_to_all(expert_y, 'ep', 1, 0, tiled=True)  198 us
    dot_general x1, matrix products, layer_body(): jnp.einsum('gsec,egch->gsh', dispatch, grad_back, preferred_element_type=...  140 us
    psum x1, blocking collectives, layer_body(): global_stats = lax.psum(local_stats, 'ep')  129 us
    dot_general x1, matrix products, layer_body(): jnp.einsum('gsec,egch->gsh', disp_first, back_y, preferred_element_type=j...  125 us
    dot_general x1, matrix products, layer_body(): jnp.einsum('gsec,egch->gsh', disp_second, back_y, preferred_element_type=...  124 us
    dot_general x1, matrix products, layer_body(): jnp.einsum('gsec,gsh->egch', dispatch, x_loc, preferred_element_type=jnp....  86.2 us
  transfers between devices with their start and end apart: 5, of which 3 were waited for; matrix products, arithmetic and copies ran while one was open for 36% of the time, Pallas kernels for 0%

commit v1 on v0

v1 whole, which is shorter than its diff:
```python
import functools

import jax
import jax.numpy as jnp
from jax import lax
from jax.experimental import pallas as pl
from jax.experimental.pallas import tpu as pltpu
from jax.sharding import PartitionSpec as P


ALPHA = 0.01
LANES = 128
MIB = 1024 * 1024
BATCH = 16
bf16, f32 = jnp.bfloat16, jnp.float32


def gelu_bf16(pre_act):
    return jax.nn.gelu(pre_act, approximate=True).astype(bf16)


def cost(flops, moved):
    return pl.CostEstimate(flops=flops, bytes_accessed=moved, transcendentals=0)


def move_rows(idx_ref, base, count, load, store):
    def step(i, _):
        ids = [idx_ref[base + i * BATCH + u] for u in range(BATCH)]
        for u, row in enumerate([load(k) for k in ids]):
            store(i * BATCH + u, row)
        return 0

    lax.fori_loop(0, count // BATCH, step, 0)


def gather_kernel(idx_ref, tiles_ref, *outs, ranges, rows):
    base = pl.program_id(0) * rows
    for (low, high), out_ref in zip(ranges, outs):
        def store(t, row, out_ref=out_ref):
            out_ref[0, t] = row

        move_rows(idx_ref, base + low, high - low, lambda k: tiles_ref[k], store)


def gather_rows(idx, tiles, ranges):
    peers, rows = idx.shape
    count, sub, _ = tiles.shape
    return pl.pallas_call(
        functools.partial(gather_kernel, ranges=ranges, rows=rows),
        grid_spec=pltpu.PrefetchScalarGridSpec(
            num_scalar_prefetch=1,
            grid=(peers,),
            in_specs=[pl.BlockSpec((count, sub, LANES), lambda p, idx: (0, 0, 0))],
            out_specs=[pl.BlockSpec((1, high - low, sub, LANES), lambda p, idx: (p, 0, 0, 0)) for low, high in ranges],
        ),
        out_shape=[jax.ShapeDtypeStruct((peers, high - low, sub, LANES), tiles.dtype) for low, high in ranges],
        compiler_params=pltpu.CompilerParams(vmem_limit_bytes=52 * MIB),
        cost_estimate=cost(30_000_000_000, 60_000_000),
    )(idx.reshape(-1), tiles)


def unpack_kernel(idx_ref, *refs, ranges, scaled, empty, block):
    count = len(ranges)
    parts, refs = refs[:count], refs[count:]
    if scaled:
        norm_ref, y_ref, out_ref, dot_ref, packed, acc_ref, sem = refs
    else:
        out_ref, packed, acc_ref, sem = refs
    peer, local = pl.program_id(0), pl.program_id(1)
    slot = lax.rem(peer, 2)

    def copies(p, s):
        return [pltpu.make_async_copy(part.at[p], packed.at[s, pl.ds(low, high - low)], sem.at[s, k])
                for k, (part, (low, high)) in enumerate(zip(parts, ranges))]

    @pl.when((peer == 0) & (local == 0))
    def _():
        blank = jnp.zeros((2, packed.shape[1] - empty) + packed.shape[2:], bf16)
        packed[:, empty:] = blank
        for copy in copies(0, 0):
            copy.start()

    @pl.when(local == 0)
    def _():
        @pl.when(peer + 1 < pl.num_programs(0))
        def _():
            for copy in copies(peer + 1, 1 - slot):
                copy.start()

        for copy in copies(peer, slot):
            copy.wait()

    base = (peer * pl.num_programs(1) + local) * block
    sub = packed.shape[2]
    pitch = sub + 1

    def store(t, row):
        acc_ref[pl.ds(t * pitch, sub), :] = row.astype(f32)

    move_rows(idx_ref, base, block, lambda k: packed[slot, k], store)
    total = None
    for j in range(sub):
        cols = slice(j * LANES, (j + 1) * LANES)
        tile = acc_ref[pl.ds(j, block, stride=pitch), :]
        if scaled:
            out_ref[0, 0, :, cols] = (norm_ref[0, 0] * tile).astype(bf16)
            product = y_ref[0, 0, :, cols].astype(f32) * tile
            total = product if total is None else total + product
        else:
            out_ref[0, 0, :, cols] = tile.astype(bf16)
    if scaled:
        dot_ref[0, 0] = total


def unpack_rows(idx, parts, ranges, empty, norm=None, y=None, first=0):
    peers, local, block = idx.shape
    sub = parts[0].shape[2]
    hidden = sub * LANES
    scaled = norm is not None
    spec = lambda width, off=0: pl.BlockSpec((1, 1, block, width), lambda p, e, idx: (e + off, p, 0, 0))
    ins = [pl.BlockSpec(memory_space=pl.ANY)] * len(parts)
    out_shape = [jax.ShapeDtypeStruct((local, peers, block, hidden), bf16)]
    if scaled:
        ins += [spec(1, first), spec(hidden, first)]
        out_shape.append(jax.ShapeDtypeStruct((local, peers, block, LANES), f32))
    out = pl.pallas_call(
        functools.partial(unpack_kernel, ranges=ranges, scaled=scaled, empty=empty, block=block),
        grid_spec=pltpu.PrefetchScalarGridSpec(
            num_scalar_prefetch=1,
            grid=(peers, local),
            in_specs=ins,
            out_specs=[spec(s.shape[-1]) for s in out_shape],
            scratch_shapes=[
                pltpu.VMEM((2, empty + 8, sub, LANES), bf16),
                pltpu.VMEM((block * (sub + 1), LANES), f32),
                pltpu.SemaphoreType.DMA((2, len(parts))),
            ],
        ),
        out_shape=out_shape,
        compiler_params=pltpu.CompilerParams(vmem_limit_bytes=32 * MIB),
        cost_estimate=cost(3_500_000_000 * local, 8_000_000 * local),
    )(idx.reshape(-1), *parts, *((norm, y) if scaled else ()))
    return out if scaled else out[0]


def pack_kernel(idx_ref, *refs, ranges, rows, count):
    ins, outs, acc_ref = refs[:count], refs[count:-1], refs[-1]
    base = pl.program_id(0) * rows
    sub = outs[0].shape[2]
    pitch = sub + 1
    at = 0
    for ref in ins:
        for e in range(ref.shape[0]):
            block = ref.shape[2]
            for j in range(sub):
                acc_ref[pl.ds(at * pitch + j, block, stride=pitch), :] = ref[e, 0, :, j * LANES:(j + 1) * LANES].astype(f32)
            at += block
    for (low, high), out_ref in zip(ranges, outs):
        def store(t, row, out_ref=out_ref):
            out_ref[0, t] = row.astype(bf16)

        move_rows(idx_ref, base + low, high - low, lambda k: acc_ref[pl.ds(k * pitch, sub), :], store)


def pack_rows(idx, grads, ranges):
    peers, rows = idx.shape
    block, hidden = grads[0].shape[2:]
    sub = hidden // LANES
    total = sum(g.shape[0] for g in grads) * block
    return pl.pallas_call(
        functools.partial(pack_kernel, ranges=ranges, rows=rows, count=len(grads)),
        grid_spec=pltpu.PrefetchScalarGridSpec(
            num_scalar_prefetch=1,
            grid=(peers,),
            in_specs=[pl.BlockSpec((g.shape[0], 1, block, hidden), lambda p, idx: (0, p, 0, 0)) for g in grads],
            out_specs=[pl.BlockSpec((1, high - low, sub, LANES), lambda p, idx: (p, 0, 0, 0)) for low, high in ranges],
            scratch_shapes=[pltpu.VMEM((total * (sub + 1), LANES), f32)],
        ),
        out_shape=[jax.ShapeDtypeStruct((peers, high - low, sub, LANES), bf16) for low, high in ranges],
        compiler_params=pltpu.CompilerParams(vmem_limit_bytes=40 * MIB),
        cost_estimate=cost(15_000_000_000, 35_000_000),
    )(idx.reshape(-1), *grads)


def combine_kernel(slot_ref, *refs, ranges, rows):
    count = len(ranges)
    parts, (r_ref, gl_ref, wg_ref, out_ref, held, acc_ref, sem) = refs[:count], refs[count:]
    block = out_ref.shape[0]
    tokens = slot_ref.shape[0] // 2
    base = pl.program_id(0) * block

    sub = held.shape[1]
    pitch = sub + 1
    peers = parts[0].shape[0]

    @pl.when(pl.program_id(0) == 0)
    def _():
        copies = [pltpu.make_async_copy(part.at[p], held.at[pl.ds(p * rows + low, high - low)], sem.at[k, p])
                  for k, (part, (low, high)) in enumerate(zip(parts, ranges)) for p in range(peers)]
        for copy in copies:
            copy.start()
        held[peers * rows:] = jnp.zeros((held.shape[0] - peers * rows,) + held.shape[1:], bf16)
        for copy in copies:
            copy.wait()

    def step(i, _):
        ones = [slot_ref[base + i * 8 + u] for u in range(8)]
        twos = [slot_ref[base + tokens + i * 8 + u] for u in range(8)]
        sums = [held[one].astype(f32) + held[two].astype(f32) for one, two in zip(ones, twos)]
        for u, row in enumerate(sums):
            acc_ref[pl.ds((i * 8 + u) * pitch, sub), :] = row
        return 0

    lax.fori_loop(0, block // 8, step, 0)
    router = lax.dot_general(gl_ref[...], wg_ref[...], (((1,), (1,)), ((), ())), preferred_element_type=f32)
    for j in range(sub):
        cols = slice(j * LANES, (j + 1) * LANES)
        out_ref[:, cols] = (r_ref[:, cols].astype(f32) + acc_ref[pl.ds(j, block, stride=pitch), :] + router[:, cols]).astype(bf16)


def combine_rows(slots_of, parts, ranges, r_rows, grad_logits, w_gate):
    tokens, hidden = r_rows.shape
    experts = w_gate.shape[1]
    peers, sub = parts[0].shape[0], parts[0].shape[2]
    rows = ranges[-1][1]
    block = 256
    return pl.pallas_call(
        functools.partial(combine_kernel, ranges=ranges, rows=rows),
        grid_spec=pltpu.PrefetchScalarGridSpec(
            num_scalar_prefetch=1,
            grid=(tokens // block,),
            in_specs=[pl.BlockSpec(memory_space=pl.ANY)] * len(parts) + [
                pl.BlockSpec((block, hidden), lambda b, s: (b, 0)),
                pl.BlockSpec((block, experts), lambda b, s: (b, 0)),
                pl.BlockSpec((hidden, experts), lambda b, s: (0, 0)),
            ],
            out_specs=pl.BlockSpec((block, hidden), lambda b, s: (b, 0)),
            scratch_shapes=[
                pltpu.VMEM((peers * rows + 8, sub, LANES), bf16),
                pltpu.VMEM((block * (sub + 1), LANES), f32),
                pltpu.SemaphoreType.DMA((len(parts), peers)),
            ],
        ),
        out_shape=jax.ShapeDtypeStruct(r_rows.shape, bf16),
        compiler_params=pltpu.CompilerParams(vmem_limit_bytes=52 * MIB),
        cost_estimate=cost(50_000_000_000, 80_000_000),
    )(slots_of.reshape(-1), *parts, r_rows, grad_logits, w_gate)


def solution(mesh):
    ep_size = mesh.shape['ep']

    def layer_body(x_loc, r_loc, w_gate, w_in_loc, w_out_loc, first_ids, second_ids, keep_ids):
        groups, seq_len, hidden = x_loc.shape
        experts = w_gate.shape[1]
        local_experts = experts // ep_size
        half = local_experts // 2
        cap_rows = 2 * seq_len // experts
        block = groups * cap_rows
        rows = local_experts * block
        mid = rows // 2
        sub = hidden // LANES
        tokens_loc = groups * seq_len
        tokens_all = tokens_loc * ep_size
        numel = tokens_all * hidden
        me = lax.axis_index('ep')
        exchange = lambda v: lax.all_to_all(v, 'ep', 0, 0, tiled=True)

        expert_ids = jnp.arange(experts, dtype=jnp.int32)
        first_hot = (first_ids[..., None] == expert_ids).astype(bf16)
        second_hot = (second_ids[..., None] == expert_ids).astype(bf16)
        second_kept = second_hot * keep_ids.astype(bf16)[..., None]
        seq_ids = jnp.arange(seq_len, dtype=jnp.int32)
        earlier = (seq_ids[:, None] > seq_ids[None, :]).astype(bf16)
        before_first = jnp.einsum('st,gte->gse', earlier, first_hot, preferred_element_type=f32)
        before_second = jnp.einsum('st,gte->gse', earlier, second_kept, preferred_element_type=f32)
        first_count = jnp.sum(first_hot, axis=1, dtype=f32)
        occupied = jnp.minimum(first_count + jnp.sum(second_kept, axis=1, dtype=f32), cap_rows)
        segments = lambda v: jnp.moveaxis(v.reshape(groups, ep_size, local_experts), 0, 2).reshape(ep_size, local_experts * groups)
        held = segments(occupied)
        starts = jnp.cumsum(held, axis=1) - held
        lead = rows - jnp.sum(held, axis=1, keepdims=True)
        place = jnp.arange(ep_size, dtype=f32)[:, None] * rows + starts
        unsegment = lambda v: jnp.moveaxis(v.reshape(ep_size, local_experts, groups), 2, 0).reshape(groups, experts)
        place_of, lead_of = unsegment(place), unsegment(jnp.broadcast_to(lead, place.shape))

        def locate(hot, before):
            pos = jnp.sum(before * hot, axis=-1)
            there = jnp.sum(place_of[:, None, :] * hot, axis=-1) + pos
            back = there + jnp.sum(lead_of[:, None, :] * hot, axis=-1)
            return pos.astype(jnp.int32), there.astype(jnp.int32), back.astype(jnp.int32)

        pos_first, there_first, back_first = locate(first_hot, before_first)
        pos_second, there_second, back_second = locate(second_hot, before_second + first_count[:, None, :])
        ok_first = pos_first < cap_rows
        ok_second = (keep_ids > 0) & (pos_second < cap_rows)
        slots_of = jnp.stack([jnp.where(ok_first, back_first, ep_size * rows), jnp.where(ok_second, back_second, ep_size * rows)])

        there = jnp.stack([jnp.where(ok_first, there_first, -1), jnp.where(ok_second, there_second, -1)]).reshape(-1)
        numbers = jnp.arange(2 * tokens_loc, dtype=jnp.int32) % tokens_loc + 1
        outer = ((there // 64)[:, None] == jnp.arange(ep_size * rows // 64, dtype=jnp.int32)).astype(bf16)
        inner = ((there % 64)[:, None] == jnp.arange(64, dtype=jnp.int32)) & (there >= 0)[:, None]
        digits = jnp.concatenate([jnp.where(inner, v.astype(bf16)[:, None], 0) for v in (numbers // 64, numbers % 64)], axis=-1)
        table = jnp.einsum('so,si->oi', outer, digits, preferred_element_type=f32)
        send_idx = jnp.maximum((table[:, :64] * 64 + table[:, 64:]).astype(jnp.int32) - 1, 0).reshape(ep_size, rows)

        x_tiles = x_loc.reshape(tokens_loc, sub, LANES)
        r_tiles = r_loc.reshape(tokens_loc, sub, LANES)
        x_ranges = ((0, rows),)
        r_ranges = ((0, mid), (mid, rows))
        x_send, = gather_rows(send_idx, x_tiles, x_ranges)

        counts = lax.all_gather(jnp.stack([first_count, occupied]), 'ep')
        frac_first = jnp.sum(counts[:, 0], axis=(0, 1)) / tokens_all
        mine = lax.dynamic_slice_in_dim(counts[:, 1], me * local_experts, local_experts, axis=2)
        mine = jnp.moveaxis(mine, 1, 2).reshape(ep_size, local_experts * groups)
        mine_ends = jnp.cumsum(mine, axis=1)
        mine_starts = mine_ends - mine
        slot_ids = jnp.arange(cap_rows, dtype=f32)
        recv_idx = jnp.where(slot_ids < mine[..., None], mine_starts[..., None] + slot_ids, float(rows)).astype(jnp.int32)
        recv_idx = recv_idx.reshape(ep_size, local_experts, block)
        packed = jnp.arange(rows, dtype=f32) - (rows - mine_ends[:, -1:])
        passed = (mine_ends[:, None, :] <= packed[..., None]).astype(f32)
        back_row = jnp.sum(passed, axis=-1) * cap_rows + packed - jnp.sum(passed * mine[:, None, :], axis=-1)
        back_idx = jnp.where(packed >= 0, back_row, 0.0).astype(jnp.int32)

        tie = lambda *values: lax.optimization_barrier(values)
        x_send, recv_idx, back_idx, frac_first = tie(x_send, recv_idx, back_idx, frac_first)
        x_recv = exchange(x_send)
        x_here, r_here, r_tiles, _ = tie(x_loc, r_loc, r_tiles, x_send)
        r_send_0, r_send_1 = gather_rows(send_idx, r_tiles, r_ranges)

        logits = jnp.einsum('gsh,he->gse', x_here, w_gate, preferred_element_type=f32)
        router_prob = jax.nn.softmax(logits, axis=-1)
        gate_first = jnp.sum(router_prob * first_hot, axis=-1)
        gate_second = jnp.sum(router_prob * second_hot, axis=-1)
        gate_sum = gate_first + gate_second
        norm_first = (gate_first / gate_sum).astype(bf16)
        norm_second = (gate_second / gate_sum).astype(bf16)
        slots = jnp.arange(cap_rows, dtype=jnp.int32)
        at_first = ((pos_first[..., None] == slots) & ok_first[..., None]).astype(bf16)
        at_second = ((pos_second[..., None] == slots) & ok_second[..., None]).astype(bf16)
        hots = jnp.concatenate([first_hot, second_hot], axis=1)
        norm_at = jnp.concatenate([at_first * norm_first[..., None], at_second * norm_second[..., None]], axis=1)
        slot_norm = jnp.einsum('gse,gsk->egk', hots, norm_at, preferred_element_type=f32)
        dot_xr = jnp.sum(x_here.astype(f32) * r_here.astype(f32))
        slot_norm, x_recv = tie(slot_norm, x_recv)
        expert_norm = lax.all_to_all(slot_norm, 'ep', 0, 1, tiled=True).reshape(local_experts, ep_size, block)

        r_send_0, expert_norm, dot_xr = tie(r_send_0, expert_norm, dot_xr)
        r_recv_0 = exchange(r_send_0)
        expert_x = unpack_rows(recv_idx, [x_recv], x_ranges, rows).reshape(local_experts, -1, hidden)
        pre_act = jnp.einsum('ech,ehf->ecf', expert_x, w_in_loc, preferred_element_type=f32)
        act_bf = gelu_bf16(pre_act)
        expert_y = jnp.einsum('ecf,efh->ech', act_bf, w_out_loc, preferred_element_type=f32).astype(bf16)

        r_send_1, expert_y, r_recv_0 = tie(r_send_1, expert_y, r_recv_0)
        r_recv_1 = exchange(r_send_1)

        def expert_bwd(parts, ranges, which):
            chunk = slice(which * half, (which + 1) * half)
            grad_y, dots = unpack_rows(recv_idx[:, chunk], parts, ranges, rows, expert_norm[..., None], expert_y.reshape(local_experts, ep_size, block, hidden), which * half)
            slot_dot = jnp.sum(dots, axis=-1)
            grad_y = grad_y.reshape(half, -1, hidden)
            grad_act = jnp.einsum('ech,efh->ecf', grad_y, w_out_loc[chunk], preferred_element_type=f32).astype(bf16)
            grad_pre = jax.vjp(gelu_bf16, pre_act[chunk])[1](grad_act)[0].astype(bf16)
            grad_slots = jnp.einsum('ecf,ehf->ech', grad_pre, w_in_loc[chunk], preferred_element_type=f32).astype(bf16)
            return grad_y, grad_pre, slot_dot, grad_slots.reshape(half, ep_size, block, hidden)

        grad_y_0, grad_pre_0, slot_dot_0, grad_slots_0 = expert_bwd([r_recv_0], r_ranges[:1], 0)
        g_send_0, = pack_rows(back_idx, [grad_slots_0], ((0, mid),))
        g_send_0, r_recv_1 = tie(g_send_0, r_recv_1)
        g_recv_0 = exchange(g_send_0)
        grad_y_1, grad_pre_1, slot_dot_1, grad_slots_1 = expert_bwd([r_recv_0, r_recv_1], r_ranges, 1)
        g_send_1, = pack_rows(back_idx, [grad_slots_0, grad_slots_1], ((mid, rows),))
        slot_dot = jnp.concatenate([slot_dot_0, slot_dot_1], axis=0)
        slot_dot, g_send_1, g_recv_0 = tie(slot_dot, g_send_1, g_recv_0)
        home_dot = lax.all_to_all(slot_dot.reshape(local_experts, ep_size * groups, cap_rows), 'ep', 1, 0, tiled=True)
        g_send_1, home_dot = tie(g_send_1, home_dot)
        g_recv_1 = exchange(g_send_1)

        grad_y = jnp.concatenate([grad_y_0, grad_y_1], axis=0)
        grad_pre = jnp.concatenate([grad_pre_0, grad_pre_1], axis=0)
        grad_w_out = jnp.einsum('ecf,ech->efh', act_bf, grad_y, preferred_element_type=f32).astype(bf16)
        grad_w_in = jnp.einsum('ech,ecf->ehf', expert_x, grad_pre, preferred_element_type=f32).astype(bf16)

        picked = lambda hot, at: jnp.sum(jnp.einsum('gse,egk->gsk', hot.astype(f32), home_dot, precision=lax.Precision.HIGHEST, preferred_element_type=f32) * at, axis=-1)
        grad_norm_first = picked(first_hot, at_first).astype(bf16).astype(f32)
        grad_norm_second = picked(second_hot, at_second).astype(bf16).astype(f32)
        gate_sq = gate_sum * gate_sum
        grad_gate_first = (grad_norm_first - grad_norm_second) * gate_second / gate_sq
        grad_gate_second = (grad_norm_second - grad_norm_first) * gate_first / gate_sq
        grad_prob = grad_gate_first[..., None] * first_hot + grad_gate_second[..., None] * second_hot + (ALPHA * hidden * experts) * frac_first
        grad_logits = router_prob * (grad_prob - jnp.sum(router_prob * grad_prob, axis=-1, keepdims=True))
        grad_logits_bf = grad_logits.astype(bf16)
        grad_gate_w = jnp.einsum('gsh,gse->he', x_loc, grad_logits_bf, preferred_element_type=f32)
        dot_sum = dot_xr + jnp.sum(slot_dot * expert_norm)
        stats = jnp.stack([jnp.sum(router_prob, axis=(0, 1)), jnp.broadcast_to(dot_sum, (experts,))])
        summed = lax.psum(jnp.concatenate([grad_gate_w, stats], axis=0), 'ep')
        grad_gate_w, prob_sum, dot_sum = summed[:hidden], summed[hidden], summed[hidden + 1, 0]
        loss_value = dot_sum / numel + ALPHA * experts * jnp.sum(frac_first * prob_sum / tokens_all)

        grad_x = combine_rows(slots_of, [g_recv_0, g_recv_1], ((0, mid), (mid, rows)), r_loc.reshape(-1, hidden), grad_logits_bf.reshape(-1, experts), w_gate)
        return loss_value, grad_x.reshape(x_loc.shape), grad_w_in, grad_w_out, grad_gate_w

    row_spec = P('ep', None, None)
    id_spec = P('ep', None)
    return jax.shard_map(layer_body, mesh=mesh, in_specs=(row_spec, row_spec, P(None, None), row_spec, row_spec, id_spec, id_spec, id_spec), out_specs=(P(), row_spec, row_spec, row_spec, P(None, None)), check_vma=False)
```

time: 2060 us -> 1330 us (0.65)
  matrix products: 917 us -> 346 us
  Pallas kernels: 0 us -> 240 us
  waiting for transfers between devices: 779 us -> 597 us
  blocking collectives: 129 us -> 13.6 us
  local copies, waits for them, and re-layouts: 141 us -> 48.4 us
    dot_general x14 -> x15, matrix products: 912 us -> 335 us  [the longest x2 68.5 us: expert_bwd(): jnp.einsum('ech,efh->ecf', grad_y, w_out_loc[chunk], preferred_element_ty...]
    all_to_all x4 -> x7, waiting for transfers between devices: 779 us -> 513 us  [the longest x5 508 us: layer_body(): exchange = lambda v: lax.all_to_all(v, 'ep', 0, 0, tiled=True)]
    pallas_call x0 -> x8, Pallas kernels: none -> 240 us  [the longest x3 118 us: unpack_rows(): pl.pallas_call(functools.partial(unpack_kernel, ranges=ranges, scaled=sca...]
    psum x1 -> x0, blocking collectives: 129 us -> none  [layer_body(): global_stats = lax.psum(local_stats, 'ep')]
    convert_element_type x4 -> x1, local copies, waits for them, and re-layouts: 91.8 us -> 0.47 us  [layer_body(): grad_logits_bf = grad_logits.astype(bf16)]
    psum x1, waiting for transfers between devices: 0.02 us -> 84.3 us  [layer_body(): summed = lax.psum(jnp.concatenate([grad_gate_w, stats], axis=0), 'ep')]
    all_to_all x2 -> x4, local copies, waits for them, and re-layouts: 45.8 us -> 0.59 us  [the longest x3 0.58 us: layer_body(): lax.all_to_all(slot_norm, 'ep', 0, 1, tiled=True)]
    unnamed x75 -> x96, local copies, waits for them, and re-layouts: 2.9 us -> 37.2 us
  transfers between devices with their start and end apart: 5 -> 8, of which waited for: 3 -> 6; matrix products, arithmetic and copies ran while one was open for 36% -> 29% of each run, Pallas kernels for 0% -> 14%
where the time goes in v1:
time: 1330 us; the launch traced here: 1320 us
  waiting for transfers between devices  597 us (45%)
  matrix products  346 us (26%)
  Pallas kernels  240 us (18%)
  local copies, waits for them, and re-layouts  48.4 us (4%)
  starting transfers between devices  29.5 us (2%)
  other arithmetic  28.6 us (2%)
  between operations  18.9 us (1%)
  blocking collectives  13.6 us (1%)
    all_to_all x5, waiting for transfers between devices, layer_body(): exchange = lambda v: lax.all_to_all(v, 'ep', 0, 0, tiled=True)  508 us
    pallas_call x3, Pallas kernels, unpack_rows(): pl.pallas_call(functools.partial(unpack_kernel, ranges=ranges, scaled=sca...  118 us
    psum x1, waiting for transfers between devices, layer_body(): summed = lax.psum(jnp.concatenate([grad_gate_w, stats], axis=0), 'ep')  84.3 us
    dot_general x2, matrix products, expert_bwd(): jnp.einsum('ech,efh->ecf', grad_y, w_out_loc[chunk], preferred_element_ty...  68.5 us
    dot_general x1, matrix products, layer_body(): jnp.einsum('ecf,ech->efh', act_bf, grad_y, preferred_element_type=f32)  59.3 us
    dot_general x1, matrix products, layer_body(): jnp.einsum('ecf,efh->ech', act_bf, w_out_loc, preferred_element_type=f32)  51.7 us
    dot_general x2, matrix products, expert_bwd(): jnp.einsum('ecf,ehf->ech', grad_pre, w_in_loc[chunk], preferred_element_t...  49.6 us
    dot_general x1, matrix products, layer_body(): jnp.einsum('ech,ehf->ecf', expert_x, w_in_loc, preferred_element_type=f32)  44.5 us
  transfers between devices with their start and end apart: 8, of which 6 were waited for; matrix products, arithmetic and copies ran while one was open for 29% of the time, Pallas kernels for 14%

profile of v1, /device:TPU:0, one launch (start us, length us, event | category | flops | bytes accessed | tf_op | source)
XLA Modules:
  0.0 1322.5 jit_solution(8461642151009558264)
XLA Ops:
  7.2 0.7 convert_element_type.232
  8.0 1.1 convert_reduce_fusion
  9.1 2.8 fusion.89
  11.9 13.6 %all-gather = f32[16,2,64]{2,1,0:T(2,128)S(1)} all-gather(f32[2,2,64]{2,1,0:T(2,128)S(1)} %pad_maximum_fusion.1), channel_id=2, replica_groups=mesh['ep'=8] {'ep'}, dimensions={0}, use_global_device_ids=true | all-gather | bytes 9216 | tf_op jit(solution)/shard_map/all_gather | solution.py:313
  26.2 2.8 fusion.92
  29.7 0.6 fusion.100
  32.1 0.5 fusion.86
  32.7 1.4 fusion.62
  34.3 15.2 %copy.180 = bf16[512,8,16,128]{3,2,1,0:T(8,128)(2,1)} copy(bf16[512,8,16,128]{3,1,2,0:T(8,128)(2,1)} %bitcast.134) | data formatting | bytes 33554432
  49.4 0.7 select_convert_fusion
  50.1 22.1 %shard_map.119 = bf16[8,1024,16,128]{3,2,1,0:T(8,128)(2,1)} custom-call(s32[8192]{0:T(1024)S(1)} %reshape_reshape.4.idx_ref, bf16[4096,16,128]{2,1,0:T(8,128)(2,1)} %bitcast.140), custom_call_target="tpu_custom_call" | custom-call | flops 30000001024 | bytes 60000000 | tf_op jit(solution)/shard_map/pallas_call | solution.py:48
  72.2 6.5 all-to-all-start
  79.1 15.2 %copy.178 = bf16[512,8,16,128]{3,2,1,0:T(8,128)(2,1)} copy(bf16[512,8,16,128]{3,1,2,0:T(8,128)(2,1)} %bitcast.137) | data formatting | bytes 33554432
  94.3 11.0 fusion.158
  105.4 1.4 fusion.153
  107.9 15.7 %multiply_reduce_fusion = f32[]{:T(128)} fusion(bf16[2,2048,2048]{2,1,0:T(8,128)(2,1)} %param.9, bf16[2,2048,2048]{2,1,0:T(8,128)(2,1)} %param.8), kind=kLoop, calls=%fused_computation.14 | loop fusion | flops 33554432 | bytes 33554436 | tf_op jit(solution)/shard_map/reduce_sum | solution.py:346
  123.6 22.2 %shard_map.120 = (bf16[8,512,16,128]{3,2,1,0:T(8,128)(2,1)}, bf16[8,512,16,128]{3,2,1,0:T(8,128)(2,1)}) custom-call(s32[8192]{0:T(1024)S(1)} %reshape_reshape.4.idx_ref, bf16[4096,16,128]{2,1,0:T(8,128)(2,1)} %bitcast.139), custom_call_target="tpu_custom_call" | custom-call | flops 30000001024 | bytes 60000000 | tf_op jit(solution)/shard_map/pallas_call | solution.py:48
  145.9 296.5 %all-to-all-done.refs_0_ = bf16[8,1024,16,128]{3,2,1,0:T(8,128)(2,1)} async-done(((bf16[8,1024,16,128]{3,2,1,0:T(8,128)(2,1)}), bf16[8,1024,16,128]{3,2,1,0:T(8,128)(2,1)}, u32[]{:S(2)}, u32[]{:S(2)}) %all-to-all-start) | async-done | bytes 33554464 | tf_op jit(solution)/shard_map/all_to_all | solution.py:267
  442.5 0.7 reshape.389
  443.2 2.1 all-to-all-start.1
  445.3 42.5 %shard_map.121 = bf16[8,8,128,2048]{3,2,1,0:T(8,128)(2,1)} custom-call(s32[8192]{0:T(1024)S(1)} %bitcast.128, bf16[8,1024,16,128]{3,2,1,0:T(8,128)(2,1)} %all-to-all-done.refs_0_), custom_call_target="tpu_custom_call" | custom-call | flops 28000000000 | bytes 64000000 | tf_op jit(solution)/shard_map/pallas_call | solution.py:126
  487.8 0.5 broadcast.365
  488.3 0.7 reduce.9
  489.2 0.7 reshape.370
  489.9 4.6 all-to-all-start.2
  494.6 44.5 %fusion.161 = f32[8,1024,1024]{2,1,0:T(8,128)} fusion(bf16[8,1024,2048]{2,1,0:T(8,128)(2,1)} %bitcast.162, bf16[8,2048,1024]{2,1,0:T(8,128)(2,1)} %param.11), kind=kOutput, calls=%fused_computation.219 | convolution fusion | flops 34359738368 | bytes 100663296 | tf_op jit(solution)/shard_map/ech,ehf->ecf/dot_general | solution.py:353
  539.0 51.7 %convolution_convert_fusion.1 = bf16[8,1024,2048]{2,1,0:T(8,128)(2,1)} fusion(bf16[8,1024,2048]{2,1,0:T(8,128)(2,1)} %param.12, f32[8,1024,1024]{2,1,0:T(8,128)} %fusion.161), kind=kOutput, calls=%fused_computation.24 | convolution fusion | flops 34452013056 | bytes 100663296 | tf_op jit(solution)/shard_map/ecf,efh->ech/dot_general | solution.py:355
  590.7 87.8 %all-to-all-done.2.refs_0_ = bf16[8,512,16,128]{3,2,1,0:T(8,128)(2,1)} async-done(((bf16[8,512,16,128]{3,2,1,0:T(8,128)(2,1)}), bf16[8,512,16,128]{3,2,1,0:T(8,128)(2,1)}, u32[]{:S(2)}, u32[]{:S(2)}) %all-to-all-start.2) | async-done | bytes 16777248 | tf_op jit(solution)/shard_map/all_to_all | solution.py:267
  678.5 4.8 all-to-all-start.3
  683.4 2.7 copy.163.refs_1_.refs_2_
  686.0 2.2 copy-done
  688.2 34.8 %shard_map.122 = (bf16[4,8,128,2048]{3,2,1,0:T(8,128)(2,1)}, f32[4,8,128,128]{3,2,1,0:T(8,128)S(1)}) custom-call(s32[4096]{0:T(1024)S(1)} %bitcast.129, bf16[8,512,16,128]{3,2,1,0:T(8,128)(2,1)} %all-to-all-done.2.refs_0_, f32[8,8,128,1]{3,2,1,0:T(8,128)S(1)} %copy-done, bf16[8,8,128,2048]{3,2,1,0:T(8,128)(2,1)} %bitcast.135), custom_call_target="tpu_custom_call" | custom-call | flops 14000000000 | bytes 32000000 | tf_op jit(solution)/shard_map/pallas_call | solution.py:126
  723.0 34.3 %fusion.18 = bf16[4,1024,1024]{2,1,0:T(8,128)(2,1)} fusion(f32[8,1024,1024]{2,1,0:T(8,128)} %fusion.161, bf16[4,1024,2048]{2,1,0:T(8,128)(2,1)} %bitcast.158, bf16[8,1024,2048]{2,1,0:T(8,128)(2,1)} %param.12), kind=kOutput, calls=%fused_computation.28 | convolution fusion | flops 17272143872 | bytes 58720256 | tf_op jit(solution)/shard_map/ech,efh->ecf/dot_general | solution.py:365
  757.3 24.8 %fusion.52 = bf16[4,1024,2048]{2,1,0:T(8,128)(2,1)} fusion(bf16[4,1024,1024]{2,1,0:T(8,128)(2,1)} %fusion.18, bf16[8,2048,1024]{2,1,0:T(8,128)(2,1)} %param.11), kind=kOutput, calls=%fused_computation.61 | convolution fusion | flops 17188257792 | bytes 41943040 | tf_op jit(solution)/shard_map/ecf,ehf->ech/dot_general | solution.py:367
  782.1 18.6 %shard_map.123 = bf16[8,512,16,128]{3,2,1,0:T(8,128)(2,1)} custom-call(s32[8192]{0:T(1024)S(1)} %bitcast.132, bf16[4,8,128,2048]{3,2,1,0:T(8,128)(2,1)} %bitcast.164), custom_call_target="tpu_custom_call" | custom-call | flops 15000000512 | bytes 35000000 | tf_op jit(solution)/shard_map/pallas_call | solution.py:170
  800.8 66.5 %all-to-all-done.3.refs_1_ = bf16[8,512,16,128]{3,2,1,0:T(8,128)(2,1)} async-done(((bf16[8,512,16,128]{3,2,1,0:T(8,128)(2,1)}), bf16[8,512,16,128]{3,2,1,0:T(8,128)(2,1)}, u32[]{:S(2)}, u32[]{:S(2)}) %all-to-all-start.3) | async-done | bytes 16777248 | tf_op jit(solution)/shard_map/all_to_all | solution.py:267
  867.2 4.9 all-to-all-start.4
  872.2 0.5 broadcast_multiply_fusion
  872.8 0.6 reduce_sum.239
  873.5 2.2 copy-done.1
  875.6 40.4 %shard_map.124 = (bf16[4,8,128,2048]{3,2,1,0:T(8,128)(2,1)}, f32[4,8,128,128]{3,2,1,0:T(8,128)S(1)}) custom-call(s32[4096]{0:T(1024)S(1)} %bitcast.130, bf16[8,512,16,128]{3,2,1,0:T(8,128)(2,1)} %all-to-all-done.2.refs_0_, bf16[8,512,16,128]{3,2,1,0:T(8,128)(2,1)} %all-to-all-done.3.refs_1_, f32[8,8,128,1]{3,2,1,0:T(8,128)S(1)} %copy-done.1, ...), custom_call_target="tpu_custom_call" | custom-call | flops 14000000000 | bytes 32000000 | tf_op jit(solution)/shard_map/pallas_call | solution.py:126
  916.0 0.6 reduce_sum.240
  916.6 34.2 %fusion.23 = bf16[4,1024,1024]{2,1,0:T(8,128)(2,1)} fusion(f32[8,1024,1024]{2,1,0:T(8,128)} %fusion.161, bf16[4,1024,2048]{2,1,0:T(8,128)(2,1)} %bitcast.160, bf16[8,1024,2048]{2,1,0:T(8,128)(2,1)} %param.12), kind=kOutput, calls=%fused_computation.33 | convolution fusion | flops 17272143872 | bytes 58720256 | tf_op jit(solution)/shard_map/ech,efh->ecf/dot_general | solution.py:365
  950.9 24.8 %fusion.55 = bf16[4,1024,2048]{2,1,0:T(8,128)(2,1)} fusion(bf16[4,1024,1024]{2,1,0:T(8,128)(2,1)} %fusion.23, bf16[8,2048,1024]{2,1,0:T(8,128)(2,1)} %param.11), kind=kOutput, calls=%fused_computation.62 | convolution fusion | flops 17188257792 | bytes 41943040 | tf_op jit(solution)/shard_map/ecf,ehf->ech/dot_general | solution.py:367
  975.7 23.0 %shard_map.125 = bf16[8,512,16,128]{3,2,1,0:T(8,128)(2,1)} custom-call(s32[8192]{0:T(1024)S(1)} %bitcast.133, bf16[4,8,128,2048]{3,2,1,0:T(8,128)(2,1)} %bitcast.165, bf16[4,8,128,2048]{3,2,1,0:T(8,128)(2,1)} %bitcast.167), custom_call_target="tpu_custom_call" | custom-call | flops 15000000512 | bytes 35000000 | tf_op jit(solution)/shard_map/pallas_call | solution.py:170
  998.7 57.4 %all-to-all-done.4.refs_0_ = bf16[8,512,16,128]{3,2,1,0:T(8,128)(2,1)} async-done(((bf16[8,512,16,128]{3,2,1,0:T(8,128)(2,1)}), bf16[8,512,16,128]{3,2,1,0:T(8,128)(2,1)}, u32[]{:S(2)}, u32[]{:S(2)}) %all-to-all-start.4) | async-done | bytes 16777248 | tf_op jit(solution)/shard_map/all_to_all | solution.py:267
  1056.2 0.7 reshape.391
  1056.9 2.1 all-to-all-start.5
  1059.4 4.3 all-to-all-done.5
  1063.8 0.7 reduce.10
  1064.6 4.5 all-to-all-start.6
  1069.2 59.3 %fusion.13 = bf16[8,1024,2048]{2,1,0:T(8,128)(2,1)} fusion(bf16[4,1024,2048]{2,1,0:T(8,128)(2,1)} %bitcast.161, bf16[4,1024,2048]{2,1,0:T(8,128)(2,1)} %bitcast.159, f32[8,1024,1024]{2,1,0:T(8,128)} %fusion.161), kind=kOutput, calls=%fused_computation.25 | convolution fusion | flops 34468790272 | bytes 100663296 | tf_op jit(solution)/shard_map/ecf,ech->efh/dot_general | solution.py:384
  1128.5 0.6 multiply_reduce_fusion.2
  1130.4 0.8 fusion.88
  1131.2 0.8 fusion.87
  1133.1 8.8 convolution_bitcast_fusion
  1141.9 0.9 concatenate.25
  1142.9 43.9 %convolution_convert_fusion = bf16[8,2048,1024]{2,1,0:T(8,128)(2,1)} fusion(bf16[8,1024,2048]{2,1,0:T(8,128)(2,1)} %bitcast.163, bf16[4,1024,1024]{2,1,0:T(8,128)(2,1)} %fusion.23, bf16[4,1024,1024]{2,1,0:T(8,128)(2,1)} %fusion.18), kind=kOutput, calls=%fused_computation.23 | convolution fusion | flops 34384904192 | bytes 83886080 | tf_op jit(solution)/shard_map/ech,ecf->ehf/dot_general | solution.py:385
  1187.3 84.3 %all-reduce.2.cloned.1.call-done = f32[2050,64]{0,1:T(8,128)} async-done(((f32[2050,64]{0,1:T(8,128)}), f32[2050,64]{0,1:T(8,128)}) %all-reduce.2.cloned.1.call-update) | async-done | bytes 524816 | tf_op jit(solution)/shard_map/psum | solution.py:399
  1271.6 1.3 slice.70
  1273.5 0.9 slice_reduce_fusion
  1274.3 0.6 multiply_reduce_fusion.3
  1275.6 1.9 slice.72
  1277.5 36.8 %shard_map.126 = bf16[4096,2048]{1,0:T(8,128)(2,1)} custom-call(s32[8192]{0:T(1024)S(1)} %bitcast.131, bf16[8,512,16,128]{3,2,1,0:T(8,128)(2,1)} %all-to-all-done.4.refs_0_, bf16[8,512,16,128]{3,2,1,0:T(8,128)(2,1)} %all-to-all-done.6.refs_1_, bf16[4096,2048]{1,0:T(8,128)(2,1)} %bitcast.138, bf16[4096,64]{1,0:T(8,128)(2,1)S(1)} %bitcast.127, ...), custom_call_target="tpu_custom_call" | custom-call | flops 49999998976 | bytes 80000000 | tf_op jit(solution)/shard_map/pallas_call | solution.py:227
  (163 shorter events, 7.4 us)
Async XLA Ops:
  7.2 23.1 %copy-start.36 = (s32[2,2048]{1,0:T(2,128)S(1)}, s32[2,2048]{1,0:T(2,128)}, u32[]{:S(2)}) copy-start(s32[2,2048]{1,0:T(2,128)} %param.15) | copy-start | bytes 49156
  7.2 22.5 %copy-start.8 = (s32[2,2048]{1,0:T(2,128)S(1)}, s32[2,2048]{1,0:T(2,128)}, u32[]{:S(2)}) copy-start(s32[2,2048]{1,0:T(2,128)} %param.14) | copy-start | bytes 49156
  7.2 22.5 %copy-start.6 = (s32[2,2048]{1,0:T(2,128)S(1)}, s32[2,2048]{1,0:T(2,128)}, u32[]{:S(2)}) copy-start(s32[2,2048]{1,0:T(2,128)} %param.13) | copy-start | bytes 49156
  11.9 66.9 %copy-start.22 = (f32[2,2048]{1,0:T(2,128)}, f32[2,2048]{1,0:T(2,128)S(1)}, u32[]{:S(2)}) copy-start(f32[2,2048]{1,0:T(2,128)S(1)} %fusion.89) | copy-start | bytes 49156
  28.9 77.8 %copy-start.12 = (f32[2,2048]{1,0:T(2,128)}, f32[2,2048]{1,0:T(2,128)S(1)}, u32[]{:S(2)}) copy-start(f32[2,2048]{1,0:T(2,128)S(1)} %fusion.92) | copy-start | bytes 49156
  30.2 0.6 copy-start.20
  30.2 19.2 %copy-start.24 = (f32[2,2048]{1,0:T(2,128)}, f32[2,2048]{1,0:T(2,128)S(1)}, u32[]{:S(2)}) copy-start(f32[2,2048]{1,0:T(2,128)S(1)} %get-tuple-element.69) | copy-start | bytes 49156
  30.3 76.7 %copy-start.27 = (pred[2,2048]{1,0:T(4,128)(4,1)}, pred[2,2048]{1,0:T(4,128)(4,1)S(1)}, u32[]{:S(2)}) copy-start(pred[2,2048]{1,0:T(4,128)(4,1)S(1)} %get-tuple-element.73) | copy-start | bytes 12292
  72.2 370.2 %all-to-all-start = ((bf16[8,1024,16,128]{3,2,1,0:T(8,128)(2,1)}), bf16[8,1024,16,128]{3,2,1,0:T(8,128)(2,1)}, u32[]{:S(2)}, u32[]{:S(2)}) async-start(bf16[8,1024,16,128]{3,2,1,0:T(8,128)(2,1)} %shard_map.119), calls=%async_computation | async-start | bytes 67108864 | tf_op jit(solution)/shard_map/all_to_all | solution.py:267
  78.7 28.1 %copy-start.32 = (s32[2,2048]{1,0:T(2,128)}, s32[2,2048]{1,0:T(2,128)S(1)}, u32[]{:S(2)}) copy-start(s32[2,2048]{1,0:T(2,128)S(1)} %convert_element_type.231) | copy-start | bytes 49156
  78.7 28.3 %copy-start.34 = (s32[2,2048]{1,0:T(2,128)}, s32[2,2048]{1,0:T(2,128)S(1)}, u32[]{:S(2)}) copy-start(s32[2,2048]{1,0:T(2,128)S(1)} %convert_element_type.237) | copy-start | bytes 49156
  79.1 15.2 %copy-start.4 = (bf16[2048,64]{0,1:T(8,128)(2,1)S(1)}, bf16[2048,64]{0,1:T(8,128)(2,1)}, u32[]{:S(2)}) copy-start(bf16[2048,64]{0,1:T(8,128)(2,1)} %param.10) | copy-start | bytes 786436
  105.3 18.3 %copy-start.2 = (f32[2,2048,64]{1,2,0:T(8,128)}, f32[2,2048,64]{1,2,0:T(8,128)S(1)}, u32[]{:S(2)}) copy-start(f32[2,2048,64]{1,2,0:T(8,128)S(1)} %get-tuple-element.87) | copy-start | bytes 3145732
  105.3 18.3 %copy-start.14 = (f32[2,2048]{1,0:T(2,128)}, f32[2,2048]{1,0:T(2,128)S(1)}, u32[]{:S(2)}) copy-start(f32[2,2048]{1,0:T(2,128)S(1)} %get-tuple-element.86) | copy-start | bytes 49156
  106.7 16.9 %copy-start.16 = (f32[2,2048]{1,0:T(2,128)}, f32[2,2048]{1,0:T(2,128)S(1)}, u32[]{:S(2)}) copy-start(f32[2,2048]{1,0:T(2,128)S(1)} %get-tuple-element.62) | copy-start | bytes 49156
  106.7 16.9 %copy-start.18 = (f32[2,2048]{1,0:T(2,128)}, f32[2,2048]{1,0:T(2,128)S(1)}, u32[]{:S(2)}) copy-start(f32[2,2048]{1,0:T(2,128)S(1)} %get-tuple-element.63) | copy-start | bytes 49156
  106.7 0.7 copy-start.37
  443.2 44.6 %all-to-all-start.1 = ((f32[8,1,1024]{2,1,0:T(1,128)}), f32[8,1,1024]{2,1,0:T(1,128)S(1)}, u32[]{:S(2)}, u32[]{:S(2)}) async-start(f32[8,1,1024]{2,1,0:T(1,128)} %reshape.389), calls=%async_computation.1 | async-start | bytes 65536 | tf_op jit(solution)/shard_map/all_to_all | solution.py:348
  489.9 188.6 %all-to-all-start.2 = ((bf16[8,512,16,128]{3,2,1,0:T(8,128)(2,1)}), bf16[8,512,16,128]{3,2,1,0:T(8,128)(2,1)}, u32[]{:S(2)}, u32[]{:S(2)}) async-start(bf16[8,512,16,128]{3,2,1,0:T(8,128)(2,1)} %get-tuple-element.42), calls=%async_computation.2 | async-start | bytes 33554432 | tf_op jit(solution)/shard_map/all_to_all | solution.py:267
  678.5 4.8 copy-start.26
  678.5 4.9 copy-start.10
  678.5 188.8 %all-to-all-start.3 = ((bf16[8,512,16,128]{3,2,1,0:T(8,128)(2,1)}), bf16[8,512,16,128]{3,2,1,0:T(8,128)(2,1)}, u32[]{:S(2)}, u32[]{:S(2)}) async-start(bf16[8,512,16,128]{3,2,1,0:T(8,128)(2,1)} %get-tuple-element.49), calls=%async_computation.3 | async-start | bytes 33554432 | tf_op jit(solution)/shard_map/all_to_all | solution.py:267
  686.0 2.2 copy-start
  800.7 71.5 %copy-start.41 = (f32[64]{0:T(128)S(1)}, f32[64]{0:T(128)}, u32[]{:S(2)}) copy-start(f32[64]{0:T(128)} %broadcast_multiply_fusion.1) | copy-start | bytes 772
  800.7 72.0 %copy-start.13 = (f32[2,2048]{1,0:T(2,128)S(1)}, f32[2,2048]{1,0:T(2,128)}, u32[]{:S(2)}) copy-start(f32[2,2048]{1,0:T(2,128)} %copy-done.12) | copy-start | bytes 49156
  800.7 72.0 %copy-start.21 = (f32[2,2048]{1,0:T(2,128)S(1)}, f32[2,2048]{1,0:T(2,128)}, u32[]{:S(2)}) copy-start(f32[2,2048]{1,0:T(2,128)} %copy-done.20) | copy-start | bytes 49156
  800.7 72.0 %copy-start.31 = (f32[2,2048]{1,0:T(2,128)S(1)}, f32[2,2048]{1,0:T(2,128)}, u32[]{:S(2)}) copy-start(f32[2,2048]{1,0:T(2,128)} %get-tuple-element.66) | copy-start | bytes 49156
  800.7 72.0 %copy-start.23 = (f32[2,2048]{1,0:T(2,128)S(1)}, f32[2,2048]{1,0:T(2,128)}, u32[]{:S(2)}) copy-start(f32[2,2048]{1,0:T(2,128)} %copy-done.22) | copy-start | bytes 49156
  800.7 72.0 %copy-start.25 = (f32[2,2048]{1,0:T(2,128)S(1)}, f32[2,2048]{1,0:T(2,128)}, u32[]{:S(2)}) copy-start(f32[2,2048]{1,0:T(2,128)} %copy-done.24) | copy-start | bytes 49156
  800.7 72.0 %copy-start.28 = (pred[2,2048]{1,0:T(4,128)(4,1)S(1)}, pred[2,2048]{1,0:T(4,128)(4,1)}, u32[]{:S(2)}) copy-start(pred[2,2048]{1,0:T(4,128)(4,1)} %copy-done.27) | copy-start | bytes 12292
  800.8 72.0 %copy-start.30 = (f32[2,2048]{1,0:T(2,128)S(1)}, f32[2,2048]{1,0:T(2,128)}, u32[]{:S(2)}) copy-start(f32[2,2048]{1,0:T(2,128)} %get-tuple-element.67) | copy-start | bytes 49156
  867.2 188.9 %all-to-all-start.4 = ((bf16[8,512,16,128]{3,2,1,0:T(8,128)(2,1)}), bf16[8,512,16,128]{3,2,1,0:T(8,128)(2,1)}, u32[]{:S(2)}, u32[]{:S(2)}) async-start(bf16[8,512,16,128]{3,2,1,0:T(8,128)(2,1)} %shard_map.123), calls=%async_computation.4 | async-start | bytes 33554432 | tf_op jit(solution)/shard_map/all_to_all | solution.py:267
  873.4 2.2 copy-start.1
  975.7 83.4 %copy-start.5 = (bf16[2048,64]{0,1:T(8,128)(2,1)S(1)}, bf16[2048,64]{0,1:T(8,128)(2,1)}, u32[]{:S(2)}) copy-start(bf16[2048,64]{0,1:T(8,128)(2,1)} %param.10) | copy-start | bytes 786436
  975.7 83.7 %copy-start.39 = (f32[64]{0:T(128)S(1)}, f32[64]{0:T(128)}, u32[]{:S(2)}) copy-start(f32[64]{0:T(128)} %get-tuple-element.61) | copy-start | bytes 772
  1056.9 6.9 all-to-all-start.5
  1064.6 212.9 %all-to-all-start.6 = ((bf16[8,512,16,128]{3,2,1,0:T(8,128)(2,1)}), bf16[8,512,16,128]{3,2,1,0:T(8,128)(2,1)}, u32[]{:S(2)}, u32[]{:S(2)}) async-start(bf16[8,512,16,128]{3,2,1,0:T(8,128)(2,1)} %shard_map.125), calls=%async_computation.6 | async-start | bytes 33554432 | tf_op jit(solution)/shard_map/all_to_all | solution.py:267
  1069.1 59.5 %copy-start.11 = (f32[8,8,128]{2,1,0:T(8,128)S(1)}, f32[8,8,128]{2,1,0:T(8,128)}, u32[]{:S(2)}) copy-start(f32[8,8,128]{2,1,0:T(8,128)} %reshape.370) | copy-start | bytes 98308
  1069.1 61.3 %copy-start.9 = (s32[2,2048]{1,0:T(2,128)S(1)}, s32[2,2048]{1,0:T(2,128)}, u32[]{:S(2)}) copy-start(s32[2,2048]{1,0:T(2,128)} %param.14) | copy-start | bytes 49156
  1069.1 61.3 %copy-start.29 = (pred[2,2048]{1,0:T(4,128)(4,1)S(1)}, pred[2,2048]{1,0:T(4,128)(4,1)}, u32[]{:S(2)}) copy-start(pred[2,2048]{1,0:T(4,128)(4,1)} %copy-done.27) | copy-start | bytes 12292
  1069.1 61.3 %copy-start.35 = (s32[2,2048]{1,0:T(2,128)S(1)}, s32[2,2048]{1,0:T(2,128)}, u32[]{:S(2)}) copy-start(s32[2,2048]{1,0:T(2,128)} %copy-done.34) | copy-start | bytes 49156
  1069.1 62.1 %copy-start.7 = (s32[2,2048]{1,0:T(2,128)S(1)}, s32[2,2048]{1,0:T(2,128)}, u32[]{:S(2)}) copy-start(s32[2,2048]{1,0:T(2,128)} %param.13) | copy-start | bytes 49156
  1069.1 62.1 %copy-start.33 = (s32[2,2048]{1,0:T(2,128)S(1)}, s32[2,2048]{1,0:T(2,128)}, u32[]{:S(2)}) copy-start(s32[2,2048]{1,0:T(2,128)} %copy-done.32) | copy-start | bytes 49156
  1069.1 62.1 %copy-start.38 = (pred[2,2048]{1,0:T(4,128)(4,1)S(1)}, pred[2,2048]{1,0:T(4,128)(4,1)}, u32[]{:S(2)}) copy-start(pred[2,2048]{1,0:T(4,128)(4,1)} %copy-done.37) | copy-start | bytes 12292
  1069.1 62.9 %copy-start.17 = (f32[2,2048]{1,0:T(2,128)S(1)}, f32[2,2048]{1,0:T(2,128)}, u32[]{:S(2)}) copy-start(f32[2,2048]{1,0:T(2,128)} %copy-done.16) | copy-start | bytes 49156
  1069.1 62.9 %copy-start.19 = (f32[2,2048]{1,0:T(2,128)S(1)}, f32[2,2048]{1,0:T(2,128)}, u32[]{:S(2)}) copy-start(f32[2,2048]{1,0:T(2,128)} %copy-done.18) | copy-start | bytes 49156
  1069.2 63.0 %copy-start.3 = (f32[2,2048,64]{1,2,0:T(8,128)S(1)}, f32[2,2048,64]{1,2,0:T(8,128)}, u32[]{:S(2)}) copy-start(f32[2,2048,64]{1,2,0:T(8,128)} %copy-done.2) | copy-start | bytes 3145732
  1069.2 63.0 %copy-start.15 = (f32[2,2048]{1,0:T(2,128)S(1)}, f32[2,2048]{1,0:T(2,128)}, u32[]{:S(2)}) copy-start(f32[2,2048]{1,0:T(2,128)} %copy-done.14) | copy-start | bytes 49156
  1069.2 63.0 %copy-start.40 = (f32[64]{0:T(128)S(1)}, f32[64]{0:T(128)}, u32[]{:S(2)}) copy-start(f32[64]{0:T(128)} %broadcast_multiply_fusion) | copy-start | bytes 772
  1069.2 202.4 %all-reduce.2.cloned.1.call-start = ((), (), s32[]{:S(2)}) async-start(), calls=%async_computation.7 | async-start | bytes 1114112 | tf_op jit(solution)/shard_map/psum | solution.py:399
  1142.8 131.5 %copy-start.42 = (f32[64]{0:T(128)S(1)}, f32[64]{0:T(128)}, u32[]{:S(2)}) copy-start(f32[64]{0:T(128)} %broadcast_multiply_fusion.1) | copy-start | bytes 772
Sparse Core Ops, SparseCore 0:
  1143.0 128.5 all-reduce.1

commit v2 on v1

--- a/solution.py
+++ b/solution.py
@@ -12,6 +12,8 @@
 LANES = 128
 MIB = 1024 * 1024
 BATCH = 16
+BASE = 27
+MORE = 32
 bf16, f32 = jnp.bfloat16, jnp.float32
 
 
@@ -70,8 +72,8 @@
     slot = lax.rem(peer, 2)
 
     def copies(p, s):
-        return [pltpu.make_async_copy(part.at[p], packed.at[s, pl.ds(low, high - low)], sem.at[s, k])
-                for k, (part, (low, high)) in enumerate(zip(parts, ranges))]
+        return [pltpu.make_async_copy(part.at[p, pl.ds(at, high - low)], packed.at[s, pl.ds(low, high - low)], sem.at[s, k])
+                for k, (part, (low, high, at)) in enumerate(zip(parts, ranges))]
 
     @pl.when((peer == 0) & (local == 0))
     def _():
@@ -259,11 +261,12 @@
         block = groups * cap_rows
         rows = local_experts * block
         mid = rows // 2
+        base = rows * BASE // 32
+        over = rows - base
         sub = hidden // LANES
         tokens_loc = groups * seq_len
         tokens_all = tokens_loc * ep_size
         numel = tokens_all * hidden
-        me = lax.axis_index('ep')
         exchange = lambda v: lax.all_to_all(v, 'ep', 0, 0, tiled=True)
 
         expert_ids = jnp.arange(experts, dtype=jnp.int32)
@@ -306,29 +309,18 @@
 
         x_tiles = x_loc.reshape(tokens_loc, sub, LANES)
         r_tiles = r_loc.reshape(tokens_loc, sub, LANES)
-        x_ranges = ((0, rows),)
-        r_ranges = ((0, mid), (mid, rows))
-        x_send, = gather_rows(send_idx, x_tiles, x_ranges)
-
-        counts = lax.all_gather(jnp.stack([first_count, occupied]), 'ep')
-        frac_first = jnp.sum(counts[:, 0], axis=(0, 1)) / tokens_all
-        mine = lax.dynamic_slice_in_dim(counts[:, 1], me * local_experts, local_experts, axis=2)
-        mine = jnp.moveaxis(mine, 1, 2).reshape(ep_size, local_experts * groups)
-        mine_ends = jnp.cumsum(mine, axis=1)
-        mine_starts = mine_ends - mine
-        slot_ids = jnp.arange(cap_rows, dtype=f32)
-        recv_idx = jnp.where(slot_ids < mine[..., None], mine_starts[..., None] + slot_ids, float(rows)).astype(jnp.int32)
-        recv_idx = recv_idx.reshape(ep_size, local_experts, block)
-        packed = jnp.arange(rows, dtype=f32) - (rows - mine_ends[:, -1:])
-        passed = (mine_ends[:, None, :] <= packed[..., None]).astype(f32)
-        back_row = jnp.sum(passed, axis=-1) * cap_rows + packed - jnp.sum(passed * mine[:, None, :], axis=-1)
-        back_idx = jnp.where(packed >= 0, back_row, 0.0).astype(jnp.int32)
+        more = base + MORE
+        x_ranges = ((0, base), (base, more), (more, rows))
+        r_ranges = ((0, mid), (mid, base), (base, more), (more, rows))
+        g_ranges = ((0, over - MORE), (over - MORE, over), (over, mid), (mid, rows))
+        x_from = ((0, base, 0), (base, more, 0), (more, rows, 0))
+        r_from = ((0, mid, 0), (mid, base, 0), (base, more, MORE), (more, rows, over - MORE))
+        x_send, x_more, x_rest = gather_rows(send_idx, x_tiles, x_ranges)
 
         tie = lambda *values: lax.optimization_barrier(values)
-        x_send, recv_idx, back_idx, frac_first = tie(x_send, recv_idx, back_idx, frac_first)
         x_recv = exchange(x_send)
         x_here, r_here, r_tiles, _ = tie(x_loc, r_loc, r_tiles, x_send)
-        r_send_0, r_send_1 = gather_rows(send_idx, r_tiles, r_ranges)
+        r_send_0, r_send_1, r_more, r_rest = gather_rows(send_idx, r_tiles, r_ranges)
 
         logits = jnp.einsum('gsh,he->gse', x_here, w_gate, preferred_element_type=f32)
         router_prob = jax.nn.softmax(logits, axis=-1)
@@ -344,12 +336,37 @@
         norm_at = jnp.concatenate([at_first * norm_first[..., None], at_second * norm_second[..., None]], axis=1)
         slot_norm = jnp.einsum('gse,gsk->egk', hots, norm_at, preferred_element_type=f32)
         dot_xr = jnp.sum(x_here.astype(f32) * r_here.astype(f32))
-        slot_norm, x_recv = tie(slot_norm, x_recv)
-        expert_norm = lax.all_to_all(slot_norm, 'ep', 0, 1, tiled=True).reshape(local_experts, ep_size, block)
-
-        r_send_0, expert_norm, dot_xr = tie(r_send_0, expert_norm, dot_xr)
+        to_rows = lambda v: jnp.moveaxis(v, 0, 1)[..., None]
+        fullest = jnp.broadcast_to(jnp.max(jnp.sum(held, axis=1)), (experts, groups, 1))
+        tally = jnp.moveaxis(first_count.reshape(groups, local_experts, ep_size), 0, 1)
+        tally = jnp.tile(tally, (ep_size, 1, 1))
+        sheet = jnp.concatenate([slot_norm, to_rows(occupied), fullest, tally], axis=-1)
+        sheet, x_recv = tie(sheet, x_recv)
+        sheet = lax.all_to_all(sheet, 'ep', 0, 1, tiled=True).reshape(local_experts, ep_size, groups, -1)
+        expert_norm = sheet[..., :cap_rows].reshape(local_experts, ep_size, block)
+        mine = jnp.moveaxis(sheet[..., cap_rows], 0, 1).reshape(ep_size, local_experts * groups)
+        excess = jnp.max(sheet[0, :, 0, cap_rows + 1]) - base
+        level = jnp.where(excess <= 0, 0, jnp.where(excess <= MORE, 1, 2)).astype(jnp.int32)
+        frac_first = jnp.sum(sheet[..., cap_rows + 2:], axis=(1, 2)).reshape(experts) / tokens_all
+        mine_ends = jnp.cumsum(mine, axis=1)
+        mine_starts = mine_ends - mine
+        slot_ids = jnp.arange(cap_rows, dtype=f32)
+        recv_idx = jnp.where(slot_ids < mine[..., None], mine_starts[..., None] + slot_ids, float(rows)).astype(jnp.int32)
+        recv_idx = recv_idx.reshape(ep_size, local_experts, block)
+        packed = jnp.arange(rows, dtype=f32) - (rows - mine_ends[:, -1:])
+        passed = (mine_ends[:, None, :] <= packed[..., None]).astype(f32)
+        back_row = jnp.sum(passed, axis=-1) * cap_rows + packed - jnp.sum(passed * mine[:, None, :], axis=-1)
+        back_idx = jnp.where(packed >= 0, back_row, 0.0).astype(jnp.int32)
+
+        def exchange_over(few, rest):
+            return lax.switch(level, (lambda u, v: (u, v), lambda u, v: (exchange(u), v), lambda u, v: (exchange(u), exchange(v))), few, rest)
+
+        xr_more, xr_rest = jnp.concatenate([x_more, r_more], axis=1), jnp.concatenate([x_rest, r_rest], axis=1)
+        xr_more, xr_rest, expert_norm = tie(xr_more, xr_rest, expert_norm)
+        xr_more, xr_rest = exchange_over(xr_more, xr_rest)
+        r_send_0, xr_more, xr_rest, dot_xr = tie(r_send_0, xr_more, xr_rest, dot_xr)
         r_recv_0 = exchange(r_send_0)
-        expert_x = unpack_rows(recv_idx, [x_recv], x_ranges, rows).reshape(local_experts, -1, hidden)
+        expert_x = unpack_rows(recv_idx, [x_recv, xr_more, xr_rest], x_from, rows).reshape(local_experts, -1, hidden)
         pre_act = jnp.einsum('ech,ehf->ecf', expert_x, w_in_loc, preferred_element_type=f32)
         act_bf = gelu_bf16(pre_act)
         expert_y = jnp.einsum('ecf,efh->ech', act_bf, w_out_loc, preferred_element_type=f32).astype(bf16)
@@ -367,12 +384,14 @@
             grad_slots = jnp.einsum('ecf,ehf->ech', grad_pre, w_in_loc[chunk], preferred_element_type=f32).astype(bf16)
             return grad_y, grad_pre, slot_dot, grad_slots.reshape(half, ep_size, block, hidden)
 
-        grad_y_0, grad_pre_0, slot_dot_0, grad_slots_0 = expert_bwd([r_recv_0], r_ranges[:1], 0)
-        g_send_0, = pack_rows(back_idx, [grad_slots_0], ((0, mid),))
-        g_send_0, r_recv_1 = tie(g_send_0, r_recv_1)
+        grad_y_0, grad_pre_0, slot_dot_0, grad_slots_0 = expert_bwd([r_recv_0], r_from[:1], 0)
+        g_rest, g_more, g_send_0 = pack_rows(back_idx, [grad_slots_0], g_ranges[:3])
+        g_more, g_rest, r_recv_1 = tie(g_more, g_rest, r_recv_1)
+        g_more, g_rest = exchange_over(g_more, g_rest)
+        g_send_0, g_more, g_rest, r_recv_1 = tie(g_send_0, g_more, g_rest, r_recv_1)
         g_recv_0 = exchange(g_send_0)
-        grad_y_1, grad_pre_1, slot_dot_1, grad_slots_1 = expert_bwd([r_recv_0, r_recv_1], r_ranges, 1)
-        g_send_1, = pack_rows(back_idx, [grad_slots_0, grad_slots_1], ((mid, rows),))
+        grad_y_1, grad_pre_1, slot_dot_1, grad_slots_1 = expert_bwd([r_recv_0, r_recv_1, xr_more, xr_rest], r_from, 1)
+        g_send_1, = pack_rows(back_idx, [grad_slots_0, grad_slots_1], g_ranges[3:])
         slot_dot = jnp.concatenate([slot_dot_0, slot_dot_1], axis=0)
         slot_dot, g_send_1, g_recv_0 = tie(slot_dot, g_send_1, g_recv_0)
         home_dot = lax.all_to_all(slot_dot.reshape(local_experts, ep_size * groups, cap_rows), 'ep', 1, 0, tiled=True)
@@ -400,7 +419,7 @@
         grad_gate_w, prob_sum, dot_sum = summed[:hidden], summed[hidden], summed[hidden + 1, 0]
         loss_value = dot_sum / numel + ALPHA * experts * jnp.sum(frac_first * prob_sum / tokens_all)
 
-        grad_x = combine_rows(slots_of, [g_recv_0, g_recv_1], ((0, mid), (mid, rows)), r_loc.reshape(-1, hidden), grad_logits_bf.reshape(-1, experts), w_gate)
+        grad_x = combine_rows(slots_of, [g_rest, g_more, g_recv_0, g_recv_1], g_ranges, r_loc.reshape(-1, hidden), grad_logits_bf.reshape(-1, experts), w_gate)
         return loss_value, grad_x.reshape(x_loc.shape), grad_w_in, grad_w_out, grad_gate_w
 
     row_spec = P('ep', None, None)

time: 1330 us -> 1150 us (0.86)
  waiting for transfers between devices: 597 us -> 378 us
  blocking collectives: 13.6 us -> 44.3 us
    all_to_all x5, waiting for transfers between devices: 508 us -> 286 us  [layer_body(): exchange = lambda v: lax.all_to_all(v, 'ep', 0, 0, tiled=True)]
    all_to_all x0 -> x2, blocking collectives: none -> 44.3 us  [layer_body(): exchange = lambda v: lax.all_to_all(v, 'ep', 0, 0, tiled=True)]
    all_gather x1 -> x0, blocking collectives: 13.6 us -> none  [layer_body(): counts = lax.all_gather(jnp.stack([first_count, occupied]), 'ep')]
    unnamed x96 -> x77, local copies, waits for them, and re-layouts: 37.2 us -> 41.2 us
  transfers between devices with their start and end apart: 8 -> 8, of which waited for: 6 -> 7; matrix products, arithmetic and copies ran while one was open for 29% -> 35% of each run, Pallas kernels for 14% -> 16%
where the time goes in v2:
time: 1150 us; the launch traced here: 1140 us
  waiting for transfers between devices  378 us (33%)
  matrix products  346 us (30%)
  Pallas kernels  236 us (21%)
  local copies, waits for them, and re-layouts  55.4 us (5%)
  blocking collectives  44.3 us (4%)
  other arithmetic  36.4 us (3%)
  starting transfers between devices  27.3 us (2%)
  between operations  19.7 us (2%)
    all_to_all x5, waiting for transfers between devices, layer_body(): exchange = lambda v: lax.all_to_all(v, 'ep', 0, 0, tiled=True)  286 us
    pallas_call x3, Pallas kernels, unpack_rows(): pl.pallas_call(functools.partial(unpack_kernel, ranges=ranges, scaled=sca...  118 us
    psum x1, waiting for transfers between devices, layer_body(): summed = lax.psum(jnp.concatenate([grad_gate_w, stats], axis=0), 'ep')  84.2 us
    dot_general x2, matrix products, expert_bwd(): jnp.einsum('ech,efh->ecf', grad_y, w_out_loc[chunk], preferred_element_ty...  68.4 us
    dot_general x1, matrix products, layer_body(): jnp.einsum('ecf,ech->efh', act_bf, grad_y, preferred_element_type=f32)  59.3 us
    dot_general x1, matrix products, layer_body(): jnp.einsum('ecf,efh->ech', act_bf, w_out_loc, preferred_element_type=f32)  51.7 us
    dot_general x2, matrix products, expert_bwd(): jnp.einsum('ecf,ehf->ech', grad_pre, w_in_loc[chunk], preferred_element_t...  49.6 us
    dot_general x1, matrix products, layer_body(): jnp.einsum('ech,ehf->ecf', expert_x, w_in_loc, preferred_element_type=f32)  44.5 us
  transfers between devices with their start and end apart: 8, of which 7 were waited for; matrix products, arithmetic and copies ran while one was open for 35% of the time, Pallas kernels for 16%

profile of v2, /device:TPU:0, one launch (start us, length us, event | category | flops | bytes accessed | tf_op | source)
XLA Modules:
  0.0 1144.1 jit_solution(13772327676716943602)
XLA Ops:
  7.2 0.8 convert_element_type.239
  8.0 1.1 convert_reduce_fusion
  9.0 2.8 fusion.89
  11.9 2.8 fusion.92
  16.7 1.4 fusion.62
  18.3 15.2 %copy.227 = bf16[512,8,16,128]{3,2,1,0:T(8,128)(2,1)} copy(bf16[512,8,16,128]{3,1,2,0:T(8,128)(2,1)} %bitcast.135) | data formatting | bytes 33554432
  33.4 21.5 %shard_map.119 = (bf16[8,864,16,128]{3,2,1,0:T(8,128)(2,1)}, bf16[8,32,16,128]{3,2,1,0:T(8,128)(2,1)S(1)}, bf16[8,128,16,128]{3,2,1,0:T(8,128)(2,1)}) custom-call(s32[8192]{0:T(1024)S(1)} %reshape_reshape.2.idx_ref, bf16[4096,16,128]{2,1,0:T(8,128)(2,1)} %bitcast.141), custom_call_target="tpu_custom_call" | custom-call | flops 30000001024 | bytes 60000000 | tf_op jit(solution)/shard_map/pallas_call | solution.py:50
  54.9 5.6 all-to-all-start.6
  61.7 15.2 %copy.225 = bf16[512,8,16,128]{3,2,1,0:T(8,128)(2,1)} copy(bf16[512,8,16,128]{3,1,2,0:T(8,128)(2,1)} %bitcast.138) | data formatting | bytes 33554432
  76.9 0.7 pad.14.clone
  77.6 11.0 fusion.159
  88.6 0.8 fusion.154
  91.1 21.7 %shard_map.120 = (bf16[8,512,16,128]{3,2,1,0:T(8,128)(2,1)}, bf16[8,352,16,128]{3,2,1,0:T(8,128)(2,1)}, bf16[8,32,16,128]{3,2,1,0:T(8,128)(2,1)S(1)}, bf16[8,128,16,128]{3,2,1,0:T(8,128)(2,1)}) custom-call(s32[8192]{0:T(1024)S(1)} %reshape_reshape.2.idx_ref, bf16[4096,16,128]{2,1,0:T(8,128)(2,1)} %bitcast.140), custom_call_target="tpu_custom_call" | custom-call | flops 30000001024 | bytes 60000000 | tf_op jit(solution)/shard_map/pallas_call | solution.py:50
  112.7 1.5 pad_maximum_fusion.1
  114.4 7.5 pad_maximum_fusion
  121.9 15.9 %multiply_reduce_fusion = f32[]{:T(128)} fusion(bf16[2,2048,2048]{2,1,0:T(8,128)(2,1)} %param.15, bf16[2,2048,2048]{2,1,0:T(8,128)(2,1)} %param.14), kind=kLoop, calls=%fused_computation.14 | loop fusion | flops 33554432 | bytes 33554436 | tf_op jit(solution)/shard_map/reduce_sum | solution.py:338
  137.8 231.2 %all-to-all-done.6.refs_0_ = bf16[8,864,16,128]{3,2,1,0:T(8,128)(2,1)} async-done(((bf16[8,864,16,128]{3,2,1,0:T(8,128)(2,1)}), bf16[8,864,16,128]{3,2,1,0:T(8,128)(2,1)}, u32[]{:S(2)}, u32[]{:S(2)}) %all-to-all-start.6) | async-done | bytes 28311584 | tf_op jit(solution)/shard_map/all_to_all | solution.py:270
  369.1 0.7 copy.197
  369.8 2.1 all-to-all-start.7
  372.2 0.7 copy.214
  372.9 3.9 all-to-all-done.7
  376.8 0.7 slice_reduce_fusion.2
  379.0 28.2 %conditional.2 = ((bf16[8,64,16,128]{3,2,1,0:T(8,128)(2,1)S(1)}, bf16[8,256,16,128]{3,2,1,0:T(8,128)(2,1)})) conditional(s32[]{:T(128)} %clamp.4, (bf16[8,64,16,128]{3,2,1,0:T(8,128)(2,1)S(1)}, bf16[8,256,16,128]{3,2,1,0:T(8,128)(2,1)}) %tuple.84, (bf16[8,64,16,128]{3,2,1,0:T(8,128)(2,1)S(1)}, ...), branch_computations={%region_16.17_spmd, %region_17.18_spmd, %region_18.19_spmd} | conditional | bytes 41943064 | solution.py:362
  379.4 27.8 %all_to_all.82 = bf16[8,64,16,128]{3,2,1,0:T(8,128)(2,1)S(1)} all-to-all(bf16[8,64,16,128]{3,2,1,0:T(8,128)(2,1)S(1)} %copy.251), channel_id=1, replica_groups=mesh['ep'=8] {'ep'}, dimensions={0} | all-to-all | bytes 4194304 | tf_op jit(solution)/shard_map/cond/branch_1_fun/all_to_all | solution.py:270
  407.2 4.7 all-to-all-start.8
  411.9 43.4 %shard_map.121 = bf16[8,8,128,2048]{3,2,1,0:T(8,128)(2,1)} custom-call(s32[8192]{0:T(1024)S(1)} %convert_element_type.253.idx_ref, bf16[8,864,16,128]{3,2,1,0:T(8,128)(2,1)} %all-to-all-done.6.refs_0_, bf16[8,64,16,128]{3,2,1,0:T(8,128)(2,1)S(1)} %get-tuple-element.98.refs_1_.refs_2_, bf16[8,256,16,128]{3,2,1,0:T(8,128)(2,1)} %get-tuple-element.99.refs_2_.refs_3_), custom_call_target="tpu_custom_call" | custom-call | flops 28000000000 | bytes 64000000 | tf_op jit(solution)/shard_map/pallas_call | solution.py:128
  455.3 44.5 %fusion.162 = f32[8,1024,1024]{2,1,0:T(8,128)} fusion(bf16[8,1024,2048]{2,1,0:T(8,128)(2,1)} %bitcast.163, bf16[8,2048,1024]{2,1,0:T(8,128)(2,1)} %param.17), kind=kOutput, calls=%fused_computation.225 | convolution fusion | flops 34359738368 | bytes 100663296 | tf_op jit(solution)/shard_map/ech,ehf->ecf/dot_general | solution.py:370
  501.5 2.7 copy.205.refs_1_.refs_4_
  504.2 51.7 %convolution_convert_fusion.1 = bf16[8,1024,2048]{2,1,0:T(8,128)(2,1)} fusion(bf16[8,1024,2048]{2,1,0:T(8,128)(2,1)} %param.18, f32[8,1024,1024]{2,1,0:T(8,128)} %fusion.162), kind=kOutput, calls=%fused_computation.24 | convolution fusion | flops 34452013056 | bytes 100663296 | tf_op jit(solution)/shard_map/ecf,efh->ech/dot_general | solution.py:372
  555.9 39.9 %all-to-all-done.8.refs_0_ = bf16[8,512,16,128]{3,2,1,0:T(8,128)(2,1)} async-done(((bf16[8,512,16,128]{3,2,1,0:T(8,128)(2,1)}), bf16[8,512,16,128]{3,2,1,0:T(8,128)(2,1)}, u32[]{:S(2)}, u32[]{:S(2)}) %all-to-all-start.8) | async-done | bytes 16777248 | tf_op jit(solution)/shard_map/all_to_all | solution.py:270
  595.8 4.4 all-to-all-start.9
  600.2 2.2 copy-done
  602.4 34.8 %shard_map.122 = (bf16[4,8,128,2048]{3,2,1,0:T(8,128)(2,1)}, f32[4,8,128,128]{3,2,1,0:T(8,128)S(1)}) custom-call(s32[4096]{0:T(1024)S(1)} %bitcast.130, bf16[8,512,16,128]{3,2,1,0:T(8,128)(2,1)} %all-to-all-done.8.refs_0_, f32[8,8,128,1]{3,2,1,0:T(8,128)S(1)} %copy-done, bf16[8,8,128,2048]{3,2,1,0:T(8,128)(2,1)} %bitcast.136), custom_call_target="tpu_custom_call" | custom-call | flops 14000000000 | bytes 32000000 | tf_op jit(solution)/shard_map/pallas_call | solution.py:128
  637.8 34.2 %fusion.18 = bf16[4,1024,1024]{2,1,0:T(8,128)(2,1)} fusion(f32[8,1024,1024]{2,1,0:T(8,128)} %fusion.162, bf16[4,1024,2048]{2,1,0:T(8,128)(2,1)} %bitcast.159, bf16[8,1024,2048]{2,1,0:T(8,128)(2,1)} %param.18), kind=kOutput, calls=%fused_computation.28 | convolution fusion | flops 17272143872 | bytes 58720256 | tf_op jit(solution)/shard_map/ech,efh->ecf/dot_general | solution.py:382
  672.0 24.8 %fusion.52 = bf16[4,1024,2048]{2,1,0:T(8,128)(2,1)} fusion(bf16[4,1024,1024]{2,1,0:T(8,128)(2,1)} %fusion.18, bf16[8,2048,1024]{2,1,0:T(8,128)(2,1)} %param.17), kind=kOutput, calls=%fused_computation.61 | convolution fusion | flops 17188257792 | bytes 41943040 | tf_op jit(solution)/shard_map/ecf,ehf->ech/dot_general | solution.py:384
  696.8 14.5 %shard_map.123 = (bf16[8,128,16,128]{3,2,1,0:T(8,128)(2,1)}, bf16[8,32,16,128]{3,2,1,0:T(8,128)(2,1)S(1)}, bf16[8,352,16,128]{3,2,1,0:T(8,128)(2,1)S(1)}) custom-call(s32[8192]{0:T(1024)S(1)} %bitcast.133, bf16[4,8,128,2048]{3,2,1,0:T(8,128)(2,1)} %bitcast.165), custom_call_target="tpu_custom_call" | custom-call | flops 15000000512 | bytes 35000000 | tf_op jit(solution)/shard_map/pallas_call | solution.py:172
  711.3 4.1 copy-done.2
  715.5 12.5 %all-to-all-done.9.refs_1_ = bf16[8,352,16,128]{3,2,1,0:T(8,128)(2,1)} async-done(((bf16[8,352,16,128]{3,2,1,0:T(8,128)(2,1)}), bf16[8,352,16,128]{3,2,1,0:T(8,128)(2,1)}, u32[]{:S(2)}, u32[]{:S(2)}) %all-to-all-start.9) | async-done | bytes 11534368 | tf_op jit(solution)/shard_map/all_to_all | solution.py:270
  727.9 16.9 %conditional.3 = ((bf16[8,32,16,128]{3,2,1,0:T(8,128)(2,1)S(1)}, bf16[8,128,16,128]{3,2,1,0:T(8,128)(2,1)})) conditional(s32[]{:T(128)} %clamp.4, (bf16[8,32,16,128]{3,2,1,0:T(8,128)(2,1)S(1)}, bf16[8,128,16,128]{3,2,1,0:T(8,128)(2,1)}) %tuple.46, (bf16[8,32,16,128]{3,2,1,0:T(8,128)(2,1)S(1)}, ...), branch_computations={%region_23.24_spmd, %region_24.25_spmd, %region_25.26_spmd} | conditional | bytes 20971544 | solution.py:362
  728.1 16.5 %all_to_all.84 = bf16[8,32,16,128]{3,2,1,0:T(8,128)(2,1)S(1)} all-to-all(bf16[8,32,16,128]{3,2,1,0:T(8,128)(2,1)S(1)} %copy.253), channel_id=1, replica_groups=mesh['ep'=8] {'ep'}, dimensions={0} | all-to-all | bytes 2097152 | tf_op jit(solution)/shard_map/cond/branch_1_fun/all_to_all | solution.py:270
  744.8 4.0 all-to-all-start.10
  748.9 2.2 copy-done.1
  751.0 40.1 %shard_map.124 = (bf16[4,8,128,2048]{3,2,1,0:T(8,128)(2,1)}, f32[4,8,128,128]{3,2,1,0:T(8,128)S(1)}) custom-call(s32[4096]{0:T(1024)S(1)} %bitcast.131, bf16[8,512,16,128]{3,2,1,0:T(8,128)(2,1)} %all-to-all-done.8.refs_0_, bf16[8,352,16,128]{3,2,1,0:T(8,128)(2,1)} %all-to-all-done.9.refs_1_, bf16[8,64,16,128]{3,2,1,0:T(8,128)(2,1)} %copy-done.4, ...), custom_call_target="tpu_custom_call" | custom-call | flops 14000000000 | bytes 32000000 | tf_op jit(solution)/shard_map/pallas_call | solution.py:128
  791.7 34.2 %fusion.23 = bf16[4,1024,1024]{2,1,0:T(8,128)(2,1)} fusion(f32[8,1024,1024]{2,1,0:T(8,128)} %fusion.162, bf16[4,1024,2048]{2,1,0:T(8,128)(2,1)} %bitcast.161, bf16[8,1024,2048]{2,1,0:T(8,128)(2,1)} %param.18), kind=kOutput, calls=%fused_computation.33 | convolution fusion | flops 17272143872 | bytes 58720256 | tf_op jit(solution)/shard_map/ech,efh->ecf/dot_general | solution.py:382
  826.0 24.8 %fusion.55 = bf16[4,1024,2048]{2,1,0:T(8,128)(2,1)} fusion(bf16[4,1024,1024]{2,1,0:T(8,128)(2,1)} %fusion.23, bf16[8,2048,1024]{2,1,0:T(8,128)(2,1)} %param.17), kind=kOutput, calls=%fused_computation.62 | convolution fusion | flops 17188257792 | bytes 41943040 | tf_op jit(solution)/shard_map/ecf,ehf->ech/dot_general | solution.py:384
  850.8 23.1 %shard_map.125 = bf16[8,512,16,128]{3,2,1,0:T(8,128)(2,1)} custom-call(s32[8192]{0:T(1024)S(1)} %bitcast.134, bf16[4,8,128,2048]{3,2,1,0:T(8,128)(2,1)} %bitcast.166, bf16[4,8,128,2048]{3,2,1,0:T(8,128)(2,1)} %bitcast.168), custom_call_target="tpu_custom_call" | custom-call | flops 15000000512 | bytes 35000000 | tf_op jit(solution)/shard_map/pallas_call | solution.py:172
  873.8 2.8 all-to-all-done.10.refs_2_
  876.7 0.7 reshape.402
  877.4 2.1 all-to-all-start.11
  879.6 0.7 div.85
  880.4 3.9 all-to-all-done.11
  884.8 0.7 reduce.9
  885.6 4.5 all-to-all-start.12
  890.2 59.3 %fusion.13 = bf16[8,1024,2048]{2,1,0:T(8,128)(2,1)} fusion(bf16[4,1024,2048]{2,1,0:T(8,128)(2,1)} %bitcast.162, bf16[4,1024,2048]{2,1,0:T(8,128)(2,1)} %bitcast.160, f32[8,1024,1024]{2,1,0:T(8,128)} %fusion.162), kind=kOutput, calls=%fused_computation.25 | convolution fusion | flops 34468790272 | bytes 100663296 | tf_op jit(solution)/shard_map/ecf,ech->efh/dot_general | solution.py:403
  951.5 0.8 fusion.88
  952.3 0.8 fusion.87
  954.2 8.8 convolution_bitcast_fusion
  963.0 0.9 concatenate.37
  963.9 44.0 %convolution_convert_fusion = bf16[8,2048,1024]{2,1,0:T(8,128)(2,1)} fusion(bf16[8,1024,2048]{2,1,0:T(8,128)(2,1)} %bitcast.164, bf16[4,1024,1024]{2,1,0:T(8,128)(2,1)} %fusion.23, bf16[4,1024,1024]{2,1,0:T(8,128)(2,1)} %fusion.18), kind=kOutput, calls=%fused_computation.23 | convolution fusion | flops 34384904192 | bytes 83886080 | tf_op jit(solution)/shard_map/ech,ecf->ehf/dot_general | solution.py:404
  1008.4 84.2 %all-reduce.2.cloned.1.call-done = f32[2050,64]{0,1:T(8,128)} async-done(((f32[2050,64]{0,1:T(8,128)}), f32[2050,64]{0,1:T(8,128)}) %all-reduce.2.cloned.1.call-update) | async-done | bytes 524816 | tf_op jit(solution)/shard_map/psum | solution.py:418
  1092.6 1.3 slice.82
  1094.5 0.9 slice_reduce_fusion.1
  1096.6 1.9 slice.84
  1098.5 37.2 %shard_map.126 = bf16[4096,2048]{1,0:T(8,128)(2,1)} custom-call(s32[8192]{0:T(1024)S(1)} %bitcast.132, bf16[8,128,16,128]{3,2,1,0:T(8,128)(2,1)} %get-tuple-element.123.refs_0_, bf16[8,32,16,128]{3,2,1,0:T(8,128)(2,1)S(1)} %copy-done.8, bf16[8,352,16,128]{3,2,1,0:T(8,128)(2,1)} %all-to-all-done.10.refs_2_, ...), custom_call_target="tpu_custom_call" | custom-call | flops 49999998976 | bytes 80000000 | tf_op jit(solution)/shard_map/pallas_call | solution.py:229
  (160 shorter events, 13.5 us)
Async XLA Ops:
  7.2 8.8 copy-start.29
  7.2 8.2 copy-start.12
  7.2 8.2 copy-start.10
  16.0 98.3 %copy-start.23 = (pred[2,2048]{1,0:T(4,128)(4,1)}, pred[2,2048]{1,0:T(4,128)(4,1)S(1)}, u32[]{:S(2)}) copy-start(pred[2,2048]{1,0:T(4,128)(4,1)S(1)} %get-tuple-element.137) | copy-start | bytes 12292
  54.9 314.1 %all-to-all-start.6 = ((bf16[8,864,16,128]{3,2,1,0:T(8,128)(2,1)}), bf16[8,864,16,128]{3,2,1,0:T(8,128)(2,1)}, u32[]{:S(2)}, u32[]{:S(2)}) async-start(bf16[8,864,16,128]{3,2,1,0:T(8,128)(2,1)} %get-tuple-element.82), calls=%async_computation.6 | async-start | bytes 56623104 | tf_op jit(solution)/shard_map/all_to_all | solution.py:270
  60.5 29.4 %copy-start.25 = (s32[2,2048]{1,0:T(2,128)}, s32[2,2048]{1,0:T(2,128)S(1)}, u32[]{:S(2)}) copy-start(s32[2,2048]{1,0:T(2,128)S(1)} %convert_element_type.238) | copy-start | bytes 49156
  60.6 29.6 %copy-start.27 = (s32[2,2048]{1,0:T(2,128)}, s32[2,2048]{1,0:T(2,128)S(1)}, u32[]{:S(2)}) copy-start(s32[2,2048]{1,0:T(2,128)S(1)} %convert_element_type.244) | copy-start | bytes 49156
  61.7 15.9 %copy-start.9 = (bf16[2048,64]{0,1:T(8,128)(2,1)S(1)}, bf16[2048,64]{0,1:T(8,128)(2,1)}, u32[]{:S(2)}) copy-start(bf16[2048,64]{0,1:T(8,128)(2,1)} %param.16) | copy-start | bytes 786436
  88.6 0.9 copy-start.16
  88.6 24.1 %copy-start.5 = (f32[2,2048,64]{1,2,0:T(8,128)}, f32[2,2048,64]{1,2,0:T(8,128)S(1)}, u32[]{:S(2)}) copy-start(f32[2,2048,64]{1,2,0:T(8,128)S(1)} %get-tuple-element.155) | copy-start | bytes 3145732
  89.4 0.6 copy-start.18
  89.4 0.6 copy-start.20
  89.4 1.2 copy-start.30
  121.9 257.1 %copy-start.3 = (bf16[8,64,16,128]{3,2,1,0:T(8,128)(2,1)S(1)}, bf16[8,64,16,128]{3,2,1,0:T(8,128)(2,1)}, u32[]{:S(2)}) copy-start(bf16[8,64,16,128]{3,2,1,0:T(8,128)(2,1)} %pad_maximum_fusion.1) | copy-start | bytes 6291460
  369.8 7.0 all-to-all-start.7
  378.4 123.1 %copy-start.14 = (f32[8,8,128]{2,1,0:T(8,128)}, f32[8,8,128]{2,1,0:T(8,128)S(1)}, u32[]{:S(2)}) copy-start(f32[8,8,128]{2,1,0:T(8,128)S(1)} %reshape.382) | copy-start | bytes 98308
  407.2 4.7 copy-start.4
  407.2 188.6 %all-to-all-start.8 = ((bf16[8,512,16,128]{3,2,1,0:T(8,128)(2,1)}), bf16[8,512,16,128]{3,2,1,0:T(8,128)(2,1)}, u32[]{:S(2)}, u32[]{:S(2)}) async-start(bf16[8,512,16,128]{3,2,1,0:T(8,128)(2,1)} %get-tuple-element.100), calls=%async_computation.8 | async-start | bytes 33554432 | tf_op jit(solution)/shard_map/all_to_all | solution.py:270
  595.8 132.2 %all-to-all-start.9 = ((bf16[8,352,16,128]{3,2,1,0:T(8,128)(2,1)}), bf16[8,352,16,128]{3,2,1,0:T(8,128)(2,1)}, u32[]{:S(2)}, u32[]{:S(2)}) async-start(bf16[8,352,16,128]{3,2,1,0:T(8,128)(2,1)} %get-tuple-element.109), calls=%async_computation.9 | async-start | bytes 23068672 | tf_op jit(solution)/shard_map/all_to_all | solution.py:270
  600.2 2.2 copy-start
  711.3 4.1 copy-start.2
  744.8 4.0 copy-start.7
  744.8 131.8 %all-to-all-start.10 = ((bf16[8,352,16,128]{3,2,1,0:T(8,128)(2,1)}), bf16[8,352,16,128]{3,2,1,0:T(8,128)(2,1)}, u32[]{:S(2)}, u32[]{:S(2)}) async-start(bf16[8,352,16,128]{3,2,1,0:T(8,128)(2,1)} %copy-done.2), calls=%async_computation.10 | async-start | bytes 23068672 | tf_op jit(solution)/shard_map/all_to_all | solution.py:270
  748.9 2.2 copy-start.1
  850.7 28.7 %copy-start.32 = (f32[8,8]{0,1:T(8,128)S(1)}, f32[8,8]{0,1:T(8,128)}, u32[]{:S(2)}) copy-start(f32[8,8]{0,1:T(8,128)} %copy.224) | copy-start | bytes 772
  877.4 6.9 all-to-all-start.11
  885.6 212.9 %all-to-all-start.12 = ((bf16[8,512,16,128]{3,2,1,0:T(8,128)(2,1)}), bf16[8,512,16,128]{3,2,1,0:T(8,128)(2,1)}, u32[]{:S(2)}, u32[]{:S(2)}) async-start(bf16[8,512,16,128]{3,2,1,0:T(8,128)(2,1)} %shard_map.125), calls=%async_computation.12 | async-start | bytes 33554432 | tf_op jit(solution)/shard_map/all_to_all | solution.py:270
  890.1 59.5 %copy-start.15 = (f32[8,8,128]{2,1,0:T(8,128)S(1)}, f32[8,8,128]{2,1,0:T(8,128)}, u32[]{:S(2)}) copy-start(f32[8,8,128]{2,1,0:T(8,128)} %copy-done.14) | copy-start | bytes 98308
  890.1 61.4 %copy-start.13 = (s32[2,2048]{1,0:T(2,128)S(1)}, s32[2,2048]{1,0:T(2,128)}, u32[]{:S(2)}) copy-start(s32[2,2048]{1,0:T(2,128)} %param.20) | copy-start | bytes 49156
  890.1 61.3 %copy-start.24 = (pred[2,2048]{1,0:T(4,128)(4,1)S(1)}, pred[2,2048]{1,0:T(4,128)(4,1)}, u32[]{:S(2)}) copy-start(pred[2,2048]{1,0:T(4,128)(4,1)} %copy-done.23) | copy-start | bytes 12292
  890.1 61.3 %copy-start.28 = (s32[2,2048]{1,0:T(2,128)S(1)}, s32[2,2048]{1,0:T(2,128)}, u32[]{:S(2)}) copy-start(s32[2,2048]{1,0:T(2,128)} %copy-done.27) | copy-start | bytes 49156
  890.1 62.2 %copy-start.11 = (s32[2,2048]{1,0:T(2,128)S(1)}, s32[2,2048]{1,0:T(2,128)}, u32[]{:S(2)}) copy-start(s32[2,2048]{1,0:T(2,128)} %param.19) | copy-start | bytes 49156
  890.1 62.2 %copy-start.26 = (s32[2,2048]{1,0:T(2,128)S(1)}, s32[2,2048]{1,0:T(2,128)}, u32[]{:S(2)}) copy-start(s32[2,2048]{1,0:T(2,128)} %copy-done.25) | copy-start | bytes 49156
  890.1 62.2 %copy-start.31 = (pred[2,2048]{1,0:T(4,128)(4,1)S(1)}, pred[2,2048]{1,0:T(4,128)(4,1)}, u32[]{:S(2)}) copy-start(pred[2,2048]{1,0:T(4,128)(4,1)} %copy-done.30) | copy-start | bytes 12292
  890.1 63.0 %copy-start.19 = (f32[2,2048]{1,0:T(2,128)S(1)}, f32[2,2048]{1,0:T(2,128)}, u32[]{:S(2)}) copy-start(f32[2,2048]{1,0:T(2,128)} %copy-done.18) | copy-start | bytes 49156
  890.1 63.0 %copy-start.21 = (f32[2,2048]{1,0:T(2,128)S(1)}, f32[2,2048]{1,0:T(2,128)}, u32[]{:S(2)}) copy-start(f32[2,2048]{1,0:T(2,128)} %copy-done.20) | copy-start | bytes 49156
  890.2 63.0 %copy-start.6 = (f32[2,2048,64]{1,2,0:T(8,128)S(1)}, f32[2,2048,64]{1,2,0:T(8,128)}, u32[]{:S(2)}) copy-start(f32[2,2048,64]{1,2,0:T(8,128)} %copy-done.5) | copy-start | bytes 3145732
  890.2 63.0 %copy-start.17 = (f32[2,2048]{1,0:T(2,128)S(1)}, f32[2,2048]{1,0:T(2,128)}, u32[]{:S(2)}) copy-start(f32[2,2048]{1,0:T(2,128)} %copy-done.16) | copy-start | bytes 49156
  890.2 202.4 %all-reduce.2.cloned.1.call-start = ((), (), s32[]{:S(2)}) async-start(), calls=%async_computation.13 | async-start | bytes 1114112 | tf_op jit(solution)/shard_map/psum | solution.py:418
  949.5 13.4 %copy-start.22 = (f32[1,64]{0,1:T(8,128)S(1)}, f32[1,64]{0,1:T(8,128)}, u32[]{:S(2)}) copy-start(f32[1,64]{0,1:T(8,128)} %copy.214) | copy-start | bytes 772
  963.9 131.4 %copy-start.33 = (f32[64]{0:T(128)S(1)}, f32[64]{0:T(128)}, u32[]{:S(2)}) copy-start(f32[64]{0:T(128)} %div.85) | copy-start | bytes 772
  963.9 134.6 %copy-start.8 = (bf16[8,32,16,128]{3,2,1,0:T(8,128)(2,1)S(1)}, bf16[8,32,16,128]{3,2,1,0:T(8,128)(2,1)}, u32[]{:S(2)}) copy-start(bf16[8,32,16,128]{3,2,1,0:T(8,128)(2,1)} %copy-done.7) | copy-start | bytes 3145732
Sparse Core Ops, SparseCore 0:
  964.0 128.4 all-reduce.1

commit v3 on v2

--- a/solution.py
+++ b/solution.py
@@ -12,7 +12,7 @@
 LANES = 128
 MIB = 1024 * 1024
 BATCH = 16
-BASE = 27
+BASE_OUT, BASE_BACK = 26, 27
 MORE = 32
 bf16, f32 = jnp.bfloat16, jnp.float32
 
@@ -261,8 +261,8 @@
         block = groups * cap_rows
         rows = local_experts * block
         mid = rows // 2
-        base = rows * BASE // 32
-        over = rows - base
+        base = rows * BASE_OUT // 32
+        over = rows * (32 - BASE_BACK) // 32
         sub = hidden // LANES
         tokens_loc = groups * seq_len
         tokens_all = tokens_loc * ep_size
@@ -280,26 +280,39 @@
         first_count = jnp.sum(first_hot, axis=1, dtype=f32)
         occupied = jnp.minimum(first_count + jnp.sum(second_kept, axis=1, dtype=f32), cap_rows)
         segments = lambda v: jnp.moveaxis(v.reshape(groups, ep_size, local_experts), 0, 2).reshape(ep_size, local_experts * groups)
+        unsegment = lambda v: jnp.moveaxis(v.reshape(ep_size, local_experts, groups), 2, 0).reshape(groups, experts)
+        peers = jnp.arange(ep_size, dtype=f32)[:, None]
+        look = lambda hot, table: jnp.sum(table * hot, axis=-1)
         held = segments(occupied)
-        starts = jnp.cumsum(held, axis=1) - held
-        lead = rows - jnp.sum(held, axis=1, keepdims=True)
-        place = jnp.arange(ep_size, dtype=f32)[:, None] * rows + starts
-        unsegment = lambda v: jnp.moveaxis(v.reshape(ep_size, local_experts, groups), 2, 0).reshape(groups, experts)
-        place_of, lead_of = unsegment(place), unsegment(jnp.broadcast_to(lead, place.shape))
-
-        def locate(hot, before):
-            pos = jnp.sum(before * hot, axis=-1)
-            there = jnp.sum(place_of[:, None, :] * hot, axis=-1) + pos
-            back = there + jnp.sum(lead_of[:, None, :] * hot, axis=-1)
-            return pos.astype(jnp.int32), there.astype(jnp.int32), back.astype(jnp.int32)
-
-        pos_first, there_first, back_first = locate(first_hot, before_first)
-        pos_second, there_second, back_second = locate(second_hot, before_second + first_count[:, None, :])
+        back_at = unsegment(peers * rows + rows - jnp.sum(held, axis=1, keepdims=True) + jnp.cumsum(held, axis=1) - held)[:, None, :]
+        pos_first = look(first_hot, before_first)
+        pos_second = look(second_hot, before_second + first_count[:, None, :])
         ok_first = pos_first < cap_rows
         ok_second = (keep_ids > 0) & (pos_second < cap_rows)
-        slots_of = jnp.stack([jnp.where(ok_first, back_first, ep_size * rows), jnp.where(ok_second, back_second, ep_size * rows)])
-
-        there = jnp.stack([jnp.where(ok_first, there_first, -1), jnp.where(ok_second, there_second, -1)]).reshape(-1)
+        slots_of = jnp.stack([
+            jnp.where(ok_first, (look(first_hot, back_at) + pos_first).astype(jnp.int32), ep_size * rows),
+            jnp.where(ok_second, (look(second_hot, back_at) + pos_second).astype(jnp.int32), ep_size * rows),
+        ])
+        pos_first, pos_second = pos_first.astype(jnp.int32), pos_second.astype(jnp.int32)
+
+        both = ok_first & ok_second & (first_ids // local_experts == second_ids // local_experts)
+        goes_first = ok_first & ~(both & (second_ids < first_ids))
+        goes_second = ok_second & ~(both & (first_ids < second_ids))
+        first_goes = first_hot * goes_first.astype(bf16)[..., None]
+        second_goes = second_hot * goes_second.astype(bf16)[..., None]
+        ahead_first = jnp.einsum('st,gte->gse', earlier, first_goes, preferred_element_type=f32)
+        ahead_second = jnp.einsum('st,gte->gse', earlier, second_goes, preferred_element_type=f32)
+        first_gone = jnp.sum(first_goes, axis=1, dtype=f32)
+        sent = segments(first_gone + jnp.sum(second_goes, axis=1, dtype=f32))
+        out_at = unsegment(jnp.cumsum(sent, axis=1) - sent)[:, None, :]
+        out_first = look(first_hot, ahead_first + out_at).astype(jnp.int32)
+        out_second = look(second_hot, ahead_second + out_at + first_gone[:, None, :]).astype(jnp.int32)
+        there = jnp.stack([
+            jnp.where(goes_first, first_ids // local_experts * rows + out_first, -1),
+            jnp.where(goes_second, second_ids // local_experts * rows + out_second, -1),
+        ]).reshape(-1)
+        read_first = jnp.where(goes_first, out_first, out_second) + 1
+        read_second = jnp.where(goes_second, out_second, out_first) + 1
         numbers = jnp.arange(2 * tokens_loc, dtype=jnp.int32) % tokens_loc + 1
         outer = ((there // 64)[:, None] == jnp.arange(ep_size * rows // 64, dtype=jnp.int32)).astype(bf16)
         inner = ((there % 64)[:, None] == jnp.arange(64, dtype=jnp.int32)) & (there >= 0)[:, None]
@@ -314,7 +327,7 @@
         r_ranges = ((0, mid), (mid, base), (base, more), (more, rows))
         g_ranges = ((0, over - MORE), (over - MORE, over), (over, mid), (mid, rows))
         x_from = ((0, base, 0), (base, more, 0), (more, rows, 0))
-        r_from = ((0, mid, 0), (mid, base, 0), (base, more, MORE), (more, rows, over - MORE))
+        r_from = ((0, mid, 0), (mid, base, 0), (base, more, MORE), (more, rows, rows - more))
         x_send, x_more, x_rest = gather_rows(send_idx, x_tiles, x_ranges)
 
         tie = lambda *values: lax.optimization_barrier(values)
@@ -333,37 +346,41 @@
         at_first = ((pos_first[..., None] == slots) & ok_first[..., None]).astype(bf16)
         at_second = ((pos_second[..., None] == slots) & ok_second[..., None]).astype(bf16)
         hots = jnp.concatenate([first_hot, second_hot], axis=1)
-        norm_at = jnp.concatenate([at_first * norm_first[..., None], at_second * norm_second[..., None]], axis=1)
-        slot_norm = jnp.einsum('gse,gsk->egk', hots, norm_at, preferred_element_type=f32)
+        digits_at = lambda at, *vs: jnp.concatenate([at * v.astype(bf16)[..., None] for v in vs], axis=-1)
+        norm_at = jnp.concatenate([
+            digits_at(at_first, norm_first, read_first // 64, read_first % 64),
+            digits_at(at_second, norm_second, read_second // 64, read_second % 64),
+        ], axis=1)
+        slot_norm, slot_high, slot_low = jnp.split(jnp.einsum('gse,gsk->egk', hots, norm_at, preferred_element_type=f32), 3, axis=-1)
+        slot_read = slot_high * 64 + slot_low
         dot_xr = jnp.sum(x_here.astype(f32) * r_here.astype(f32))
         to_rows = lambda v: jnp.moveaxis(v, 0, 1)[..., None]
-        fullest = jnp.broadcast_to(jnp.max(jnp.sum(held, axis=1)), (experts, groups, 1))
+        degree = lambda v, top: jnp.sum(jnp.max(jnp.sum(v, axis=1)) > jnp.array([top, top + MORE], f32)).astype(f32)
+        levels = jnp.broadcast_to(jnp.stack([degree(sent, base), degree(held, rows - over)]), (experts, groups, 2))
         tally = jnp.moveaxis(first_count.reshape(groups, local_experts, ep_size), 0, 1)
         tally = jnp.tile(tally, (ep_size, 1, 1))
-        sheet = jnp.concatenate([slot_norm, to_rows(occupied), fullest, tally], axis=-1)
+        sheet = jnp.concatenate([slot_norm, slot_read, levels, to_rows(occupied), tally], axis=-1)
         sheet, x_recv = tie(sheet, x_recv)
         sheet = lax.all_to_all(sheet, 'ep', 0, 1, tiled=True).reshape(local_experts, ep_size, groups, -1)
         expert_norm = sheet[..., :cap_rows].reshape(local_experts, ep_size, block)
-        mine = jnp.moveaxis(sheet[..., cap_rows], 0, 1).reshape(ep_size, local_experts * groups)
-        excess = jnp.max(sheet[0, :, 0, cap_rows + 1]) - base
-        level = jnp.where(excess <= 0, 0, jnp.where(excess <= MORE, 1, 2)).astype(jnp.int32)
-        frac_first = jnp.sum(sheet[..., cap_rows + 2:], axis=(1, 2)).reshape(experts) / tokens_all
+        sheet_read, sheet = sheet[..., cap_rows:2 * cap_rows], sheet[..., 2 * cap_rows:]
+        level_out, level_back = jnp.max(sheet[0, :, 0, :2], axis=0).astype(jnp.int32)
+        mine = jnp.moveaxis(sheet[..., 2], 0, 1).reshape(ep_size, local_experts * groups)
+        frac_first = jnp.sum(sheet[..., 3:], axis=(1, 2)).reshape(experts) / tokens_all
         mine_ends = jnp.cumsum(mine, axis=1)
-        mine_starts = mine_ends - mine
-        slot_ids = jnp.arange(cap_rows, dtype=f32)
-        recv_idx = jnp.where(slot_ids < mine[..., None], mine_starts[..., None] + slot_ids, float(rows)).astype(jnp.int32)
-        recv_idx = recv_idx.reshape(ep_size, local_experts, block)
+        recv_idx = jnp.where(sheet_read > 0, sheet_read - 1, float(rows)).astype(jnp.int32)
+        recv_idx = jnp.moveaxis(recv_idx.reshape(local_experts, ep_size, block), 0, 1)
         packed = jnp.arange(rows, dtype=f32) - (rows - mine_ends[:, -1:])
         passed = (mine_ends[:, None, :] <= packed[..., None]).astype(f32)
         back_row = jnp.sum(passed, axis=-1) * cap_rows + packed - jnp.sum(passed * mine[:, None, :], axis=-1)
         back_idx = jnp.where(packed >= 0, back_row, 0.0).astype(jnp.int32)
 
-        def exchange_over(few, rest):
+        def exchange_over(level, few, rest):
             return lax.switch(level, (lambda u, v: (u, v), lambda u, v: (exchange(u), v), lambda u, v: (exchange(u), exchange(v))), few, rest)
 
         xr_more, xr_rest = jnp.concatenate([x_more, r_more], axis=1), jnp.concatenate([x_rest, r_rest], axis=1)
         xr_more, xr_rest, expert_norm = tie(xr_more, xr_rest, expert_norm)
-        xr_more, xr_rest = exchange_over(xr_more, xr_rest)
+        xr_more, xr_rest = exchange_over(level_out, xr_more, xr_rest)
         r_send_0, xr_more, xr_rest, dot_xr = tie(r_send_0, xr_more, xr_rest, dot_xr)
         r_recv_0 = exchange(r_send_0)
         expert_x = unpack_rows(recv_idx, [x_recv, xr_more, xr_rest], x_from, rows).reshape(local_experts, -1, hidden)
@@ -387,7 +404,7 @@
         grad_y_0, grad_pre_0, slot_dot_0, grad_slots_0 = expert_bwd([r_recv_0], r_from[:1], 0)
         g_rest, g_more, g_send_0 = pack_rows(back_idx, [grad_slots_0], g_ranges[:3])
         g_more, g_rest, r_recv_1 = tie(g_more, g_rest, r_recv_1)
-        g_more, g_rest = exchange_over(g_more, g_rest)
+        g_more, g_rest = exchange_over(level_back, g_more, g_rest)
         g_send_0, g_more, g_rest, r_recv_1 = tie(g_send_0, g_more, g_rest, r_recv_1)
         g_recv_0 = exchange(g_send_0)
         grad_y_1, grad_pre_1, slot_dot_1, grad_slots_1 = expert_bwd([r_recv_0, r_recv_1, xr_more, xr_rest], r_from, 1)

time: 1150 us -> 1110 us (0.965)
  waiting for transfers between devices: 378 us -> 345 us
  blocking collectives: 44.3 us -> 16.8 us
    all_to_all x5, waiting for transfers between devices: 286 us -> 253 us  [layer_body(): exchange = lambda v: lax.all_to_all(v, 'ep', 0, 0, tiled=True)]
    all_to_all x2 -> x1, blocking collectives: 44.3 us -> 16.8 us  [layer_body(): exchange = lambda v: lax.all_to_all(v, 'ep', 0, 0, tiled=True)]
    unnamed x77 -> x81, local copies, waits for them, and re-layouts: 41.2 us -> 40.7 us
  transfers between devices with their start and end apart: 8 -> 8, of which waited for: 7 -> 7; matrix products, arithmetic and copies ran while one was open for 35% -> 37% of each run, Pallas kernels for 16% -> 16%
where the time goes in v3:
time: 1110 us; the launch traced here: 1100 us
  matrix products  351 us (32%)
  waiting for transfers between devices  345 us (31%)
  Pallas kernels  236 us (21%)
  local copies, waits for them, and re-layouts  54.7 us (5%)
  other arithmetic  44.4 us (4%)
  starting transfers between devices  26.9 us (2%)
  between operations  21.5 us (2%)
  blocking collectives  16.8 us (2%)
    all_to_all x5, waiting for transfers between devices, layer_body(): exchange = lambda v: lax.all_to_all(v, 'ep', 0, 0, tiled=True)  253 us
    pallas_call x3, Pallas kernels, unpack_rows(): pl.pallas_call(functools.partial(unpack_kernel, ranges=ranges, scaled=sca...  118 us
    psum x1, waiting for transfers between devices, layer_body(): summed = lax.psum(jnp.concatenate([grad_gate_w, stats], axis=0), 'ep')  84.2 us
    dot_general x2, matrix products, expert_bwd(): jnp.einsum('ech,efh->ecf', grad_y, w_out_loc[chunk], preferred_element_ty...  68.4 us
    dot_general x1, matrix products, layer_body(): jnp.einsum('ecf,ech->efh', act_bf, grad_y, preferred_element_type=f32)  59.3 us
    dot_general x1, matrix products, layer_body(): jnp.einsum('ecf,efh->ech', act_bf, w_out_loc, preferred_element_type=f32)  51.7 us
    dot_general x2, matrix products, expert_bwd(): jnp.einsum('ecf,ehf->ech', grad_pre, w_in_loc[chunk], preferred_element_t...  49.6 us
    dot_general x1, matrix products, layer_body(): jnp.einsum('ech,ehf->ecf', expert_x, w_in_loc, preferred_element_type=f32)  44.5 us
  transfers between devices with their start and end apart: 8, of which 7 were waited for; matrix products, arithmetic and copies ran while one was open for 37% of the time, Pallas kernels for 16%

profile of v3, /device:TPU:0, one launch (start us, length us, event | category | flops | bytes accessed | tf_op | source)
XLA Modules:
  0.0 1098.0 jit_solution(11554680825843199593)
XLA Ops:
  7.2 0.9 convert_reduce_fusion
  8.2 2.8 fusion.135
  11.0 0.7 convert_element_type.247
  11.7 2.8 fusion.132
  15.9 2.0 fusion.126
  18.0 2.0 fusion.129
  20.8 1.4 fusion.66
  22.3 15.2 %copy.258 = bf16[512,8,16,128]{3,2,1,0:T(8,128)(2,1)} copy(bf16[512,8,16,128]{3,1,2,0:T(8,128)(2,1)} %bitcast.180) | data formatting | bytes 33554432
  37.5 21.5 %shard_map.137 = (bf16[8,832,16,128]{3,2,1,0:T(8,128)(2,1)}, bf16[8,32,16,128]{3,2,1,0:T(8,128)(2,1)S(1)}, bf16[8,160,16,128]{3,2,1,0:T(8,128)(2,1)}) custom-call(s32[8192]{0:T(1024)S(1)} %reshape_reshape.4.idx_ref, bf16[4096,16,128]{2,1,0:T(8,128)(2,1)} %bitcast.186), custom_call_target="tpu_custom_call" | custom-call | flops 30000001024 | bytes 60000000 | tf_op jit(solution)/shard_map/pallas_call | solution.py:50
  59.0 5.6 all-to-all-start.6
  65.7 1.3 fusion.207
  69.1 1.3 fusion.206
  71.4 15.2 %copy.256 = bf16[512,8,16,128]{3,2,1,0:T(8,128)(2,1)} copy(bf16[512,8,16,128]{3,1,2,0:T(8,128)(2,1)} %bitcast.183) | data formatting | bytes 33554432
  86.6 11.0 %fusion.227 = (f32[2,2048]{1,0:T(2,128)S(1)}, f32[2,2048,64]{1,2,0:T(8,128)S(1)}) fusion(bf16[2,2048,2048]{2,1,0:T(8,128)(2,1)} %param.16, bf16[2048,64]{0,1:T(8,128)(2,1)S(1)} %copy-done.9), kind=kOutput, calls=%fused_computation.296 | convolution fusion | flops 1074266112 | bytes 18104320 | tf_op jit(solution)/shard_map/sub | solution.py:339
  97.7 0.8 fusion.217
  98.8 0.8 fusion.159
  99.6 1.3 fusion.138
  101.1 21.7 %shard_map.138 = (bf16[8,512,16,128]{3,2,1,0:T(8,128)(2,1)}, bf16[8,320,16,128]{3,2,1,0:T(8,128)(2,1)}, bf16[8,32,16,128]{3,2,1,0:T(8,128)(2,1)S(1)}, bf16[8,160,16,128]{3,2,1,0:T(8,128)(2,1)}) custom-call(s32[8192]{0:T(1024)S(1)} %reshape_reshape.4.idx_ref, bf16[4096,16,128]{2,1,0:T(8,128)(2,1)} %bitcast.185), custom_call_target="tpu_custom_call" | custom-call | flops 30000001024 | bytes 60000000 | tf_op jit(solution)/shard_map/pallas_call | solution.py:50
  122.8 1.5 pad_maximum_fusion.1
  124.4 12.1 %pad_maximum_fusion = bf16[8,320,16,128]{3,2,1,0:T(8,128)(2,1)} fusion(bf16[8,160,16,128]{3,2,1,0:T(8,128)(2,1)} %get-tuple-element.92, bf16[8,160,16,128]{3,2,1,0:T(8,128)(2,1)} %get-tuple-element.91), kind=kLoop, calls=%fused_computation.65 | loop fusion | flops 5242880 | bytes 20971520 | tf_op jit(solution)/shard_map/concatenate | solution.py:381
  136.5 15.9 %multiply_reduce_fusion = f32[]{:T(128)} fusion(bf16[2,2048,2048]{2,1,0:T(8,128)(2,1)} %param.17, bf16[2,2048,2048]{2,1,0:T(8,128)(2,1)} %param.16), kind=kLoop, calls=%fused_computation.14 | loop fusion | flops 33554432 | bytes 33554436 | tf_op jit(solution)/shard_map/reduce_sum | solution.py:356
  152.4 209.7 %all-to-all-done.6.refs_0_ = bf16[8,832,16,128]{3,2,1,0:T(8,128)(2,1)} async-done(((bf16[8,832,16,128]{3,2,1,0:T(8,128)(2,1)}), bf16[8,832,16,128]{3,2,1,0:T(8,128)(2,1)}, u32[]{:S(2)}, u32[]{:S(2)}) %all-to-all-start.6) | async-done | bytes 27263008 | tf_op jit(solution)/shard_map/all_to_all | solution.py:270
  362.0 0.8 copy.222
  362.8 2.1 all-to-all-start.7
  365.6 4.7 all-to-all-done.7
  372.5 4.5 all-to-all-start.8
  377.1 43.4 %shard_map.139 = bf16[8,8,128,2048]{3,2,1,0:T(8,128)(2,1)} custom-call(s32[8192]{0:T(1024)S(1)} %bitcast.179, bf16[8,832,16,128]{3,2,1,0:T(8,128)(2,1)} %all-to-all-done.6.refs_0_, bf16[8,64,16,128]{3,2,1,0:T(8,128)(2,1)S(1)} %get-tuple-element.98.refs_1_.refs_2_, bf16[8,320,16,128]{3,2,1,0:T(8,128)(2,1)} %get-tuple-element.99.refs_2_.refs_3_), custom_call_target="tpu_custom_call" | custom-call | flops 28000000000 | bytes 64000000 | tf_op jit(solution)/shard_map/pallas_call | solution.py:128
  420.5 44.5 %fusion.230 = f32[8,1024,1024]{2,1,0:T(8,128)} fusion(bf16[8,1024,2048]{2,1,0:T(8,128)(2,1)} %bitcast.213, bf16[8,2048,1024]{2,1,0:T(8,128)(2,1)} %param.19), kind=kOutput, calls=%fused_computation.298 | convolution fusion | flops 34359738368 | bytes 100663296 | tf_op jit(solution)/shard_map/ech,ehf->ecf/dot_general | solution.py:387
  467.6 2.7 copy.228.refs_1_.refs_4_
  470.3 51.7 %convolution_convert_fusion.1 = bf16[8,1024,2048]{2,1,0:T(8,128)(2,1)} fusion(bf16[8,1024,2048]{2,1,0:T(8,128)(2,1)} %param.20, f32[8,1024,1024]{2,1,0:T(8,128)} %fusion.230), kind=kOutput, calls=%fused_computation.24 | convolution fusion | flops 34452013056 | bytes 100663296 | tf_op jit(solution)/shard_map/ecf,efh->ech/dot_general | solution.py:389
  522.0 39.0 %all-to-all-done.8.refs_0_ = bf16[8,512,16,128]{3,2,1,0:T(8,128)(2,1)} async-done(((bf16[8,512,16,128]{3,2,1,0:T(8,128)(2,1)}), bf16[8,512,16,128]{3,2,1,0:T(8,128)(2,1)}, u32[]{:S(2)}, u32[]{:S(2)}) %all-to-all-start.8) | async-done | bytes 16777248 | tf_op jit(solution)/shard_map/all_to_all | solution.py:270
  561.0 4.1 all-to-all-start.9
  565.0 2.2 copy-done
  567.2 34.8 %shard_map.140 = (bf16[4,8,128,2048]{3,2,1,0:T(8,128)(2,1)}, f32[4,8,128,128]{3,2,1,0:T(8,128)S(1)}) custom-call(s32[4096]{0:T(1024)S(1)} %bitcast.174, bf16[8,512,16,128]{3,2,1,0:T(8,128)(2,1)} %all-to-all-done.8.refs_0_, f32[8,8,128,1]{3,2,1,0:T(8,128)S(1)} %copy-done, bf16[8,8,128,2048]{3,2,1,0:T(8,128)(2,1)} %bitcast.181), custom_call_target="tpu_custom_call" | custom-call | flops 14000000000 | bytes 32000000 | tf_op jit(solution)/shard_map/pallas_call | solution.py:128
  602.6 34.2 %fusion.18 = bf16[4,1024,1024]{2,1,0:T(8,128)(2,1)} fusion(f32[8,1024,1024]{2,1,0:T(8,128)} %fusion.230, bf16[4,1024,2048]{2,1,0:T(8,128)(2,1)} %bitcast.209, bf16[8,1024,2048]{2,1,0:T(8,128)(2,1)} %param.20), kind=kOutput, calls=%fused_computation.28 | convolution fusion | flops 17272143872 | bytes 58720256 | tf_op jit(solution)/shard_map/ech,efh->ecf/dot_general | solution.py:399
  636.9 24.8 %fusion.56 = bf16[4,1024,2048]{2,1,0:T(8,128)(2,1)} fusion(bf16[4,1024,1024]{2,1,0:T(8,128)(2,1)} %fusion.18, bf16[8,2048,1024]{2,1,0:T(8,128)(2,1)} %param.19), kind=kOutput, calls=%fused_computation.63 | convolution fusion | flops 17188257792 | bytes 41943040 | tf_op jit(solution)/shard_map/ecf,ehf->ech/dot_general | solution.py:401
  661.7 14.5 %shard_map.141 = (bf16[8,128,16,128]{3,2,1,0:T(8,128)(2,1)}, bf16[8,32,16,128]{3,2,1,0:T(8,128)(2,1)S(1)}, bf16[8,352,16,128]{3,2,1,0:T(8,128)(2,1)S(1)}) custom-call(s32[8192]{0:T(1024)S(1)} %bitcast.177, bf16[4,8,128,2048]{3,2,1,0:T(8,128)(2,1)} %bitcast.215), custom_call_target="tpu_custom_call" | custom-call | flops 15000000512 | bytes 35000000 | tf_op jit(solution)/shard_map/pallas_call | solution.py:172
  676.2 4.1 copy-done.2
  680.4 1.2 all-to-all-done.9.refs_1_
  681.6 17.4 %conditional.3 = ((bf16[8,32,16,128]{3,2,1,0:T(8,128)(2,1)S(1)}, bf16[8,128,16,128]{3,2,1,0:T(8,128)(2,1)})) conditional(s32[]{:T(128)} %bitcast.35, (bf16[8,32,16,128]{3,2,1,0:T(8,128)(2,1)S(1)}, bf16[8,128,16,128]{3,2,1,0:T(8,128)(2,1)}) %tuple.46, (bf16[8,32,16,128]{3,2,1,0:T(8,128)(2,1)S(1)}, ...), branch_computations={%region_30.31_spmd, %region_31.32_spmd, %region_32.33_spmd} | conditional | bytes 20971544 | solution.py:379
  681.7 16.8 %all_to_all.84 = bf16[8,32,16,128]{3,2,1,0:T(8,128)(2,1)S(1)} all-to-all(bf16[8,32,16,128]{3,2,1,0:T(8,128)(2,1)S(1)} %copy.286), channel_id=1, replica_groups=mesh['ep'=8] {'ep'}, dimensions={0} | all-to-all | bytes 2097152 | tf_op jit(solution)/shard_map/cond/branch_1_fun/all_to_all | solution.py:270
  699.0 4.0 all-to-all-start.10
  703.0 2.2 copy-done.1
  705.2 40.1 %shard_map.142 = (bf16[4,8,128,2048]{3,2,1,0:T(8,128)(2,1)}, f32[4,8,128,128]{3,2,1,0:T(8,128)S(1)}) custom-call(s32[4096]{0:T(1024)S(1)} %bitcast.175, bf16[8,512,16,128]{3,2,1,0:T(8,128)(2,1)} %all-to-all-done.8.refs_0_, bf16[8,320,16,128]{3,2,1,0:T(8,128)(2,1)} %all-to-all-done.9.refs_1_, bf16[8,64,16,128]{3,2,1,0:T(8,128)(2,1)} %copy-done.4, ...), custom_call_target="tpu_custom_call" | custom-call | flops 14000000000 | bytes 32000000 | tf_op jit(solution)/shard_map/pallas_call | solution.py:128
  745.9 34.2 %fusion.23 = bf16[4,1024,1024]{2,1,0:T(8,128)(2,1)} fusion(f32[8,1024,1024]{2,1,0:T(8,128)} %fusion.230, bf16[4,1024,2048]{2,1,0:T(8,128)(2,1)} %bitcast.211, bf16[8,1024,2048]{2,1,0:T(8,128)(2,1)} %param.20), kind=kOutput, calls=%fused_computation.33 | convolution fusion | flops 17272143872 | bytes 58720256 | tf_op jit(solution)/shard_map/ech,efh->ecf/dot_general | solution.py:399
  780.1 24.8 %fusion.59 = bf16[4,1024,2048]{2,1,0:T(8,128)(2,1)} fusion(bf16[4,1024,1024]{2,1,0:T(8,128)(2,1)} %fusion.23, bf16[8,2048,1024]{2,1,0:T(8,128)(2,1)} %param.19), kind=kOutput, calls=%fused_computation.64 | convolution fusion | flops 17188257792 | bytes 41943040 | tf_op jit(solution)/shard_map/ecf,ehf->ech/dot_general | solution.py:401
  804.9 23.0 %shard_map.143 = bf16[8,512,16,128]{3,2,1,0:T(8,128)(2,1)} custom-call(s32[8192]{0:T(1024)S(1)} %bitcast.178, bf16[4,8,128,2048]{3,2,1,0:T(8,128)(2,1)} %bitcast.216, bf16[4,8,128,2048]{3,2,1,0:T(8,128)(2,1)} %bitcast.218), custom_call_target="tpu_custom_call" | custom-call | flops 15000000512 | bytes 35000000 | tf_op jit(solution)/shard_map/pallas_call | solution.py:172
  827.9 2.8 all-to-all-done.10.refs_2_
  830.9 0.7 reshape.384
  831.6 2.1 all-to-all-start.11
  834.6 3.9 all-to-all-done.11
  838.9 0.7 reduce.13
  839.8 4.5 all-to-all-start.12
  844.4 59.3 %fusion.13 = bf16[8,1024,2048]{2,1,0:T(8,128)(2,1)} fusion(bf16[4,1024,2048]{2,1,0:T(8,128)(2,1)} %bitcast.212, bf16[4,1024,2048]{2,1,0:T(8,128)(2,1)} %bitcast.210, f32[8,1024,1024]{2,1,0:T(8,128)} %fusion.230), kind=kOutput, calls=%fused_computation.25 | convolution fusion | flops 34468790272 | bytes 100663296 | tf_op jit(solution)/shard_map/ecf,ech->efh/dot_general | solution.py:420
  905.6 0.8 fusion.125
  906.5 0.8 fusion.124
  908.3 8.8 convolution_bitcast_fusion
  917.2 0.9 concatenate.45
  918.1 44.0 %convolution_convert_fusion = bf16[8,2048,1024]{2,1,0:T(8,128)(2,1)} fusion(bf16[8,1024,2048]{2,1,0:T(8,128)(2,1)} %bitcast.214, bf16[4,1024,1024]{2,1,0:T(8,128)(2,1)} %fusion.23, bf16[4,1024,1024]{2,1,0:T(8,128)(2,1)} %fusion.18), kind=kOutput, calls=%fused_computation.23 | convolution fusion | flops 34384904192 | bytes 83886080 | tf_op jit(solution)/shard_map/ech,ecf->ehf/dot_general | solution.py:421
  962.5 84.2 %all-reduce.2.cloned.1.call-done = f32[2050,64]{0,1:T(8,128)} async-done(((f32[2050,64]{0,1:T(8,128)}), f32[2050,64]{0,1:T(8,128)}) %all-reduce.2.cloned.1.call-update) | async-done | bytes 524816 | tf_op jit(solution)/shard_map/psum | solution.py:435
  1046.7 1.3 slice.91
  1048.6 0.9 slice_reduce_fusion.1
  1050.8 1.9 slice.93
  1052.7 37.2 %shard_map.144 = bf16[4096,2048]{1,0:T(8,128)(2,1)} custom-call(s32[8192]{0:T(1024)S(1)} %bitcast.176, bf16[8,128,16,128]{3,2,1,0:T(8,128)(2,1)} %get-tuple-element.123.refs_0_, bf16[8,32,16,128]{3,2,1,0:T(8,128)(2,1)S(1)} %copy-done.8, bf16[8,352,16,128]{3,2,1,0:T(8,128)(2,1)} %all-to-all-done.10.refs_2_, ...), custom_call_target="tpu_custom_call" | custom-call | flops 49999998976 | bytes 80000000 | tf_op jit(solution)/shard_map/pallas_call | solution.py:229
  (175 shorter events, 15.7 us)
Async XLA Ops:
  7.2 7.3 copy-start.10
  7.2 7.3 copy-start.31
  7.2 7.3 copy-start.12
  14.6 109.7 %copy-start.22 = (pred[2,2048]{1,0:T(4,128)(4,1)}, pred[2,2048]{1,0:T(4,128)(4,1)S(1)}, u32[]{:S(2)}) copy-start(pred[2,2048]{1,0:T(4,128)(4,1)S(1)} %get-tuple-element.141) | copy-start | bytes 12292
  14.7 109.7 %copy-start.25 = (pred[2,2048]{1,0:T(4,128)(4,1)}, pred[2,2048]{1,0:T(4,128)(4,1)S(1)}, u32[]{:S(2)}) copy-start(pred[2,2048]{1,0:T(4,128)(4,1)S(1)} %get-tuple-element.144) | copy-start | bytes 12292
  59.0 6.7 copy-start.35
  59.0 10.1 copy-start.34
  59.0 12.1 %copy-start.9 = (bf16[2048,64]{0,1:T(8,128)(2,1)S(1)}, bf16[2048,64]{0,1:T(8,128)(2,1)}, u32[]{:S(2)}) copy-start(bf16[2048,64]{0,1:T(8,128)(2,1)} %param.18) | copy-start | bytes 786436
  59.0 303.0 %all-to-all-start.6 = ((bf16[8,832,16,128]{3,2,1,0:T(8,128)(2,1)}), bf16[8,832,16,128]{3,2,1,0:T(8,128)(2,1)}, u32[]{:S(2)}, u32[]{:S(2)}) async-start(bf16[8,832,16,128]{3,2,1,0:T(8,128)(2,1)} %get-tuple-element.82), calls=%async_computation.6 | async-start | bytes 54525952 | tf_op jit(solution)/shard_map/all_to_all | solution.py:270
  64.8 34.0 %copy-start.27 = (s32[2,2048]{1,0:T(2,128)}, s32[2,2048]{1,0:T(2,128)S(1)}, u32[]{:S(2)}) copy-start(s32[2,2048]{1,0:T(2,128)S(1)} %convert_element_type.259) | copy-start | bytes 49156
  64.8 34.0 %copy-start.29 = (s32[2,2048]{1,0:T(2,128)}, s32[2,2048]{1,0:T(2,128)S(1)}, u32[]{:S(2)}) copy-start(s32[2,2048]{1,0:T(2,128)S(1)} %convert_element_type.263) | copy-start | bytes 49156
  97.7 3.2 copy-start.16
  97.7 25.1 %copy-start.5 = (f32[2,2048,64]{1,2,0:T(8,128)}, f32[2,2048,64]{1,2,0:T(8,128)S(1)}, u32[]{:S(2)}) copy-start(f32[2,2048,64]{1,2,0:T(8,128)S(1)} %get-tuple-element.184) | copy-start | bytes 3145732
  98.5 24.3 %copy-start.18 = (f32[2,2048]{1,0:T(2,128)}, f32[2,2048]{1,0:T(2,128)S(1)}, u32[]{:S(2)}) copy-start(f32[2,2048]{1,0:T(2,128)S(1)} %get-tuple-element.128) | copy-start | bytes 49156
  98.5 24.3 %copy-start.20 = (f32[2,2048]{1,0:T(2,128)}, f32[2,2048]{1,0:T(2,128)S(1)}, u32[]{:S(2)}) copy-start(f32[2,2048]{1,0:T(2,128)S(1)} %get-tuple-element.129) | copy-start | bytes 49156
  136.5 235.6 %copy-start.3 = (bf16[8,64,16,128]{3,2,1,0:T(8,128)(2,1)S(1)}, bf16[8,64,16,128]{3,2,1,0:T(8,128)(2,1)}, u32[]{:S(2)}) copy-start(bf16[8,64,16,128]{3,2,1,0:T(8,128)(2,1)} %pad_maximum_fusion.1) | copy-start | bytes 6291460
  362.8 7.5 all-to-all-start.7
  371.2 96.3 %copy-start.14 = (f32[8,8,128]{2,1,0:T(8,128)}, f32[8,8,128]{2,1,0:T(8,128)S(1)}, u32[]{:S(2)}) copy-start(f32[8,8,128]{2,1,0:T(8,128)S(1)} %reshape.363) | copy-start | bytes 98308
  372.5 4.6 copy-start.4
  372.5 188.5 %all-to-all-start.8 = ((bf16[8,512,16,128]{3,2,1,0:T(8,128)(2,1)}), bf16[8,512,16,128]{3,2,1,0:T(8,128)(2,1)}, u32[]{:S(2)}, u32[]{:S(2)}) async-start(bf16[8,512,16,128]{3,2,1,0:T(8,128)(2,1)} %get-tuple-element.100), calls=%async_computation.8 | async-start | bytes 33554432 | tf_op jit(solution)/shard_map/all_to_all | solution.py:270
  561.0 120.6 %all-to-all-start.9 = ((bf16[8,320,16,128]{3,2,1,0:T(8,128)(2,1)}), bf16[8,320,16,128]{3,2,1,0:T(8,128)(2,1)}, u32[]{:S(2)}, u32[]{:S(2)}) async-start(bf16[8,320,16,128]{3,2,1,0:T(8,128)(2,1)} %get-tuple-element.109), calls=%async_computation.9 | async-start | bytes 20971520 | tf_op jit(solution)/shard_map/all_to_all | solution.py:270
  565.0 2.2 copy-start
  676.2 4.1 copy-start.2
  699.0 4.0 copy-start.7
  699.0 131.8 %all-to-all-start.10 = ((bf16[8,352,16,128]{3,2,1,0:T(8,128)(2,1)}), bf16[8,352,16,128]{3,2,1,0:T(8,128)(2,1)}, u32[]{:S(2)}, u32[]{:S(2)}) async-start(bf16[8,352,16,128]{3,2,1,0:T(8,128)(2,1)} %copy-done.2), calls=%async_computation.10 | async-start | bytes 23068672 | tf_op jit(solution)/shard_map/all_to_all | solution.py:270
  703.0 2.2 copy-start.1
  804.9 28.8 %copy-start.32 = (f32[8,8]{0,1:T(8,128)S(1)}, f32[8,8]{0,1:T(8,128)}, u32[]{:S(2)}) copy-start(f32[8,8]{0,1:T(8,128)} %copy.255) | copy-start | bytes 772
  831.6 6.9 all-to-all-start.11
  839.8 212.9 %all-to-all-start.12 = ((bf16[8,512,16,128]{3,2,1,0:T(8,128)(2,1)}), bf16[8,512,16,128]{3,2,1,0:T(8,128)(2,1)}, u32[]{:S(2)}, u32[]{:S(2)}) async-start(bf16[8,512,16,128]{3,2,1,0:T(8,128)(2,1)} %shard_map.143), calls=%async_computation.12 | async-start | bytes 33554432 | tf_op jit(solution)/shard_map/all_to_all | solution.py:270
  844.2 59.5 %copy-start.15 = (f32[8,8,128]{2,1,0:T(8,128)S(1)}, f32[8,8,128]{2,1,0:T(8,128)}, u32[]{:S(2)}) copy-start(f32[8,8,128]{2,1,0:T(8,128)} %copy-done.14) | copy-start | bytes 98308
  844.2 61.4 %copy-start.13 = (s32[2,2048]{1,0:T(2,128)S(1)}, s32[2,2048]{1,0:T(2,128)}, u32[]{:S(2)}) copy-start(s32[2,2048]{1,0:T(2,128)} %param.22) | copy-start | bytes 49156
  844.2 61.4 %copy-start.26 = (pred[2,2048]{1,0:T(4,128)(4,1)S(1)}, pred[2,2048]{1,0:T(4,128)(4,1)}, u32[]{:S(2)}) copy-start(pred[2,2048]{1,0:T(4,128)(4,1)} %copy-done.25) | copy-start | bytes 12292
  844.3 61.4 %copy-start.30 = (s32[2,2048]{1,0:T(2,128)S(1)}, s32[2,2048]{1,0:T(2,128)}, u32[]{:S(2)}) copy-start(s32[2,2048]{1,0:T(2,128)} %copy-done.29) | copy-start | bytes 49156
  844.3 62.2 %copy-start.11 = (s32[2,2048]{1,0:T(2,128)S(1)}, s32[2,2048]{1,0:T(2,128)}, u32[]{:S(2)}) copy-start(s32[2,2048]{1,0:T(2,128)} %param.21) | copy-start | bytes 49156
  844.3 62.2 %copy-start.23 = (pred[2,2048]{1,0:T(4,128)(4,1)S(1)}, pred[2,2048]{1,0:T(4,128)(4,1)}, u32[]{:S(2)}) copy-start(pred[2,2048]{1,0:T(4,128)(4,1)} %copy-done.22) | copy-start | bytes 12292
  844.3 62.2 %copy-start.28 = (s32[2,2048]{1,0:T(2,128)S(1)}, s32[2,2048]{1,0:T(2,128)}, u32[]{:S(2)}) copy-start(s32[2,2048]{1,0:T(2,128)} %copy-done.27) | copy-start | bytes 49156
  844.3 63.0 %copy-start.19 = (f32[2,2048]{1,0:T(2,128)S(1)}, f32[2,2048]{1,0:T(2,128)}, u32[]{:S(2)}) copy-start(f32[2,2048]{1,0:T(2,128)} %copy-done.18) | copy-start | bytes 49156
  844.3 63.0 %copy-start.21 = (f32[2,2048]{1,0:T(2,128)S(1)}, f32[2,2048]{1,0:T(2,128)}, u32[]{:S(2)}) copy-start(f32[2,2048]{1,0:T(2,128)} %copy-done.20) | copy-start | bytes 49156
  844.3 63.0 %copy-start.6 = (f32[2,2048,64]{1,2,0:T(8,128)S(1)}, f32[2,2048,64]{1,2,0:T(8,128)}, u32[]{:S(2)}) copy-start(f32[2,2048,64]{1,2,0:T(8,128)} %copy-done.5) | copy-start | bytes 3145732
  844.3 63.0 %copy-start.17 = (f32[2,2048]{1,0:T(2,128)S(1)}, f32[2,2048]{1,0:T(2,128)}, u32[]{:S(2)}) copy-start(f32[2,2048]{1,0:T(2,128)} %copy-done.16) | copy-start | bytes 49156
  844.3 202.4 %all-reduce.2.cloned.1.call-start = ((), (), s32[]{:S(2)}) async-start(), calls=%async_computation.13 | async-start | bytes 1114112 | tf_op jit(solution)/shard_map/psum | solution.py:435
  903.7 13.4 %copy-start.24 = (f32[1,64]{0,1:T(8,128)S(1)}, f32[1,64]{0,1:T(8,128)}, u32[]{:S(2)}) copy-start(f32[1,64]{0,1:T(8,128)} %copy.241) | copy-start | bytes 772
  918.1 131.5 %copy-start.33 = (f32[64]{0:T(128)S(1)}, f32[64]{0:T(128)}, u32[]{:S(2)}) copy-start(f32[64]{0:T(128)} %div.141) | copy-start | bytes 772
  918.1 134.6 %copy-start.8 = (bf16[8,32,16,128]{3,2,1,0:T(8,128)(2,1)S(1)}, bf16[8,32,16,128]{3,2,1,0:T(8,128)(2,1)}, u32[]{:S(2)}) copy-start(bf16[8,32,16,128]{3,2,1,0:T(8,128)(2,1)} %copy-done.7) | copy-start | bytes 3145732
Sparse Core Ops, SparseCore 0:
  918.2 128.4 all-reduce.1

commit v4 on v3

--- a/solution.py
+++ b/solution.py
@@ -13,7 +13,7 @@
 MIB = 1024 * 1024
 BATCH = 16
 BASE_OUT, BASE_BACK = 26, 27
-MORE = 32
+STEPS = (32, 32)
 bf16, f32 = jnp.bfloat16, jnp.float32
 
 
@@ -322,18 +322,21 @@
 
         x_tiles = x_loc.reshape(tokens_loc, sub, LANES)
         r_tiles = r_loc.reshape(tokens_loc, sub, LANES)
-        more = base + MORE
-        x_ranges = ((0, base), (base, more), (more, rows))
-        r_ranges = ((0, mid), (mid, base), (base, more), (more, rows))
-        g_ranges = ((0, over - MORE), (over - MORE, over), (over, mid), (mid, rows))
-        x_from = ((0, base, 0), (base, more, 0), (more, rows, 0))
-        r_from = ((0, mid, 0), (mid, base, 0), (base, more, MORE), (more, rows, rows - more))
-        x_send, x_more, x_rest = gather_rows(send_idx, x_tiles, x_ranges)
+        extra = lambda start: [start + sum(STEPS[:k]) for k in range(len(STEPS) + 1)]
+        spans = lambda edges: tuple(zip(edges[:-1], edges[1:]))
+        out_over = spans(extra(base) + [rows])
+        back_over = spans([0] + [rows - v for v in extra(rows - over)[::-1]])
+        x_ranges = ((0, base), *out_over)
+        r_ranges = ((0, mid), (mid, base), *out_over)
+        g_ranges = (*back_over, (over, mid), (mid, rows))
+        x_from = tuple((low, high, 0) for low, high in x_ranges)
+        r_from = ((0, mid, 0), (mid, base, 0), *((low, high, high - low) for low, high in out_over))
+        x_send, *x_over = gather_rows(send_idx, x_tiles, x_ranges)
 
         tie = lambda *values: lax.optimization_barrier(values)
         x_recv = exchange(x_send)
         x_here, r_here, r_tiles, _ = tie(x_loc, r_loc, r_tiles, x_send)
-        r_send_0, r_send_1, r_more, r_rest = gather_rows(send_idx, r_tiles, r_ranges)
+        r_send_0, r_send_1, *r_over = gather_rows(send_idx, r_tiles, r_ranges)
 
         logits = jnp.einsum('gsh,he->gse', x_here, w_gate, preferred_element_type=f32)
         router_prob = jax.nn.softmax(logits, axis=-1)
@@ -355,7 +358,7 @@
         slot_read = slot_high * 64 + slot_low
         dot_xr = jnp.sum(x_here.astype(f32) * r_here.astype(f32))
         to_rows = lambda v: jnp.moveaxis(v, 0, 1)[..., None]
-        degree = lambda v, top: jnp.sum(jnp.max(jnp.sum(v, axis=1)) > jnp.array([top, top + MORE], f32)).astype(f32)
+        degree = lambda v, top: jnp.sum(jnp.max(jnp.sum(v, axis=1)) > jnp.array(extra(top), f32)).astype(f32)
         levels = jnp.broadcast_to(jnp.stack([degree(sent, base), degree(held, rows - over)]), (experts, groups, 2))
         tally = jnp.moveaxis(first_count.reshape(groups, local_experts, ep_size), 0, 1)
         tally = jnp.tile(tally, (ep_size, 1, 1))
@@ -375,15 +378,16 @@
         back_row = jnp.sum(passed, axis=-1) * cap_rows + packed - jnp.sum(passed * mine[:, None, :], axis=-1)
         back_idx = jnp.where(packed >= 0, back_row, 0.0).astype(jnp.int32)
 
-        def exchange_over(level, few, rest):
-            return lax.switch(level, (lambda u, v: (u, v), lambda u, v: (exchange(u), v), lambda u, v: (exchange(u), exchange(v))), few, rest)
-
-        xr_more, xr_rest = jnp.concatenate([x_more, r_more], axis=1), jnp.concatenate([x_rest, r_rest], axis=1)
-        xr_more, xr_rest, expert_norm = tie(xr_more, xr_rest, expert_norm)
-        xr_more, xr_rest = exchange_over(level_out, xr_more, xr_rest)
-        r_send_0, xr_more, xr_rest, dot_xr = tie(r_send_0, xr_more, xr_rest, dot_xr)
+        def exchange_over(level, pieces):
+            branch = lambda k: lambda *ps: tuple(exchange(p) if i < k else p for i, p in enumerate(ps))
+            return lax.switch(level, [branch(k) for k in range(len(pieces) + 1)], *pieces)
+
+        xr_over = [jnp.concatenate(pair, axis=1) for pair in zip(x_over, r_over)]
+        *xr_over, expert_norm = tie(*xr_over, expert_norm)
+        xr_over = exchange_over(level_out, xr_over)
+        r_send_0, dot_xr, *xr_over = tie(r_send_0, dot_xr, *xr_over)
         r_recv_0 = exchange(r_send_0)
-        expert_x = unpack_rows(recv_idx, [x_recv, xr_more, xr_rest], x_from, rows).reshape(local_experts, -1, hidden)
+        expert_x = unpack_rows(recv_idx, [x_recv, *xr_over], x_from, rows).reshape(local_experts, -1, hidden)
         pre_act = jnp.einsum('ech,ehf->ecf', expert_x, w_in_loc, preferred_element_type=f32)
         act_bf = gelu_bf16(pre_act)
         expert_y = jnp.einsum('ecf,efh->ech', act_bf, w_out_loc, preferred_element_type=f32).astype(bf16)
@@ -402,13 +406,13 @@
             return grad_y, grad_pre, slot_dot, grad_slots.reshape(half, ep_size, block, hidden)
 
         grad_y_0, grad_pre_0, slot_dot_0, grad_slots_0 = expert_bwd([r_recv_0], r_from[:1], 0)
-        g_rest, g_more, g_send_0 = pack_rows(back_idx, [grad_slots_0], g_ranges[:3])
-        g_more, g_rest, r_recv_1 = tie(g_more, g_rest, r_recv_1)
-        g_more, g_rest = exchange_over(level_back, g_more, g_rest)
-        g_send_0, g_more, g_rest, r_recv_1 = tie(g_send_0, g_more, g_rest, r_recv_1)
+        *g_over, g_send_0 = pack_rows(back_idx, [grad_slots_0], g_ranges[:-1])
+        r_recv_1, *g_over = tie(r_recv_1, *g_over)
+        g_over = exchange_over(level_back, g_over[::-1])[::-1]
+        g_send_0, r_recv_1, *g_over = tie(g_send_0, r_recv_1, *g_over)
         g_recv_0 = exchange(g_send_0)
-        grad_y_1, grad_pre_1, slot_dot_1, grad_slots_1 = expert_bwd([r_recv_0, r_recv_1, xr_more, xr_rest], r_from, 1)
-        g_send_1, = pack_rows(back_idx, [grad_slots_0, grad_slots_1], g_ranges[3:])
+        grad_y_1, grad_pre_1, slot_dot_1, grad_slots_1 = expert_bwd([r_recv_0, r_recv_1, *xr_over], r_from, 1)
+        g_send_1, = pack_rows(back_idx, [grad_slots_0, grad_slots_1], g_ranges[-1:])
         slot_dot = jnp.concatenate([slot_dot_0, slot_dot_1], axis=0)
         slot_dot, g_send_1, g_recv_0 = tie(slot_dot, g_send_1, g_recv_0)
         home_dot = lax.all_to_all(slot_dot.reshape(local_experts, ep_size * groups, cap_rows), 'ep', 1, 0, tiled=True)
@@ -436,7 +440,7 @@
         grad_gate_w, prob_sum, dot_sum = summed[:hidden], summed[hidden], summed[hidden + 1, 0]
         loss_value = dot_sum / numel + ALPHA * experts * jnp.sum(frac_first * prob_sum / tokens_all)
 
-        grad_x = combine_rows(slots_of, [g_rest, g_more, g_recv_0, g_recv_1], g_ranges, r_loc.reshape(-1, hidden), grad_logits_bf.reshape(-1, experts), w_gate)
+        grad_x = combine_rows(slots_of, [*g_over, g_recv_0, g_recv_1], g_ranges, r_loc.reshape(-1, hidden), grad_logits_bf.reshape(-1, experts), w_gate)
         return loss_value, grad_x.reshape(x_loc.shape), grad_w_in, grad_w_out, grad_gate_w
 
     row_spec = P('ep', None, None)

time: 1110 us -> 1110 us (level)
    unnamed x81 -> x85, local copies, waits for them, and re-layouts: 40.7 us -> 40.7 us
where the time goes in v4:
time: 1110 us; the launch traced here: 1100 us
  matrix products  351 us (32%)
  waiting for transfers between devices  348 us (31%)
  Pallas kernels  236 us (21%)
  local copies, waits for them, and re-layouts  54.7 us (5%)
  other arithmetic  41.8 us (4%)
  starting transfers between devices  27 us (2%)
  between operations  21.6 us (2%)
  blocking collectives  16.6 us (1%)
    all_to_all x5, waiting for transfers between devices, layer_body(): exchange = lambda v: lax.all_to_all(v, 'ep', 0, 0, tiled=True)  255 us
    pallas_call x3, Pallas kernels, unpack_rows(): pl.pallas_call(functools.partial(unpack_kernel, ranges=ranges, scaled=sca...  118 us
    psum x1, waiting for transfers between devices, layer_body(): summed = lax.psum(jnp.concatenate([grad_gate_w, stats], axis=0), 'ep')  84.2 us
    dot_general x2, matrix products, expert_bwd(): jnp.einsum('ech,efh->ecf', grad_y, w_out_loc[chunk], preferred_element_ty...  68.4 us
    dot_general x1, matrix products, layer_body(): jnp.einsum('ecf,ech->efh', act_bf, grad_y, preferred_element_type=f32)  59.3 us
    dot_general x1, matrix products, layer_body(): jnp.einsum('ecf,efh->ech', act_bf, w_out_loc, preferred_element_type=f32)  51.7 us
    dot_general x2, matrix products, expert_bwd(): jnp.einsum('ecf,ehf->ech', grad_pre, w_in_loc[chunk], preferred_element_t...  49.6 us
    dot_general x1, matrix products, layer_body(): jnp.einsum('ech,ehf->ecf', expert_x, w_in_loc, preferred_element_type=f32)  44.5 us
  transfers between devices with their start and end apart: 8, of which 7 were waited for; matrix products, arithmetic and copies ran while one was open for 37% of the time, Pallas kernels for 16%

profile of v4, /device:TPU:0, one launch (start us, length us, event | category | flops | bytes accessed | tf_op | source)
XLA Modules:
  0.0 1098.1 jit_solution(926226820138571560)
XLA Ops:
  7.2 0.9 convert_reduce_fusion
  8.2 2.8 fusion.135
  11.0 0.7 convert_element_type.247
  11.7 2.8 fusion.132
  15.9 2.0 fusion.126
  18.0 2.0 fusion.129
  20.8 1.4 fusion.66
  22.3 15.2 %copy.258 = bf16[512,8,16,128]{3,2,1,0:T(8,128)(2,1)} copy(bf16[512,8,16,128]{3,1,2,0:T(8,128)(2,1)} %bitcast.180) | data formatting | bytes 33554432
  37.5 21.7 %shard_map.137 = (bf16[8,832,16,128]{3,2,1,0:T(8,128)(2,1)}, bf16[8,32,16,128]{3,2,1,0:T(8,128)(2,1)S(1)}, bf16[8,32,16,128]{3,2,1,0:T(8,128)(2,1)}, bf16[8,128,16,128]{3,2,1,0:T(8,128)(2,1)}) custom-call(s32[8192]{0:T(1024)S(1)} %reshape_reshape.4.idx_ref, bf16[4096,16,128]{2,1,0:T(8,128)(2,1)} %bitcast.188), custom_call_target="tpu_custom_call" | custom-call | flops 30000001024 | bytes 60000000 | tf_op jit(solution)/shard_map/pallas_call | solution.py:50
  59.2 5.6 all-to-all-start.12
  65.9 1.3 fusion.207
  69.3 1.3 fusion.206
  71.6 15.2 %copy.256 = bf16[512,8,16,128]{3,2,1,0:T(8,128)(2,1)} copy(bf16[512,8,16,128]{3,1,2,0:T(8,128)(2,1)} %bitcast.185) | data formatting | bytes 33554432
  86.8 11.0 %fusion.227 = (f32[2,2048]{1,0:T(2,128)S(1)}, f32[2,2048,64]{1,2,0:T(8,128)S(1)}) fusion(bf16[2,2048,2048]{2,1,0:T(8,128)(2,1)} %param.18, bf16[2048,64]{0,1:T(8,128)(2,1)S(1)} %copy-done.10), kind=kOutput, calls=%fused_computation.297 | convolution fusion | flops 1074266112 | bytes 18104320 | tf_op jit(solution)/shard_map/sub | solution.py:342
  97.9 0.8 fusion.217
  99.0 0.8 fusion.159
  99.8 1.3 fusion.138
  101.3 21.7 %shard_map.138 = (bf16[8,512,16,128]{3,2,1,0:T(8,128)(2,1)}, bf16[8,320,16,128]{3,2,1,0:T(8,128)(2,1)}, bf16[8,32,16,128]{3,2,1,0:T(8,128)(2,1)S(1)}, bf16[8,32,...) custom-call(s32[8192]{0:T(1024)S(1)} %reshape_reshape.4.idx_ref, bf16[4096,16,128]{2,1,0:T(8,128)(2,1)} %bitcast.187), custom_call_target="tpu_custom_call" | custom-call | flops 30000001024 | bytes 60000000 | tf_op jit(solution)/shard_map/pallas_call | solution.py:50
  123.0 3.7 pad_maximum_fusion.1
  126.7 7.4 pad_maximum_fusion
  134.1 15.9 %multiply_reduce_fusion = f32[]{:T(128)} fusion(bf16[2,2048,2048]{2,1,0:T(8,128)(2,1)} %param.19, bf16[2,2048,2048]{2,1,0:T(8,128)(2,1)} %param.18), kind=kLoop, calls=%fused_computation.14 | loop fusion | flops 33554432 | bytes 33554436 | tf_op jit(solution)/shard_map/reduce_sum | solution.py:359
  150.0 212.2 %all-to-all-done.12.refs_0_ = bf16[8,832,16,128]{3,2,1,0:T(8,128)(2,1)} async-done(((bf16[8,832,16,128]{3,2,1,0:T(8,128)(2,1)}), bf16[8,832,16,128]{3,2,1,0:T(8,128)(2,1)}, u32[]{:S(2)}, u32[]{:S(2)}) %all-to-all-start.12) | async-done | bytes 27263008 | tf_op jit(solution)/shard_map/all_to_all | solution.py:270
  362.2 0.8 copy.222
  363.0 2.1 all-to-all-start.13
  365.8 4.7 all-to-all-done.13
  372.7 4.5 all-to-all-start.14
  377.3 43.4 %shard_map.139 = bf16[8,8,128,2048]{3,2,1,0:T(8,128)(2,1)} custom-call(s32[8192]{0:T(1024)S(1)} %bitcast.179, bf16[8,832,16,128]{3,2,1,0:T(8,128)(2,1)} %all-to-all-done.12.refs_0_, bf16[8,64,16,128]{3,2,1,0:T(8,128)(2,1)S(1)} %get-tuple-element.145.refs_1_.refs_2_, bf16[8,64,16,128]{3,2,1,0:T(8,128)(2,1)} %get-tuple-element.146.refs_2_.refs_3_, ...), custom_call_target="tpu_custom_call" | custom-call | flops 28000000000 | bytes 64000000 | tf_op jit(solution)/shard_map/pallas_call | solution.py:128
  420.7 44.5 %fusion.230 = f32[8,1024,1024]{2,1,0:T(8,128)} fusion(bf16[8,1024,2048]{2,1,0:T(8,128)(2,1)} %bitcast.215, bf16[8,2048,1024]{2,1,0:T(8,128)(2,1)} %param.21), kind=kOutput, calls=%fused_computation.299 | convolution fusion | flops 34359738368 | bytes 100663296 | tf_op jit(solution)/shard_map/ech,ehf->ecf/dot_general | solution.py:391
  467.8 2.7 copy.228.refs_1_.refs_5_
  470.5 51.7 %convolution_convert_fusion.1 = bf16[8,1024,2048]{2,1,0:T(8,128)(2,1)} fusion(bf16[8,1024,2048]{2,1,0:T(8,128)(2,1)} %param.22, f32[8,1024,1024]{2,1,0:T(8,128)} %fusion.230), kind=kOutput, calls=%fused_computation.24 | convolution fusion | flops 34452013056 | bytes 100663296 | tf_op jit(solution)/shard_map/ecf,efh->ech/dot_general | solution.py:393
  522.2 39.0 %all-to-all-done.14.refs_0_ = bf16[8,512,16,128]{3,2,1,0:T(8,128)(2,1)} async-done(((bf16[8,512,16,128]{3,2,1,0:T(8,128)(2,1)}), bf16[8,512,16,128]{3,2,1,0:T(8,128)(2,1)}, u32[]{:S(2)}, u32[]{:S(2)}) %all-to-all-start.14) | async-done | bytes 16777248 | tf_op jit(solution)/shard_map/all_to_all | solution.py:270
  561.2 4.0 all-to-all-start.15
  565.2 2.2 copy-done
  567.4 34.8 %shard_map.140 = (bf16[4,8,128,2048]{3,2,1,0:T(8,128)(2,1)}, f32[4,8,128,128]{3,2,1,0:T(8,128)S(1)}) custom-call(s32[4096]{0:T(1024)S(1)} %bitcast.174, bf16[8,512,16,128]{3,2,1,0:T(8,128)(2,1)} %all-to-all-done.14.refs_0_, f32[8,8,128,1]{3,2,1,0:T(8,128)S(1)} %copy-done, bf16[8,8,128,2048]{3,2,1,0:T(8,128)(2,1)} %bitcast.181), custom_call_target="tpu_custom_call" | custom-call | flops 14000000000 | bytes 32000000 | tf_op jit(solution)/shard_map/pallas_call | solution.py:128
  602.8 34.2 %fusion.18 = bf16[4,1024,1024]{2,1,0:T(8,128)(2,1)} fusion(f32[8,1024,1024]{2,1,0:T(8,128)} %fusion.230, bf16[4,1024,2048]{2,1,0:T(8,128)(2,1)} %bitcast.211, bf16[8,1024,2048]{2,1,0:T(8,128)(2,1)} %param.22), kind=kOutput, calls=%fused_computation.28 | convolution fusion | flops 17272143872 | bytes 58720256 | tf_op jit(solution)/shard_map/ech,efh->ecf/dot_general | solution.py:403
  637.0 24.8 %fusion.56 = bf16[4,1024,2048]{2,1,0:T(8,128)(2,1)} fusion(bf16[4,1024,1024]{2,1,0:T(8,128)(2,1)} %fusion.18, bf16[8,2048,1024]{2,1,0:T(8,128)(2,1)} %param.21), kind=kOutput, calls=%fused_computation.63 | convolution fusion | flops 17188257792 | bytes 41943040 | tf_op jit(solution)/shard_map/ecf,ehf->ech/dot_general | solution.py:405
  661.9 14.3 %shard_map.141 = (bf16[8,96,16,128]{3,2,1,0:T(8,128)(2,1)}, bf16[8,32,16,128]{3,2,1,0:T(8,128)(2,1)S(1)}, bf16[8,32,16,128]{3,2,1,0:T(8,128)(2,1)S(1)}, bf16[8,352,16,128]{3,2,1,0:T(8,128)(2,1)S(1)}) custom-call(s32[8192]{0:T(1024)S(1)} %bitcast.177, bf16[4,8,128,2048]{3,2,1,0:T(8,128)(2,1)} %bitcast.217), custom_call_target="tpu_custom_call" | custom-call | flops 15000000512 | bytes 35000000 | tf_op jit(solution)/shard_map/pallas_call | solution.py:172
  676.2 4.1 copy-done.2
  680.3 1.4 all-to-all-done.15.refs_1_
  681.7 17.2 %conditional.3 = ((bf16[8,32,16,128]{3,2,1,0:T(8,128)(2,1)S(1)}, bf16[8,32,16,128]{3,2,1,0:T(8,128)(2,1)S(1)}, bf16[8,96,16,128]{3,2,1,0:T(8,128)(2,1)})) conditional(s32[]{:T(128)} %bitcast.35, (bf16[8,32,16,128]{3,2,1,0:T(8,128)(2,1)S(1)}, bf16[8,32,16,128]{3,2,1,0:T(8,128)(2,1)S(1)}, ...), branch_computations={%region_31.32_spmd, %region_32.33_spmd, %region_33.34_spmd, %regio... | conditional | bytes 20971552 | solution.py:383
  681.9 16.6 %all_to_all.110 = bf16[8,32,16,128]{3,2,1,0:T(8,128)(2,1)S(1)} all-to-all(bf16[8,32,16,128]{3,2,1,0:T(8,128)(2,1)S(1)} %copy.300), channel_id=1, replica_groups=mesh['ep'=8] {'ep'}, dimensions={0} | all-to-all | bytes 2097152 | tf_op jit(solution)/shard_map/cond/branch_1_fun/all_to_all | solution.py:270
  699.0 4.1 all-to-all-start.16
  703.0 2.2 copy-done.1
  705.2 40.1 %shard_map.142 = (bf16[4,8,128,2048]{3,2,1,0:T(8,128)(2,1)}, f32[4,8,128,128]{3,2,1,0:T(8,128)S(1)}) custom-call(s32[4096]{0:T(1024)S(1)} %bitcast.175, bf16[8,512,16,128]{3,2,1,0:T(8,128)(2,1)} %all-to-all-done.14.refs_0_, bf16[8,320,16,128]{3,2,1,0:T(8,128)(2,1)} %all-to-all-done.15.refs_1_, bf16[8,64,16,128]{3,2,1,0:T(8,128)(2,1)} %copy-done.4, ...), custom_call_target="tpu_custom_call" | custom-call | flops 14000000000 | bytes 32000000 | tf_op jit(solution)/shard_map/pallas_call | solution.py:128
  745.9 34.2 %fusion.23 = bf16[4,1024,1024]{2,1,0:T(8,128)(2,1)} fusion(f32[8,1024,1024]{2,1,0:T(8,128)} %fusion.230, bf16[4,1024,2048]{2,1,0:T(8,128)(2,1)} %bitcast.213, bf16[8,1024,2048]{2,1,0:T(8,128)(2,1)} %param.22), kind=kOutput, calls=%fused_computation.33 | convolution fusion | flops 17272143872 | bytes 58720256 | tf_op jit(solution)/shard_map/ech,efh->ecf/dot_general | solution.py:403
  780.2 24.8 %fusion.59 = bf16[4,1024,2048]{2,1,0:T(8,128)(2,1)} fusion(bf16[4,1024,1024]{2,1,0:T(8,128)(2,1)} %fusion.23, bf16[8,2048,1024]{2,1,0:T(8,128)(2,1)} %param.21), kind=kOutput, calls=%fused_computation.64 | convolution fusion | flops 17188257792 | bytes 41943040 | tf_op jit(solution)/shard_map/ecf,ehf->ech/dot_general | solution.py:405
  804.9 23.0 %shard_map.143 = bf16[8,512,16,128]{3,2,1,0:T(8,128)(2,1)} custom-call(s32[8192]{0:T(1024)S(1)} %bitcast.178, bf16[4,8,128,2048]{3,2,1,0:T(8,128)(2,1)} %bitcast.218, bf16[4,8,128,2048]{3,2,1,0:T(8,128)(2,1)} %bitcast.220), custom_call_target="tpu_custom_call" | custom-call | flops 15000000512 | bytes 35000000 | tf_op jit(solution)/shard_map/pallas_call | solution.py:172
  828.0 2.8 all-to-all-done.16.refs_3_
  830.9 0.7 reshape.384
  831.6 2.1 all-to-all-start.17
  834.5 3.9 all-to-all-done.17
  838.9 0.7 reduce.13
  839.8 4.5 all-to-all-start.18
  844.4 59.3 %fusion.13 = bf16[8,1024,2048]{2,1,0:T(8,128)(2,1)} fusion(bf16[4,1024,2048]{2,1,0:T(8,128)(2,1)} %bitcast.214, bf16[4,1024,2048]{2,1,0:T(8,128)(2,1)} %bitcast.212, f32[8,1024,1024]{2,1,0:T(8,128)} %fusion.230), kind=kOutput, calls=%fused_computation.25 | convolution fusion | flops 34468790272 | bytes 100663296 | tf_op jit(solution)/shard_map/ecf,ech->efh/dot_general | solution.py:424
  905.6 0.8 fusion.125
  906.5 0.8 fusion.124
  908.3 8.8 convolution_bitcast_fusion
  917.2 0.9 concatenate.49
  918.1 44.0 %convolution_convert_fusion = bf16[8,2048,1024]{2,1,0:T(8,128)(2,1)} fusion(bf16[8,1024,2048]{2,1,0:T(8,128)(2,1)} %bitcast.216, bf16[4,1024,1024]{2,1,0:T(8,128)(2,1)} %fusion.23, bf16[4,1024,1024]{2,1,0:T(8,128)(2,1)} %fusion.18), kind=kOutput, calls=%fused_computation.23 | convolution fusion | flops 34384904192 | bytes 83886080 | tf_op jit(solution)/shard_map/ech,ecf->ehf/dot_general | solution.py:425
  962.6 84.2 %all-reduce.2.cloned.1.call-done = f32[2050,64]{0,1:T(8,128)} async-done(((f32[2050,64]{0,1:T(8,128)}), f32[2050,64]{0,1:T(8,128)}) %all-reduce.2.cloned.1.call-update) | async-done | bytes 524816 | tf_op jit(solution)/shard_map/psum | solution.py:439
  1046.7 1.3 slice.91
  1048.6 0.9 slice_reduce_fusion.1
  1050.8 1.9 slice.93
  1052.7 37.2 %shard_map.144 = bf16[4096,2048]{1,0:T(8,128)(2,1)} custom-call(s32[8192]{0:T(1024)S(1)} %bitcast.176, bf16[8,96,16,128]{3,2,1,0:T(8,128)(2,1)} %get-tuple-element.174.refs_0_, bf16[8,32,16,128]{3,2,1,0:T(8,128)(2,1)} %copy-done.9, bf16[8,32,16,128]{3,2,1,0:T(8,128)(2,1)S(1)} %copy-done.8, bf16[8,352,16,128]{3,2,1,0:T(8,128)(2,1)} %all-to-all-done.16.refs_3_, ...), custom_call_target="tpu_custom_call" | custom-call | flops 49999998976 | bytes 80000000 | tf_op jit(solution)/shard_map/pallas_call | solution.py:229
  (179 shorter events, 15.7 us)
Async XLA Ops:
  7.2 7.3 copy-start.11
  7.2 7.3 copy-start.33
  7.2 7.3 copy-start.14
  14.6 112.0 %copy-start.24 = (pred[2,2048]{1,0:T(4,128)(4,1)}, pred[2,2048]{1,0:T(4,128)(4,1)S(1)}, u32[]{:S(2)}) copy-start(pred[2,2048]{1,0:T(4,128)(4,1)S(1)} %get-tuple-element.193) | copy-start | bytes 12292
  14.7 112.0 %copy-start.27 = (pred[2,2048]{1,0:T(4,128)(4,1)}, pred[2,2048]{1,0:T(4,128)(4,1)S(1)}, u32[]{:S(2)}) copy-start(pred[2,2048]{1,0:T(4,128)(4,1)S(1)} %get-tuple-element.196) | copy-start | bytes 12292
  59.2 6.7 copy-start.37
  59.2 10.1 copy-start.36
  59.2 12.1 %copy-start.10 = (bf16[2048,64]{0,1:T(8,128)(2,1)S(1)}, bf16[2048,64]{0,1:T(8,128)(2,1)}, u32[]{:S(2)}) copy-start(bf16[2048,64]{0,1:T(8,128)(2,1)} %param.20) | copy-start | bytes 786436
  59.2 303.0 %all-to-all-start.12 = ((bf16[8,832,16,128]{3,2,1,0:T(8,128)(2,1)}), bf16[8,832,16,128]{3,2,1,0:T(8,128)(2,1)}, u32[]{:S(2)}, u32[]{:S(2)}) async-start(bf16[8,832,16,128]{3,2,1,0:T(8,128)(2,1)} %get-tuple-element.125), calls=%async_computation.12 | async-start | bytes 54525952 | tf_op jit(solution)/shard_map/all_to_all | solution.py:270
  64.9 34.0 %copy-start.29 = (s32[2,2048]{1,0:T(2,128)}, s32[2,2048]{1,0:T(2,128)S(1)}, u32[]{:S(2)}) copy-start(s32[2,2048]{1,0:T(2,128)S(1)} %convert_element_type.259) | copy-start | bytes 49156
  65.0 34.0 %copy-start.31 = (s32[2,2048]{1,0:T(2,128)}, s32[2,2048]{1,0:T(2,128)S(1)}, u32[]{:S(2)}) copy-start(s32[2,2048]{1,0:T(2,128)S(1)} %convert_element_type.263) | copy-start | bytes 49156
  97.8 3.2 copy-start.18
  97.9 25.2 %copy-start.5 = (f32[2,2048,64]{1,2,0:T(8,128)}, f32[2,2048,64]{1,2,0:T(8,128)S(1)}, u32[]{:S(2)}) copy-start(f32[2,2048,64]{1,2,0:T(8,128)S(1)} %get-tuple-element.236) | copy-start | bytes 3145732
  98.7 24.3 %copy-start.20 = (f32[2,2048]{1,0:T(2,128)}, f32[2,2048]{1,0:T(2,128)S(1)}, u32[]{:S(2)}) copy-start(f32[2,2048]{1,0:T(2,128)S(1)} %get-tuple-element.180) | copy-start | bytes 49156
  98.7 24.3 %copy-start.22 = (f32[2,2048]{1,0:T(2,128)}, f32[2,2048]{1,0:T(2,128)S(1)}, u32[]{:S(2)}) copy-start(f32[2,2048]{1,0:T(2,128)S(1)} %get-tuple-element.181) | copy-start | bytes 49156
  101.3 21.7 %copy-start.13 = (bf16[8,32,16,128]{3,2,1,0:T(8,128)(2,1)S(1)}, bf16[8,32,16,128]{3,2,1,0:T(8,128)(2,1)}, u32[]{:S(2)}) copy-start(bf16[8,32,16,128]{3,2,1,0:T(8,128)(2,1)} %get-tuple-element.135) | copy-start | bytes 3145732
  134.1 238.1 %copy-start.3 = (bf16[8,64,16,128]{3,2,1,0:T(8,128)(2,1)S(1)}, bf16[8,64,16,128]{3,2,1,0:T(8,128)(2,1)}, u32[]{:S(2)}) copy-start(bf16[8,64,16,128]{3,2,1,0:T(8,128)(2,1)} %get-tuple-element.139) | copy-start | bytes 6291460
  363.0 7.5 all-to-all-start.13
  371.4 96.4 %copy-start.16 = (f32[8,8,128]{2,1,0:T(8,128)}, f32[8,8,128]{2,1,0:T(8,128)S(1)}, u32[]{:S(2)}) copy-start(f32[8,8,128]{2,1,0:T(8,128)S(1)} %reshape.363) | copy-start | bytes 98308
  372.7 4.6 copy-start.4
  372.7 188.5 %all-to-all-start.14 = ((bf16[8,512,16,128]{3,2,1,0:T(8,128)(2,1)}), bf16[8,512,16,128]{3,2,1,0:T(8,128)(2,1)}, u32[]{:S(2)}, u32[]{:S(2)}) async-start(bf16[8,512,16,128]{3,2,1,0:T(8,128)(2,1)} %get-tuple-element.148), calls=%async_computation.14 | async-start | bytes 33554432 | tf_op jit(solution)/shard_map/all_to_all | solution.py:270
  561.2 120.6 %all-to-all-start.15 = ((bf16[8,320,16,128]{3,2,1,0:T(8,128)(2,1)}), bf16[8,320,16,128]{3,2,1,0:T(8,128)(2,1)}, u32[]{:S(2)}, u32[]{:S(2)}) async-start(bf16[8,320,16,128]{3,2,1,0:T(8,128)(2,1)} %get-tuple-element.155), calls=%async_computation.15 | async-start | bytes 20971520 | tf_op jit(solution)/shard_map/all_to_all | solution.py:270
  565.2 2.2 copy-start
  676.2 4.1 copy-start.2
  698.9 4.1 copy-start.7
  698.9 4.1 copy-start.9
  699.0 131.8 %all-to-all-start.16 = ((bf16[8,352,16,128]{3,2,1,0:T(8,128)(2,1)}), bf16[8,352,16,128]{3,2,1,0:T(8,128)(2,1)}, u32[]{:S(2)}, u32[]{:S(2)}) async-start(bf16[8,352,16,128]{3,2,1,0:T(8,128)(2,1)} %copy-done.2), calls=%async_computation.16 | async-start | bytes 23068672 | tf_op jit(solution)/shard_map/all_to_all | solution.py:270
  703.0 2.2 copy-start.1
  804.9 28.7 %copy-start.34 = (f32[8,8]{0,1:T(8,128)S(1)}, f32[8,8]{0,1:T(8,128)}, u32[]{:S(2)}) copy-start(f32[8,8]{0,1:T(8,128)} %copy.255) | copy-start | bytes 772
  831.6 6.9 all-to-all-start.17
  839.8 212.9 %all-to-all-start.18 = ((bf16[8,512,16,128]{3,2,1,0:T(8,128)(2,1)}), bf16[8,512,16,128]{3,2,1,0:T(8,128)(2,1)}, u32[]{:S(2)}, u32[]{:S(2)}) async-start(bf16[8,512,16,128]{3,2,1,0:T(8,128)(2,1)} %shard_map.143), calls=%async_computation.18 | async-start | bytes 33554432 | tf_op jit(solution)/shard_map/all_to_all | solution.py:270
  844.2 59.5 %copy-start.17 = (f32[8,8,128]{2,1,0:T(8,128)S(1)}, f32[8,8,128]{2,1,0:T(8,128)}, u32[]{:S(2)}) copy-start(f32[8,8,128]{2,1,0:T(8,128)} %copy-done.16) | copy-start | bytes 98308
  844.2 61.4 %copy-start.15 = (s32[2,2048]{1,0:T(2,128)S(1)}, s32[2,2048]{1,0:T(2,128)}, u32[]{:S(2)}) copy-start(s32[2,2048]{1,0:T(2,128)} %param.24) | copy-start | bytes 49156
  844.3 61.4 %copy-start.28 = (pred[2,2048]{1,0:T(4,128)(4,1)S(1)}, pred[2,2048]{1,0:T(4,128)(4,1)}, u32[]{:S(2)}) copy-start(pred[2,2048]{1,0:T(4,128)(4,1)} %copy-done.27) | copy-start | bytes 12292
  844.3 61.4 %copy-start.32 = (s32[2,2048]{1,0:T(2,128)S(1)}, s32[2,2048]{1,0:T(2,128)}, u32[]{:S(2)}) copy-start(s32[2,2048]{1,0:T(2,128)} %copy-done.31) | copy-start | bytes 49156
  844.3 62.2 %copy-start.12 = (s32[2,2048]{1,0:T(2,128)S(1)}, s32[2,2048]{1,0:T(2,128)}, u32[]{:S(2)}) copy-start(s32[2,2048]{1,0:T(2,128)} %param.23) | copy-start | bytes 49156
  844.3 62.2 %copy-start.25 = (pred[2,2048]{1,0:T(4,128)(4,1)S(1)}, pred[2,2048]{1,0:T(4,128)(4,1)}, u32[]{:S(2)}) copy-start(pred[2,2048]{1,0:T(4,128)(4,1)} %copy-done.24) | copy-start | bytes 12292
  844.3 62.2 %copy-start.30 = (s32[2,2048]{1,0:T(2,128)S(1)}, s32[2,2048]{1,0:T(2,128)}, u32[]{:S(2)}) copy-start(s32[2,2048]{1,0:T(2,128)} %copy-done.29) | copy-start | bytes 49156
  844.3 63.0 %copy-start.21 = (f32[2,2048]{1,0:T(2,128)S(1)}, f32[2,2048]{1,0:T(2,128)}, u32[]{:S(2)}) copy-start(f32[2,2048]{1,0:T(2,128)} %copy-done.20) | copy-start | bytes 49156
  844.3 63.0 %copy-start.23 = (f32[2,2048]{1,0:T(2,128)S(1)}, f32[2,2048]{1,0:T(2,128)}, u32[]{:S(2)}) copy-start(f32[2,2048]{1,0:T(2,128)} %copy-done.22) | copy-start | bytes 49156
  844.3 63.0 %copy-start.6 = (f32[2,2048,64]{1,2,0:T(8,128)S(1)}, f32[2,2048,64]{1,2,0:T(8,128)}, u32[]{:S(2)}) copy-start(f32[2,2048,64]{1,2,0:T(8,128)} %copy-done.5) | copy-start | bytes 3145732
  844.3 63.0 %copy-start.19 = (f32[2,2048]{1,0:T(2,128)S(1)}, f32[2,2048]{1,0:T(2,128)}, u32[]{:S(2)}) copy-start(f32[2,2048]{1,0:T(2,128)} %copy-done.18) | copy-start | bytes 49156
  844.3 202.4 %all-reduce.2.cloned.1.call-start = ((), (), s32[]{:S(2)}) async-start(), calls=%async_computation.19 | async-start | bytes 1114112 | tf_op jit(solution)/shard_map/psum | solution.py:439
  903.7 13.5 %copy-start.26 = (f32[1,64]{0,1:T(8,128)S(1)}, f32[1,64]{0,1:T(8,128)}, u32[]{:S(2)}) copy-start(f32[1,64]{0,1:T(8,128)} %copy.241) | copy-start | bytes 772
  918.1 131.4 %copy-start.35 = (f32[64]{0:T(128)S(1)}, f32[64]{0:T(128)}, u32[]{:S(2)}) copy-start(f32[64]{0:T(128)} %div.141) | copy-start | bytes 772
  918.1 134.6 %copy-start.8 = (bf16[8,32,16,128]{3,2,1,0:T(8,128)(2,1)S(1)}, bf16[8,32,16,128]{3,2,1,0:T(8,128)(2,1)}, u32[]{:S(2)}) copy-start(bf16[8,32,16,128]{3,2,1,0:T(8,128)(2,1)} %copy-done.7) | copy-start | bytes 3145732
Sparse Core Ops, SparseCore 0:
  918.2 128.4 all-reduce.1
